TPU v7x, 128 devices: a whole 4x4x4 slice. The times are simulated.
128 devices in a mesh: gx: 16 (over z, y_lo, core), gy: 4 (over x), gz: 2 (over y_hi).
Axes of the slice: x: 4, y: 4 (y_hi: 2, y_lo: 2; y = y_hi * 2 + y_lo), z: 4, core: 2. Of those that a mesh axis runs over, the one named last changes fastest.
Arguments:
- models: float32 [2, 256, 128, 256], P(None, 'gx', 'gy', 'gz'), may hold values from -6 to 6
- targets: float32 [2, 256, 128, 256], P(None, 'gx', 'gy', 'gz'), may hold values from -6 to 6
- weights: float32 [2, 256, 128, 256], P(None, 'gx', 'gy', 'gz'), may hold values from 0.5 to 12, as said below
Outputs:
- updated: float32 [2, 256, 128, 256], P(None, 'gx', 'gy', 'gz')
- applied_last: float32 [2, 256, 128, 256], P(None, 'gx', 'gy', 'gz')
Inputs may be any that keep to these rules, and one draw needn't show every extreme that they name: Positive data weights.
All inputs are finite; a program needn't handle non-finite values.
Results may differ from a plain program's by a relative error of at most 0.00016.
Values sent between devices are 32-bit elements; how exact they have to be, the bound alone decides.
No kernel may reach another device: no remote copies, remote signals or barrier semaphores. Data moves between devices by JAX's collectives and lax.ppermute only.
A program may use at most 128 MiB of HBM per device.

v0:
```python
import functools

import jax
import jax.numpy as jnp
from jax import lax
from jax.sharding import Mesh
from jax.sharding import PartitionSpec as P

ITERS = 3
GX_GY_GZ = ("gx_0", "gx_1", "gx_2", "gy", "gz")
GX = ("gx_0", "gx_1", "gx_2")


def padded_2(cells, sides, width):
    for axis, dim in sides:
        count = lax.axis_size(axis)
        ends = count - 1
        head = lax.slice_in_dim(cells, 0, width, axis=dim)
        tail = lax.slice_in_dim(cells, cells.shape[dim] - width, cells.shape[dim], axis=dim)
        cells = jnp.concatenate(
            [
                lax.ppermute(tail, axis, [(i, (i + 1) % count) for i in range(ends)]),
                cells,
                lax.ppermute(head, axis, [((i + 1) % count, i) for i in range(ends)]),
            ],
            axis=dim,
        )
    return cells


def one_axis_at_a_time(value, axes):
    return functools.reduce(lax.psum, axes, value)


def central_padded(padded, which):
    if which == 0:
        return 0.5 * (padded[2:, 1:-1, 1:-1] - padded[:-2, 1:-1, 1:-1])
    if which == 1:
        return 0.5 * (padded[1:-1, 2:, 1:-1] - padded[1:-1, :-2, 1:-1])
    return 0.5 * (padded[1:-1, 1:-1, 2:] - padded[1:-1, 1:-1, :-2])


def laplace_padded(padded):
    center = padded[1:-1, 1:-1, 1:-1]
    neighbours = padded[2:, 1:-1, 1:-1] + padded[:-2, 1:-1, 1:-1]
    neighbours = neighbours + padded[1:-1, 2:, 1:-1] + padded[1:-1, :-2, 1:-1]
    neighbours = neighbours + padded[1:-1, 1:-1, 2:] + padded[1:-1, 1:-1, :-2]
    return 6.0 * center - neighbours


def vector_cross(first_vec, second_vec):
    return (
        first_vec[1] * second_vec[2] - first_vec[2] * second_vec[1],
        first_vec[2] * second_vec[0] - first_vec[0] * second_vec[2],
        first_vec[0] * second_vec[1] - first_vec[1] * second_vec[0],
    )


def coupled_fields(padded_models):
    first_grad = [central_padded(padded_models[0], k) for k in range(3)]
    second_grad = [central_padded(padded_models[1], k) for k in range(3)]
    crossed = vector_cross(first_grad, second_grad)
    first_flux = vector_cross(second_grad, crossed)
    second_flux = vector_cross(crossed, first_grad)
    return jnp.stack(list(first_flux) + list(second_flux))


def coupling_terms(padded_fields):
    first_div = (
        central_padded(padded_fields[0], 0)
        + central_padded(padded_fields[1], 1)
        + central_padded(padded_fields[2], 2)
    )
    second_div = (
        central_padded(padded_fields[3], 0)
        + central_padded(padded_fields[4], 1)
        + central_padded(padded_fields[5], 2)
    )
    return -2.0 * jnp.stack([first_div, second_div])


def edge_keep(cells, device_pos, devices):
    position = jnp.arange(cells + 2)
    low_out = jnp.logical_and(position == 0, device_pos == 0)
    high_out = jnp.logical_and(position == cells + 1, device_pos == devices - 1)
    return jnp.logical_not(jnp.logical_or(low_out, high_out)).astype(jnp.float32)


def local(models, targets, weights):
    cells_x, cells_y, cells_z = (models.shape[1], models.shape[2], models.shape[3])
    current = models
    applied = jnp.zeros_like(models)
    for iteration in range(ITERS):
        deeper = padded_2(current, ((GX, 1), ("gy", 2), ("gz", 3)), 2)
        padded = deeper[:, 1:-1, 1:-1, 1:-1]
        rim_mask = (
            edge_keep(cells_x, lax.axis_index(GX), lax.axis_size(GX))[:, None, None]
            * edge_keep(cells_y, lax.axis_index("gy"), lax.axis_size("gy"))[None, :, None]
            * edge_keep(cells_z, lax.axis_index("gz"), lax.axis_size("gz"))[None, None, :]
        )
        padded_fields = coupled_fields(deeper) * rim_mask[None]
        smooth = jnp.stack([laplace_padded(padded[0]), laplace_padded(padded[1])])
        coupling = coupling_terms(padded_fields)
        gradient = weights * (current - targets) + 1.0 * smooth + 0.05 * coupling
        local_norm = jnp.sum(gradient * gradient)
        padded_grad = padded_2(gradient, ((GX, 1), ("gy", 2), ("gz", 3)), 1)
        applied = weights * gradient + 1.0 * jnp.stack(
            [laplace_padded(padded_grad[0]), laplace_padded(padded_grad[1])]
        )
        local_curv = jnp.sum(gradient * applied)
        grad_norm, curvature = (
            one_axis_at_a_time(local_norm, GX_GY_GZ),
            one_axis_at_a_time(local_curv, GX_GY_GZ),
        )
        step_size = grad_norm / curvature
        current = current - step_size * gradient
    return (current, applied)


def solution(mesh):
    finer = Mesh(
        mesh.devices.reshape(4, 2, 2, mesh.shape["gy"], mesh.shape["gz"]),
        ("gx_0", "gx_1", "gx_2", "gy", "gz"),
    )
    in_specs = (P(None, GX, "gy", "gz"), P(None, GX, "gy", "gz"), P(None, GX, "gy", "gz"))
    out_specs = (P(None, GX, "gy", "gz"), P(None, GX, "gy", "gz"))
    return jax.shard_map(local, mesh=finer, in_specs=in_specs, out_specs=out_specs, check_vma=False)
```

profile of v0, /device:TPU:16, one launch (start us, length us, event | category | flops | bytes accessed | tf_op | source)
XLA Modules:
  0.0 439.4 jit_solution(4943765046524625919)
XLA Ops:
  13.5 3.8 collective-permute-done.3
  24.9 6.1 %collective-permute-start.5 = (f32[2,20,36,2]{2,3,1,0:T(2,128)S(1)}, f32[2,20,36,2]{2,3,1,0:T(2,128)S(1)}, u32[]{:S(2)}, u32[]{:S(2)}) collective-permute-start(f32[2,20,36,2]{2,3,1,0:T(2,128)S(1)} %get-tuple-element.79), channel_id=1, source_target_pairs={{1,0},{3,2},{5,4},{7,6},{9,8},{11,10},{13,12},{15,14},{17,16},{19,... | collective-permute-start | bytes 34568 | tf_op jit(solution)/shard_map/ppermute | solution.py:24
  35.1 4.7 %fusion.63 = (f32[1,16,32,128]{2,3,1,0:T(8,128)}, f32[1,16,32,128]{2,3,1,0:T(8,128)}) fusion(f32[18,34,130]{1,2,0:T(8,128)S(1)} %get-tuple-element.115, f32[18,34,130]{1,2,0:T(8,128)S(1)} %get-tuple-element.114), kind=kLoop, calls=%fused_computation.232 | loop fusion | flops 917504 | bytes 4194304 | tf_op jit(solution)/shard_map/stack | solution.py:102
  43.5 4.7 %bitcast_dynamic-update-slice_fusion.17 = (f32[6,18,34,130]{2,3,1,0:T(8,128)}, f32[18,34,130]{1,2,0:T(8,128)S(1)}, f32[18,34,130]{1,2,0:T(8,128)S(1)}, f32[18,34...) fusion(f32[20,36,132]{1,2,0:T(8,128)S(1)} %get-tuple-element.11, ...), kind=kLoop, calls=%fused_computation.98 | loop fusion | flops 1670759 | bytes 7618176
  59.4 4.0 fusion.56
  70.0 5.6 %collective-permute-done.7 = f32[2,1,32,128]{3,2,1,0:T(8,128)S(1)} collective-permute-done((f32[2,1,32,128]{3,2,1,0:T(8,128)S(1)}, f32[2,1,32,128]{3,2,1,0:T(8,128)S(1)}, u32[]{:S(2)}, u32[]{:S(2)}) %collective-permute-start.7) | collective-permute-done | bytes 32800 | tf_op jit(solution)/shard_map/ppermute | solution.py:24
  88.5 5.3 %collective-permute-start.11 = (f32[2,18,34,1]{2,0,3,1:T(2,128)S(1)}, f32[2,18,34,1]{2,0,3,1:T(2,128)S(1)}, u32[]{:S(2)}, u32[]{:S(2)}) collective-permute-start(f32[2,18,34,1]{2,0,3,1:T(2,128)S(1)} %copy.100), channel_id=1, source_target_pairs={{1,0},{3,2},{5,4},{7,6},{9,8},{11,10},{13,12},{15,14},{17,16},{19,... | collective-permute-start | bytes 14696 | tf_op jit(solution)/shard_map/ppermute | solution.py:24
  95.5 5.4 %collective-permute-done.10 = f32[2,18,34,1]{2,0,3,1:T(2,128)S(1)} collective-permute-done((f32[2,18,34,1]{2,0,3,1:T(2,128)S(1)}, f32[2,18,34,1]{2,0,3,1:T(2,128)S(1)}, u32[]{:S(2)}, u32[]{:S(2)}) %collective-permute-start.10) | collective-permute-done | bytes 4928 | tf_op jit(solution)/shard_map/ppermute | solution.py:22
  108.2 16.4 %all-reduce.5 = (f32[]{:T(128)}, f32[]{:T(128)}) all-reduce(f32[]{:T(128)} %get-tuple-element.9, f32[]{:T(128)} %get-tuple-element.8), channel_id=1, replica_groups=mesh['gx_0'=4,'gx_1'=2,'gx_2'=2,'gy'=4,'gz'=2] {'gx_0'}, use_global_device_ids=true, to_apply=%region_1.0 | all-reduce | flops 2 | bytes 16 | tf_op jit(solution)/shard_map/psum | solution.py:32
  124.6 5.5 %all-reduce.14 = (f32[]{:T(128)}, f32[]{:T(128)}) all-reduce(f32[]{:T(128)} %get-tuple-element.20, f32[]{:T(128)} %get-tuple-element.21), channel_id=1, replica_groups=mesh['gx_0'=4,'gx_1'=2,'gx_2'=2,'gy'=4,'gz'=2] {'gx_1'}, use_global_device_ids=true, to_apply=%region_2.0 | all-reduce | flops 2 | bytes 16 | tf_op jit(solution)/shard_map/psum | solution.py:32
  133.2 10.6 %all-reduce.2 = (f32[]{:T(128)}, f32[]{:T(128)}) all-reduce(f32[]{:T(128)} %get-tuple-element.32, f32[]{:T(128)} %get-tuple-element.33), channel_id=1, replica_groups=mesh['gx_0'=4,'gx_1'=2,'gx_2'=2,'gy'=4,'gz'=2] {'gy'}, use_global_device_ids=true, to_apply=%region_4.0 | all-reduce | flops 2 | bytes 16 | tf_op jit(solution)/shard_map/psum | solution.py:32
  143.7 7.1 %all-reduce.8 = (f32[]{:T(128)}, f32[]{:T(128)}) all-reduce(f32[]{:T(128)} %get-tuple-element.14, f32[]{:T(128)} %get-tuple-element.15), channel_id=1, replica_groups=mesh['gx_0'=4,'gx_1'=2,'gx_2'=2,'gy'=4,'gz'=2] {'gz'}, use_global_device_ids=true, to_apply=%region_5.0 | all-reduce | flops 2 | bytes 16 | tf_op jit(solution)/shard_map/psum | solution.py:32
  158.4 4.5 %collective-permute-start.14 = (f32[2,20,2,128]{3,2,1,0:T(2,128)S(1)}, f32[2,20,2,128]{3,2,1,0:T(2,128)S(1)}, u32[]{:S(2)}, u32[]{:S(2)}) collective-permute-start(f32[2,20,2,128]{3,2,1,0:T(2,128)S(1)} %get-tuple-element.124), channel_id=1, source_target_pairs={{0,2},{2,4},{4,6},{1,3},{3,5},{5,7},{8,10},{10,12},{12,14},{9,11},... | collective-permute-start | bytes 122888 | tf_op jit(solution)/shard_map/ppermute | solution.py:22
  172.3 6.1 %collective-permute-start.17 = (f32[2,20,36,2]{2,3,1,0:T(2,128)S(1)}, f32[2,20,36,2]{2,3,1,0:T(2,128)S(1)}, u32[]{:S(2)}, u32[]{:S(2)}) collective-permute-start(f32[2,20,36,2]{2,3,1,0:T(2,128)S(1)} %get-tuple-element.77), channel_id=1, source_target_pairs={{1,0},{3,2},{5,4},{7,6},{9,8},{11,10},{13,12},{15,14},{17,16},{19,... | collective-permute-start | bytes 34568 | tf_op jit(solution)/shard_map/ppermute | solution.py:24
  192.7 7.6 %bitcast_dynamic-update-slice_fusion.11 = (f32[6,18,34,130]{2,3,1,0:T(8,128)S(1)}, f32[18,34,130]{1,2,0:T(8,128)S(1)}, f32[18,34,130]{1,2,0:T(8,128)S(1)}, f32[1...) fusion(f32[20,36,132]{1,2,0:T(8,128)} %get-tuple-element.109, ...), kind=kLoop, calls=%fused_computation.92 | loop fusion | flops 1670759 | bytes 15099264
  209.7 4.0 fusion.40
  236.0 5.3 %collective-permute-start.23 = (f32[2,18,34,1]{2,0,3,1:T(2,128)S(1)}, f32[2,18,34,1]{2,0,3,1:T(2,128)S(1)}, u32[]{:S(2)}, u32[]{:S(2)}) collective-permute-start(f32[2,18,34,1]{2,0,3,1:T(2,128)S(1)} %copy.118), channel_id=1, source_target_pairs={{1,0},{3,2},{5,4},{7,6},{9,8},{11,10},{13,12},{15,14},{17,16},{19,... | collective-permute-start | bytes 14696 | tf_op jit(solution)/shard_map/ppermute | solution.py:24
  242.9 5.6 %collective-permute-done.22 = f32[2,18,34,1]{2,0,3,1:T(2,128)S(1)} collective-permute-done((f32[2,18,34,1]{2,0,3,1:T(2,128)S(1)}, f32[2,18,34,1]{2,0,3,1:T(2,128)S(1)}, u32[]{:S(2)}, u32[]{:S(2)}) %collective-permute-start.22) | collective-permute-done | bytes 4928 | tf_op jit(solution)/shard_map/ppermute | solution.py:22
  255.9 13.0 %all-reduce.4 = (f32[]{:T(128)}, f32[]{:T(128)}) all-reduce(f32[]{:T(128)} %get-tuple-element.7, f32[]{:T(128)} %get-tuple-element.6), channel_id=1, replica_groups=mesh['gx_0'=4,'gx_1'=2,'gx_2'=2,'gy'=4,'gz'=2] {'gx_0'}, use_global_device_ids=true, to_apply=%region_13.0 | all-reduce | flops 2 | bytes 16 | tf_op jit(solution)/shard_map/psum | solution.py:32
  268.8 5.6 %all-reduce.13 = (f32[]{:T(128)}, f32[]{:T(128)}) all-reduce(f32[]{:T(128)} %get-tuple-element.18, f32[]{:T(128)} %get-tuple-element.19), channel_id=1, replica_groups=mesh['gx_0'=4,'gx_1'=2,'gx_2'=2,'gy'=4,'gz'=2] {'gx_1'}, use_global_device_ids=true, to_apply=%region_14.0 | all-reduce | flops 2 | bytes 16 | tf_op jit(solution)/shard_map/psum | solution.py:32
  277.5 10.6 %all-reduce.1 = (f32[]{:T(128)}, f32[]{:T(128)}) all-reduce(f32[]{:T(128)} %get-tuple-element.30, f32[]{:T(128)} %get-tuple-element.31), channel_id=1, replica_groups=mesh['gx_0'=4,'gx_1'=2,'gx_2'=2,'gy'=4,'gz'=2] {'gy'}, use_global_device_ids=true, to_apply=%region_16.0 | all-reduce | flops 2 | bytes 16 | tf_op jit(solution)/shard_map/psum | solution.py:32
  288.2 7.1 %all-reduce.7 = (f32[]{:T(128)}, f32[]{:T(128)}) all-reduce(f32[]{:T(128)} %get-tuple-element.12, f32[]{:T(128)} %get-tuple-element.13), channel_id=1, replica_groups=mesh['gx_0'=4,'gx_1'=2,'gx_2'=2,'gy'=4,'gz'=2] {'gz'}, use_global_device_ids=true, to_apply=%region_17.0 | all-reduce | flops 2 | bytes 16 | tf_op jit(solution)/shard_map/psum | solution.py:32
  302.8 4.5 %collective-permute-start.26 = (f32[2,20,2,128]{3,2,1,0:T(2,128)S(1)}, f32[2,20,2,128]{3,2,1,0:T(2,128)S(1)}, u32[]{:S(2)}, u32[]{:S(2)}) collective-permute-start(f32[2,20,2,128]{3,2,1,0:T(2,128)S(1)} %get-tuple-element.122), channel_id=1, source_target_pairs={{0,2},{2,4},{4,6},{1,3},{3,5},{5,7},{8,10},{10,12},{12,14},{9,11},... | collective-permute-start | bytes 122888 | tf_op jit(solution)/shard_map/ppermute | solution.py:22
  318.9 5.7 %collective-permute-done.28 = f32[2,20,36,2]{2,1,3,0:T(8,128)S(1)} collective-permute-done((f32[2,20,36,2]{2,1,3,0:T(8,128)S(1)}, f32[2,20,36,2]{2,1,3,0:T(8,128)S(1)}, u32[]{:S(2)}, u32[]{:S(2)}) %collective-permute-start.28) | collective-permute-done | bytes 11552 | tf_op jit(solution)/shard_map/ppermute | solution.py:22
  337.4 7.8 %bitcast_dynamic-update-slice_fusion.5 = (f32[6,18,34,130]{2,3,1,0:T(8,128)S(1)}, f32[18,34,130]{1,2,0:T(8,128)S(1)}, f32[18,34,130]{1,2,0:T(8,128)S(1)}, f32[18...) fusion(f32[20,36,132]{1,2,0:T(8,128)} %get-tuple-element.105, ...), kind=kLoop, calls=%fused_computation.86 | loop fusion | flops 1670759 | bytes 15099264
  354.6 4.0 fusion.24
  365.7 3.9 collective-permute-done.31
  383.9 5.6 %collective-permute-done.34 = f32[2,18,34,1]{2,0,3,1:T(2,128)S(1)} collective-permute-done((f32[2,18,34,1]{2,0,3,1:T(2,128)S(1)}, f32[2,18,34,1]{2,0,3,1:T(2,128)S(1)}, u32[]{:S(2)}, u32[]{:S(2)}) %collective-permute-start.34) | collective-permute-done | bytes 4928 | tf_op jit(solution)/shard_map/ppermute | solution.py:22
  397.5 13.2 %all-reduce.3 = (f32[]{:T(128)}, f32[]{:T(128)}) all-reduce(f32[]{:T(128)} %get-tuple-element.5, f32[]{:T(128)} %get-tuple-element.4), channel_id=1, replica_groups=mesh['gx_0'=4,'gx_1'=2,'gx_2'=2,'gy'=4,'gz'=2] {'gx_0'}, use_global_device_ids=true, to_apply=%region_25.0 | all-reduce | flops 2 | bytes 16 | tf_op jit(solution)/shard_map/psum | solution.py:32
  410.6 5.6 %all-reduce.12 = (f32[]{:T(128)}, f32[]{:T(128)}) all-reduce(f32[]{:T(128)} %get-tuple-element.16, f32[]{:T(128)} %get-tuple-element.17), channel_id=1, replica_groups=mesh['gx_0'=4,'gx_1'=2,'gx_2'=2,'gy'=4,'gz'=2] {'gx_1'}, use_global_device_ids=true, to_apply=%region_26.0 | all-reduce | flops 2 | bytes 16 | tf_op jit(solution)/shard_map/psum | solution.py:32
  419.4 10.6 %all-reduce = (f32[]{:T(128)}, f32[]{:T(128)}) all-reduce(f32[]{:T(128)} %get-tuple-element.28, f32[]{:T(128)} %get-tuple-element.29), channel_id=1, replica_groups=mesh['gx_0'=4,'gx_1'=2,'gx_2'=2,'gy'=4,'gz'=2] {'gy'}, use_global_device_ids=true, to_apply=%region_28.0 | all-reduce | flops 2 | bytes 16 | tf_op jit(solution)/shard_map/psum | solution.py:32
  429.9 7.1 %all-reduce.6 = (f32[]{:T(128)}, f32[]{:T(128)}) all-reduce(f32[]{:T(128)} %get-tuple-element.10, f32[]{:T(128)} %get-tuple-element.11), channel_id=1, replica_groups=mesh['gx_0'=4,'gx_1'=2,'gx_2'=2,'gy'=4,'gz'=2] {'gz'}, use_global_device_ids=true, to_apply=%region_29.0 | all-reduce | flops 2 | bytes 16 | tf_op jit(solution)/shard_map/psum | solution.py:32
  (290 shorter events, 216.7 us)
Async XLA Ops:
  1.5 6.3 %collective-permute-start.1 = (f32[2,2,32,128]{3,2,1,0:T(8,128)S(1)}, f32[2,2,32,128]{3,2,1,0:T(8,128)S(1)}, u32[]{:S(2)}, u32[]{:S(2)}) collective-permute-start(f32[2,2,32,128]{3,2,1,0:T(8,128)S(1)} %get-tuple-element.144), channel_id=1, source_target_pairs={{8,0},{16,8},{24,16},{32,24},{40,32},{48,40},{56,48},{64,56},{72,6... | collective-permute-start | bytes 196616 | tf_op jit(solution)/shard_map/ppermute | solution.py:24
  2.8 3.9 collective-permute-start
  7.9 11.8 %collective-permute-start.2 = (f32[2,20,2,128]{3,2,1,0:T(2,128)S(1)}, f32[2,20,2,128]{3,2,1,0:T(2,128)S(1)}, u32[]{:S(2)}, u32[]{:S(2)}) collective-permute-start(f32[2,20,2,128]{3,2,1,0:T(2,128)S(1)} %get-tuple-element.126), channel_id=1, source_target_pairs={{0,2},{2,4},{4,6},{1,3},{3,5},{5,7},{8,10},{10,12},{12,14},{9,11},... | collective-permute-start | bytes 122888 | tf_op jit(solution)/shard_map/ppermute | solution.py:22
  11.3 6.1 %collective-permute-start.3 = (f32[2,20,2,128]{3,2,1,0:T(2,128)S(1)}, f32[2,20,2,128]{3,2,1,0:T(2,128)S(1)}, u32[]{:S(2)}, u32[]{:S(2)}) collective-permute-start(f32[2,20,2,128]{3,2,1,0:T(2,128)S(1)} %get-tuple-element.127), channel_id=1, source_target_pairs={{2,0},{4,2},{6,4},{3,1},{5,3},{7,5},{10,8},{12,10},{14,12},{11,9},... | collective-permute-start | bytes 122888 | tf_op jit(solution)/shard_map/ppermute | solution.py:24
  23.5 8.8 %collective-permute-start.4 = (f32[2,20,36,2]{2,3,1,0:T(2,128)S(1)}, f32[2,20,36,2]{2,3,1,0:T(2,128)S(1)}, u32[]{:S(2)}, u32[]{:S(2)}) collective-permute-start(f32[2,20,36,2]{2,3,1,0:T(2,128)S(1)} %get-tuple-element.78), channel_id=1, source_target_pairs={{0,1},{2,3},{4,5},{6,7},{8,9},{10,11},{12,13},{14,15},{16,17},{18,... | collective-permute-start | bytes 34568 | tf_op jit(solution)/shard_map/ppermute | solution.py:22
  24.9 7.7 %collective-permute-start.5 = (f32[2,20,36,2]{2,3,1,0:T(2,128)S(1)}, f32[2,20,36,2]{2,3,1,0:T(2,128)S(1)}, u32[]{:S(2)}, u32[]{:S(2)}) collective-permute-start(f32[2,20,36,2]{2,3,1,0:T(2,128)S(1)} %get-tuple-element.79), channel_id=1, source_target_pairs={{1,0},{3,2},{5,4},{7,6},{9,8},{11,10},{13,12},{15,14},{17,16},{19,... | collective-permute-start | bytes 34568 | tf_op jit(solution)/shard_map/ppermute | solution.py:24
  68.7 6.9 %collective-permute-start.7 = (f32[2,1,32,128]{3,2,1,0:T(8,128)S(1)}, f32[2,1,32,128]{3,2,1,0:T(8,128)S(1)}, u32[]{:S(2)}, u32[]{:S(2)}) collective-permute-start(f32[2,1,32,128]{3,2,1,0:T(8,128)S(1)} %get-tuple-element.143), channel_id=1, source_target_pairs={{8,0},{16,8},{24,16},{32,24},{40,32},{48,40},{56,48},{64,56},{72,6... | collective-permute-start | bytes 98312 | tf_op jit(solution)/shard_map/ppermute | solution.py:24
  75.7 6.5 %collective-permute-start.8 = (f32[2,18,1,128]{3,0,2,1:T(2,128)S(1)}, f32[2,18,1,128]{3,0,2,1:T(2,128)S(1)}, u32[]{:S(2)}, u32[]{:S(2)}) collective-permute-start(f32[2,18,1,128]{3,0,2,1:T(2,128)S(1)} %copy.145), channel_id=1, source_target_pairs={{0,2},{2,4},{4,6},{1,3},{3,5},{5,7},{8,10},{10,12},{12,14},{9,11},... | collective-permute-start | bytes 55304 | tf_op jit(solution)/shard_map/ppermute | solution.py:22
  79.2 5.7 %collective-permute-start.9 = (f32[2,18,1,128]{3,0,2,1:T(2,128)S(1)}, f32[2,18,1,128]{3,0,2,1:T(2,128)S(1)}, u32[]{:S(2)}, u32[]{:S(2)}) collective-permute-start(f32[2,18,1,128]{3,0,2,1:T(2,128)S(1)} %copy.146), channel_id=1, source_target_pairs={{2,0},{4,2},{6,4},{3,1},{5,3},{7,5},{10,8},{12,10},{14,12},{11,9},... | collective-permute-start | bytes 55304 | tf_op jit(solution)/shard_map/ppermute | solution.py:24
  88.5 7.0 %collective-permute-start.11 = (f32[2,18,34,1]{2,0,3,1:T(2,128)S(1)}, f32[2,18,34,1]{2,0,3,1:T(2,128)S(1)}, u32[]{:S(2)}, u32[]{:S(2)}) collective-permute-start(f32[2,18,34,1]{2,0,3,1:T(2,128)S(1)} %copy.100), channel_id=1, source_target_pairs={{1,0},{3,2},{5,4},{7,6},{9,8},{11,10},{13,12},{15,14},{17,16},{19,... | collective-permute-start | bytes 14696 | tf_op jit(solution)/shard_map/ppermute | solution.py:24
  93.8 7.2 %collective-permute-start.10 = (f32[2,18,34,1]{2,0,3,1:T(2,128)S(1)}, f32[2,18,34,1]{2,0,3,1:T(2,128)S(1)}, u32[]{:S(2)}, u32[]{:S(2)}) collective-permute-start(f32[2,18,34,1]{2,0,3,1:T(2,128)S(1)} %copy.99), channel_id=1, source_target_pairs={{0,1},{2,3},{4,5},{6,7},{8,9},{10,11},{12,13},{14,15},{16,17},{18,... | collective-permute-start | bytes 14696 | tf_op jit(solution)/shard_map/ppermute | solution.py:22
  153.6 3.4 collective-permute-start.13
  157.0 7.7 %collective-permute-start.15 = (f32[2,20,2,128]{3,2,1,0:T(2,128)S(1)}, f32[2,20,2,128]{3,2,1,0:T(2,128)S(1)}, u32[]{:S(2)}, u32[]{:S(2)}) collective-permute-start(f32[2,20,2,128]{3,2,1,0:T(2,128)S(1)} %get-tuple-element.125), channel_id=1, source_target_pairs={{2,0},{4,2},{6,4},{3,1},{5,3},{7,5},{10,8},{12,10},{14,12},{11,9},... | collective-permute-start | bytes 122888 | tf_op jit(solution)/shard_map/ppermute | solution.py:24
  158.4 8.7 %collective-permute-start.14 = (f32[2,20,2,128]{3,2,1,0:T(2,128)S(1)}, f32[2,20,2,128]{3,2,1,0:T(2,128)S(1)}, u32[]{:S(2)}, u32[]{:S(2)}) collective-permute-start(f32[2,20,2,128]{3,2,1,0:T(2,128)S(1)} %get-tuple-element.124), channel_id=1, source_target_pairs={{0,2},{2,4},{4,6},{1,3},{3,5},{5,7},{8,10},{10,12},{12,14},{9,11},... | collective-permute-start | bytes 122888 | tf_op jit(solution)/shard_map/ppermute | solution.py:22
  170.9 7.5 %collective-permute-start.16 = (f32[2,20,36,2]{2,3,1,0:T(2,128)S(1)}, f32[2,20,36,2]{2,3,1,0:T(2,128)S(1)}, u32[]{:S(2)}, u32[]{:S(2)}) collective-permute-start(f32[2,20,36,2]{2,3,1,0:T(2,128)S(1)} %get-tuple-element.76), channel_id=1, source_target_pairs={{0,1},{2,3},{4,5},{6,7},{8,9},{10,11},{12,13},{14,15},{16,17},{18,... | collective-permute-start | bytes 34568 | tf_op jit(solution)/shard_map/ppermute | solution.py:22
  172.3 7.7 %collective-permute-start.17 = (f32[2,20,36,2]{2,3,1,0:T(2,128)S(1)}, f32[2,20,36,2]{2,3,1,0:T(2,128)S(1)}, u32[]{:S(2)}, u32[]{:S(2)}) collective-permute-start(f32[2,20,36,2]{2,3,1,0:T(2,128)S(1)} %get-tuple-element.77), channel_id=1, source_target_pairs={{1,0},{3,2},{5,4},{7,6},{9,8},{11,10},{13,12},{15,14},{17,16},{19,... | collective-permute-start | bytes 34568 | tf_op jit(solution)/shard_map/ppermute | solution.py:24
  216.7 4.5 %collective-permute-start.18 = (f32[2,1,32,128]{3,2,1,0:T(8,128)S(1)}, f32[2,1,32,128]{3,2,1,0:T(8,128)S(1)}, u32[]{:S(2)}, u32[]{:S(2)}) collective-permute-start(f32[2,1,32,128]{3,2,1,0:T(8,128)S(1)} %get-tuple-element.138), channel_id=1, source_target_pairs={{0,8},{8,16},{16,24},{24,32},{32,40},{40,48},{48,56},{56,64},{64,7... | collective-permute-start | bytes 98312 | tf_op jit(solution)/shard_map/ppermute | solution.py:22
  219.8 4.3 collective-permute-start.19
  224.2 5.6 %collective-permute-start.20 = (f32[2,18,1,128]{3,0,2,1:T(2,128)S(1)}, f32[2,18,1,128]{3,0,2,1:T(2,128)S(1)}, u32[]{:S(2)}, u32[]{:S(2)}) collective-permute-start(f32[2,18,1,128]{3,0,2,1:T(2,128)S(1)} %copy.147), channel_id=1, source_target_pairs={{0,2},{2,4},{4,6},{1,3},{3,5},{5,7},{8,10},{10,12},{12,14},{9,11},... | collective-permute-start | bytes 55304 | tf_op jit(solution)/shard_map/ppermute | solution.py:22
  226.7 5.7 %collective-permute-start.21 = (f32[2,18,1,128]{3,0,2,1:T(2,128)S(1)}, f32[2,18,1,128]{3,0,2,1:T(2,128)S(1)}, u32[]{:S(2)}, u32[]{:S(2)}) collective-permute-start(f32[2,18,1,128]{3,0,2,1:T(2,128)S(1)} %copy.148), channel_id=1, source_target_pairs={{2,0},{4,2},{6,4},{3,1},{5,3},{7,5},{10,8},{12,10},{14,12},{11,9},... | collective-permute-start | bytes 55304 | tf_op jit(solution)/shard_map/ppermute | solution.py:24
  236.0 6.9 %collective-permute-start.23 = (f32[2,18,34,1]{2,0,3,1:T(2,128)S(1)}, f32[2,18,34,1]{2,0,3,1:T(2,128)S(1)}, u32[]{:S(2)}, u32[]{:S(2)}) collective-permute-start(f32[2,18,34,1]{2,0,3,1:T(2,128)S(1)} %copy.118), channel_id=1, source_target_pairs={{1,0},{3,2},{5,4},{7,6},{9,8},{11,10},{13,12},{15,14},{17,16},{19,... | collective-permute-start | bytes 14696 | tf_op jit(solution)/shard_map/ppermute | solution.py:24
  241.4 7.2 %collective-permute-start.22 = (f32[2,18,34,1]{2,0,3,1:T(2,128)S(1)}, f32[2,18,34,1]{2,0,3,1:T(2,128)S(1)}, u32[]{:S(2)}, u32[]{:S(2)}) collective-permute-start(f32[2,18,34,1]{2,0,3,1:T(2,128)S(1)} %copy.117), channel_id=1, source_target_pairs={{0,1},{2,3},{4,5},{6,7},{8,9},{10,11},{12,13},{14,15},{16,17},{18,... | collective-permute-start | bytes 14696 | tf_op jit(solution)/shard_map/ppermute | solution.py:22
  298.0 3.4 collective-permute-start.25
  301.5 7.7 %collective-permute-start.27 = (f32[2,20,2,128]{3,2,1,0:T(2,128)S(1)}, f32[2,20,2,128]{3,2,1,0:T(2,128)S(1)}, u32[]{:S(2)}, u32[]{:S(2)}) collective-permute-start(f32[2,20,2,128]{3,2,1,0:T(2,128)S(1)} %get-tuple-element.123), channel_id=1, source_target_pairs={{2,0},{4,2},{6,4},{3,1},{5,3},{7,5},{10,8},{12,10},{14,12},{11,9},... | collective-permute-start | bytes 122888 | tf_op jit(solution)/shard_map/ppermute | solution.py:24
  302.8 8.7 %collective-permute-start.26 = (f32[2,20,2,128]{3,2,1,0:T(2,128)S(1)}, f32[2,20,2,128]{3,2,1,0:T(2,128)S(1)}, u32[]{:S(2)}, u32[]{:S(2)}) collective-permute-start(f32[2,20,2,128]{3,2,1,0:T(2,128)S(1)} %get-tuple-element.122), channel_id=1, source_target_pairs={{0,2},{2,4},{4,6},{1,3},{3,5},{5,7},{8,10},{10,12},{12,14},{9,11},... | collective-permute-start | bytes 122888 | tf_op jit(solution)/shard_map/ppermute | solution.py:22
  315.3 3.5 collective-permute-start.29
  317.1 7.5 %collective-permute-start.28 = (f32[2,20,36,2]{2,1,3,0:T(8,128)S(1)}, f32[2,20,36,2]{2,1,3,0:T(8,128)S(1)}, u32[]{:S(2)}, u32[]{:S(2)}) collective-permute-start(f32[2,20,36,2]{2,1,3,0:T(8,128)S(1)} %copy.126), channel_id=1, source_target_pairs={{0,1},{2,3},{4,5},{6,7},{8,9},{10,11},{12,13},{14,15},{16,17},{18,... | collective-permute-start | bytes 34568 | tf_op jit(solution)/shard_map/ppermute | solution.py:22
  361.5 4.1 collective-permute-start.30
  364.3 5.2 %collective-permute-start.31 = (f32[2,1,32,128]{3,2,1,0:T(8,128)S(1)}, f32[2,1,32,128]{3,2,1,0:T(8,128)S(1)}, u32[]{:S(2)}, u32[]{:S(2)}) collective-permute-start(f32[2,1,32,128]{3,2,1,0:T(8,128)S(1)} %get-tuple-element.135), channel_id=1, source_target_pairs={{8,0},{16,8},{24,16},{32,24},{40,32},{48,40},{56,48},{64,56},{72,6... | collective-permute-start | bytes 98312 | tf_op jit(solution)/shard_map/ppermute | solution.py:24
  369.6 5.0 %collective-permute-start.32 = (f32[2,18,1,128]{3,0,2,1:T(2,128)S(1)}, f32[2,18,1,128]{3,0,2,1:T(2,128)S(1)}, u32[]{:S(2)}, u32[]{:S(2)}) collective-permute-start(f32[2,18,1,128]{3,0,2,1:T(2,128)S(1)} %copy.149), channel_id=1, source_target_pairs={{0,2},{2,4},{4,6},{1,3},{3,5},{5,7},{8,10},{10,12},{12,14},{9,11},... | collective-permute-start | bytes 55304 | tf_op jit(solution)/shard_map/ppermute | solution.py:22
  371.6 5.7 %collective-permute-start.33 = (f32[2,18,1,128]{3,0,2,1:T(2,128)S(1)}, f32[2,18,1,128]{3,0,2,1:T(2,128)S(1)}, u32[]{:S(2)}, u32[]{:S(2)}) collective-permute-start(f32[2,18,1,128]{3,0,2,1:T(2,128)S(1)} %copy.150), channel_id=1, source_target_pairs={{2,0},{4,2},{6,4},{3,1},{5,3},{7,5},{10,8},{12,10},{14,12},{11,9},... | collective-permute-start | bytes 55304 | tf_op jit(solution)/shard_map/ppermute | solution.py:24
  382.3 7.2 %collective-permute-start.34 = (f32[2,18,34,1]{2,0,3,1:T(2,128)S(1)}, f32[2,18,34,1]{2,0,3,1:T(2,128)S(1)}, u32[]{:S(2)}, u32[]{:S(2)}) collective-permute-start(f32[2,18,34,1]{2,0,3,1:T(2,128)S(1)} %copy.139), channel_id=1, source_target_pairs={{0,1},{2,3},{4,5},{6,7},{8,9},{10,11},{12,13},{14,15},{16,17},{18,... | collective-permute-start | bytes 14696 | tf_op jit(solution)/shard_map/ppermute | solution.py:22
  (45 other events, 365.6 us)
where the time goes:
time: 448 us; the launch traced here: 439 us
  blocking collectives  122 us (27%)
  other arithmetic  105 us (23%)
  starting transfers between devices  83.4 us (19%)
  local copies, waits for them, and re-layouts  75.5 us (17%)
  waiting for transfers between devices  47.3 us (11%)
  between operations  6.17 us (1%)
    psum x15, blocking collectives, one_axis_at_a_time(): return functools.reduce(lax.psum, axes, value)  122 us
    ppermute x18, starting transfers between devices, padded_2(): lax.ppermute(tail, axis, [(i, (i + 1) % count) for i in range(ends)])  42 us
    ppermute x18, starting transfers between devices, padded_2(): lax.ppermute(head, axis, [((i + 1) % count, i) for i in range(ends)])  41.4 us
    unnamed x15, other arithmetic  28.1 us
    ppermute x18, waiting for transfers between devices, padded_2(): lax.ppermute(head, axis, [((i + 1) % count, i) for i in range(ends)])  24.1 us
    ppermute x18, waiting for transfers between devices, padded_2(): lax.ppermute(tail, axis, [(i, (i + 1) % count) for i in range(ends)])  23.3 us
    another operation x5, other arithmetic, coupling_terms(): return -2.0 * jnp.stack([first_div, second_div])  16.9 us
    another operation x5, other arithmetic, local(): smooth = jnp.stack([laplace_padded(padded[0]), laplace_padded(padded[1])])  15.4 us
  transfers between devices with their start and end apart: 36, of which 17 were waited for; matrix products, arithmetic and copies ran while one was open for 6% of the time, Pallas kernels for 0%

commit v1 on v0

v1 whole, which is shorter than its diff:
```python
import jax
import jax.numpy as jnp
from jax import lax
from jax.experimental import pallas as pl
from jax.experimental.pallas import tpu as pltpu
from jax.sharding import PartitionSpec as P

ALL = ("gx", "gy", "gz")
F32 = jnp.float32
NX, NY, NZ = 16, 32, 128
D, DW = 7, 5
X0, Y0 = 7, 8
XE, YE = NX + 2 * D, 56
GRID_X, GRID_Y = 256, 128
EDGE_ROWS = 224
COUPLE = 0.05 * -2.0 * 0.0625


def lane_ids(rows):
    return lax.broadcasted_iota(jnp.int32, (rows, NZ), 1)


def row_ids(rows):
    return lax.broadcasted_iota(jnp.int32, (rows, NZ), 0)


def face_layers():
    return ((0, D, 0), (1, DW, 2 * D), (2, DW, 2 * (D + DW)))


def pack_faces(c, w, t, xp, xn, yp, yn, z, zp, zn):
    iz = lax.axis_index("gz")
    fields = (c, w, t)
    for f, depth, at in face_layers():
        for layer in range(depth):
            for m in range(2):
                xp[at + 2 * layer + m] = fields[f][m, NX - depth + layer]
                xn[at + 2 * layer + m] = fields[f][m, layer]
    for m in range(2):
        for x in range(NX):
            row = (m * NX + x) * (D + 2 * DW)
            for f, depth in ((0, D), (1, DW), (2, DW)):
                yp[row : row + depth] = fields[f][m, x, NY - depth : NY]
                yn[row : row + depth] = fields[f][m, x, 0:depth]
                row += depth
    lane = lane_ids(NY)
    for m in range(2):
        packed = []
        for f in range(3):
            acc = jnp.zeros((NY, NZ), F32)
            for x in range(NX):
                shift = (8 * x + 8 * (1 - iz)) % NZ
                moved = pltpu.roll(fields[f][m, x], shift, 1)
                acc = jnp.where(lane // 8 == x, moved, acc)
            z[f, m] = acc
            packed.append(acc)
        zp[m] = jnp.where(
            lane < 48,
            pltpu.roll(packed[0], 48, 1),
            jnp.where(lane < 80, pltpu.roll(packed[1], 80, 1), pltpu.roll(packed[2], 112, 1)),
        )
        zn[m] = jnp.where(
            lane < 48,
            packed[0],
            jnp.where(lane < 80, pltpu.roll(packed[1], 48, 1), pltpu.roll(packed[2], 80, 1)),
        )


def xy_pieces():
    row = 0
    for side in range(2):
        for m in range(2):
            for f, depth, at in face_layers():
                for away in range(1, depth):
                    count = depth - away
                    layer = depth - away if side == 0 else away - 1
                    place = X0 - away if side == 0 else X0 + NX - 1 + away
                    yield row, count, side, m, f, at + 2 * layer + m, place
                    row += count


def yz_pieces():
    row = 164
    for m in range(2):
        for f, count in ((0, 6), (1, 4), (2, 4)):
            yield row, count, m, f
            row += count


def xyz_pieces():
    row = 192
    for side in range(2):
        for m in range(2):
            yield row, 6, side, m
            row += 6


def pack_edges(xm, xq, z, zm, zq, yp, yn):
    for row, count, side, m, f, layer, place in xy_pieces():
        face = (xm, xq)[side]
        yp[row : row + count] = face[layer, NY - count : NY]
        yn[row : row + count] = face[layer, 0:count]
    for row, count, m, f in yz_pieces():
        yp[row : row + count] = z[f, m, NY - count : NY]
        yn[row : row + count] = z[f, m, 0:count]
    for row, count, side, m in xyz_pieces():
        face = (zm, zq)[side]
        yp[row : row + count] = face[m, NY - count : NY]
        yn[row : row + count] = face[m, 0:count]
    yp[216:224] = jnp.zeros((8, NZ), F32)
    yn[216:224] = jnp.zeros((8, NZ), F32)


def groups():
    for f, first, count in ((0, 0, 6), (1, 6, 4), (2, 10, 4)):
        for k in range(count):
            yield f, first + k, k, count


def assemble(c, w, t, xm, xq, ym, yq, z, zm, zq, em, eq, fields):
    iz = lax.axis_index("gz")

    def clear(x, carry):
        for field in fields:
            for tile in range(2):
                for m in range(2):
                    field[tile, m, x] = jnp.zeros((YE, NZ), F32)
        return carry

    lax.fori_loop(0, XE, clear, 0)

    def own(x, carry):
        for field, source in zip(fields, (c, w, t)):
            for m in range(2):
                field[0, m, X0 + x, Y0 : Y0 + NY] = source[m, x]
        return carry

    lax.fori_loop(0, NX, own, 0)
    top = Y0 + NY
    for f, depth, at in face_layers():
        for layer in range(depth):
            for m in range(2):
                fields[f][0, m, X0 - depth + layer, Y0:top] = xm[at + 2 * layer + m]
                fields[f][0, m, X0 + NX + layer, Y0:top] = xq[at + 2 * layer + m]
    for m in range(2):
        for x in range(NX):
            row = (m * NX + x) * (D + 2 * DW)
            for f, depth in ((0, D), (1, DW), (2, DW)):
                fields[f][0, m, X0 + x, Y0 - depth : Y0] = ym[row : row + depth]
                fields[f][0, m, X0 + x, top : top + depth] = yq[row : row + depth]
                row += depth
    for row, count, side, m, f, layer, place in xy_pieces():
        fields[f][0, m, place, Y0 - count : Y0] = em[row : row + count]
        fields[f][0, m, place, top : top + count] = eq[row : row + count]

    def keep(rows):
        lane = lane_ids(rows)
        return (lane // 8) == 15 * iz

    keep_all, keep_few = keep(NY), keep(8)

    def unpack(rows, group, mask):
        shift = (2 * NZ - 8 * (group + iz)) % NZ
        return jnp.where(mask, pltpu.roll(rows, shift, 1), 0.0)

    for m in range(2):
        for f in range(3):
            packed = z[f, m]
            for x in range(NX):
                fields[f][1, m, X0 + x, Y0:top] = unpack(packed, x, keep_all)
    for row, count, m, f in yz_pieces():
        low, high = em[row : row + 8], eq[row : row + 8]
        for x in range(NX):
            fields[f][1, m, X0 + x, Y0 - count : Y0] = unpack(low, x, keep_few)[0:count]
            fields[f][1, m, X0 + x, top : top + count] = unpack(high, x, keep_few)[0:count]
    for side in range(2):
        for m in range(2):
            packed = (zm, zq)[side][m]
            for f, group, k, count in groups():
                place = X0 - count + k if side == 0 else X0 + NX + k
                fields[f][1, m, place, Y0:top] = unpack(packed, group, keep_all)
    for row, rows, side, m in xyz_pieces():
        low, high = em[row : row + 8], eq[row : row + 8]
        for f, group, k, count in groups():
            place = X0 - count + k if side == 0 else X0 + NX + k
            fields[f][1, m, place, Y0 - rows : Y0] = unpack(low, group, keep_few)[0:rows]
            fields[f][1, m, place, top : top + rows] = unpack(high, group, keep_few)[0:rows]


def cross(a, b):
    return (
        a[1] * b[2] - a[2] * b[1],
        a[2] * b[0] - a[0] * b[2],
        a[0] * b[1] - a[1] * b[0],
    )


def z_pairs(main, halo, first, last):
    main_up, halo_up = pltpu.roll(main, NZ - 1, 1), pltpu.roll(halo, NZ - 1, 1)
    main_down, halo_down = pltpu.roll(main, 1, 1), pltpu.roll(halo, 1, 1)
    return (
        (jnp.where(last, halo_up, main_up), jnp.where(first, halo_down, main_down)),
        (jnp.where(last, main_up, halo_up), jnp.where(first, main_down, halo_down)),
    )


def gradients(C, W, T, G, Fl, depth):
    ix, iy, iz = lax.axis_index("gx"), lax.axis_index("gy"), lax.axis_index("gz")
    lane = lane_ids(8)
    first, last = lane == 0, lane == NZ - 1
    halo_lanes = (lane // 8) == 15 * iz

    def masks(x, y):
        place = ix * NX + (x - X0)
        inside_x = jnp.logical_and(place >= 0, place < GRID_X).astype(F32)
        row = row_ids(8) + (iy * NY + (y - Y0))
        own = jnp.where(jnp.logical_and(row >= 0, row < GRID_Y), inside_x, 0.0)
        return own, jnp.where(halo_lanes, own, 0.0)

    def flux_at(x, carry):
        for k in range(-(-(NY + 2 * depth + 2) // 8)):
            y = Y0 - depth - 1 + 8 * k
            keep = masks(x, y)
            slope = [[None, None], [None, None]]
            for m in range(2):
                shifted = z_pairs(C[0, m, x, y : y + 8], C[1, m, x, y : y + 8], first, last)
                for tile in range(2):
                    slope[tile][m] = (
                        C[tile, m, x + 1, y : y + 8] - C[tile, m, x - 1, y : y + 8],
                        C[tile, m, x, y + 1 : y + 9] - C[tile, m, x, y - 1 : y + 7],
                        shifted[tile][0] - shifted[tile][1],
                    )
            for tile in range(2):
                a, b = slope[tile]
                crossed = tuple(keep[tile] * v for v in cross(a, b))
                flux = cross(b, crossed) + cross(crossed, a)
                for n in range(6):
                    Fl[tile, n, x, y : y + 8] = flux[n]
        return carry

    lax.fori_loop(X0 - depth - 1, X0 + NX + depth + 1, flux_at, 0)

    def gradient_at(x, carry):
        for k in range(-(-(NY + 2 * depth) // 8)):
            y = Y0 - depth + 8 * k
            here, up, down = slice(y, y + 8), slice(y + 1, y + 9), slice(y - 1, y + 7)
            keep = masks(x, y)
            for m in range(2):
                n = 3 * m
                own = [C[tile, m, x, here] for tile in range(2)]
                around = z_pairs(own[0], own[1], first, last)
                along = z_pairs(Fl[0, n + 2, x, here], Fl[1, n + 2, x, here], first, last)
                for tile in range(2):
                    near = around[tile][0] + around[tile][1]
                    near = near + (C[tile, m, x + 1, here] + C[tile, m, x - 1, here])
                    near = near + (C[tile, m, x, up] + C[tile, m, x, down])
                    spread = along[tile][0] - along[tile][1]
                    spread = spread + (Fl[tile, n, x + 1, here] - Fl[tile, n, x - 1, here])
                    spread = spread + (Fl[tile, n + 1, x, up] - Fl[tile, n + 1, x, down])
                    value = W[tile, m, x, here] * (own[tile] - T[tile, m, x, here])
                    value = value + (6.0 * own[tile] - near) + COUPLE * spread
                    G[tile, m, x, here] = keep[tile] * value
        return carry

    lax.fori_loop(X0 - depth, X0 + NX + depth, gradient_at, 0)


def totals(W, G, applied, sums):
    lane = lane_ids(8)
    first, last = lane == 0, lane == NZ - 1

    def body(x, carry):
        norm, curve = carry
        for k in range(NY // 8):
            y = Y0 + 8 * k
            here, up, down = slice(y, y + 8), slice(y + 1, y + 9), slice(y - 1, y + 7)
            for m in range(2):
                own = G[0, m, x, here]
                above = pltpu.roll(own, NZ - 1, 1)
                above = jnp.where(last, pltpu.roll(G[1, m, x, here], NZ - 1, 1), above)
                near = above + G[0, m, x + 1, here] + G[0, m, x, up]
                if applied is None:
                    near = near + near
                else:
                    below = pltpu.roll(own, 1, 1)
                    below = jnp.where(first, pltpu.roll(G[1, m, x, here], 1, 1), below)
                    near = near + below + G[0, m, x - 1, here] + G[0, m, x, down]
                value = W[0, m, x, here] * own + (6.0 * own - near)
                if applied is not None:
                    applied[m, x - X0, 8 * k : 8 * k + 8] = value
                norm = norm + own * own
                curve = curve + own * value
        return norm, curve

    zero = jnp.zeros((8, NZ), F32)
    norm, curve = lax.fori_loop(X0, X0 + NX, body, (zero, zero))
    norm, curve = jnp.sum(norm), jnp.sum(curve)
    row = jnp.where(lane == 0, norm, jnp.where(lane == 1, curve, 0.0))
    for k in range(sums.shape[0] // 8):
        sums[8 * k : 8 * k + 8] = row


def step_of(gathered):
    column = jnp.sum(gathered[...], axis=0, keepdims=True)
    lane = lane_ids(1)
    norm = jnp.sum(jnp.where(lane == 0, column, 0.0), axis=1, keepdims=True)
    curve = jnp.sum(jnp.where(lane == 1, column, 0.0), axis=1, keepdims=True)
    return jnp.broadcast_to(norm, (8, NZ)) / jnp.broadcast_to(curve, (8, NZ))


def moved(C, G, step, New, depth):
    def body(x, carry):
        for k in range(-(-(NY + 2 * depth) // 8)):
            y = Y0 - depth + 8 * k
            for tile in range(2):
                for m in range(2):
                    here = (tile, m, x, slice(y, y + 8))
                    New[here] = C[here] - step * G[here]
        return carry

    lax.fori_loop(X0 - depth, X0 + NX + depth, body, 0)


def first_step(*refs):
    blocks, (C, W, T, G, sums, Fl) = refs[:12], refs[12:]
    assemble(*blocks, (C, W, T))
    gradients(C, W, T, G, Fl, 5)
    totals(W, G, None, sums)


def next_step(C, W, T, G, gathered, New, Gnew, sums, Fl):
    moved(C, G, step_of(gathered), New, 5)
    gradients(New, W, T, Gnew, Fl, 3)
    totals(W, Gnew, None, sums)


def last_step(C, W, T, G, gathered, current, gradient, applied, sums, New, Gnew, Fl):
    moved(C, G, step_of(gathered), New, 3)
    gradients(New, W, T, Gnew, Fl, 1)
    totals(W, Gnew, applied, sums)

    def body(x, carry):
        for m in range(2):
            current[m, x] = New[0, m, X0 + x, Y0 : Y0 + NY]
            gradient[m, x] = Gnew[0, m, X0 + x, Y0 : Y0 + NY]
        return carry

    lax.fori_loop(0, NX, body, 0)


def finish(current, gradient, gathered, updated):
    step = step_of(gathered)

    def body(x, carry):
        for m in range(2):
            for k in range(NY // 8):
                here = (m, x, slice(8 * k, 8 * k + 8))
                updated[here] = current[here] - step * gradient[here]
        return carry

    lax.fori_loop(0, NX, body, 0)


def call(body, name, outs, scratch=(), **more):
    return pl.pallas_call(
        body,
        out_shape=tuple(jax.ShapeDtypeStruct(s, F32) for s in outs),
        scratch_shapes=[pltpu.VMEM(s, F32) for s in scratch],
        compiler_params=pltpu.CompilerParams(vmem_limit_bytes=48 * 1024 * 1024),
        name=name,
        **more,
    )


def local(models, targets, weights):
    nx, ny = lax.axis_size("gx"), lax.axis_size("gy")
    devices = nx * ny * 2
    block = (2, NX, NY, NZ)
    x_face = (2 * (D + 2 * DW), NY, NZ)
    y_face = (2 * NX * (D + 2 * DW), NZ)
    z_edge = (2, NY, NZ)
    xp, xn, yp, yn, z, zp, zn = call(
        pack_faces, "pack_faces", (x_face, x_face, y_face, y_face, (3, 2, NY, NZ), z_edge, z_edge)
    )(models, weights, targets)
    up_x = [(i, i + 1) for i in range(nx - 1)]
    down_x = [(i + 1, i) for i in range(nx - 1)]
    up_y = [(i, i + 1) for i in range(ny - 1)]
    down_y = [(i + 1, i) for i in range(ny - 1)]
    up_xz = [(2 * i + k, 2 * i + 2 + 1 - k) for i in range(nx - 1) for k in range(2)]
    down_xz = [(2 * i + 2 + k, 2 * i + 1 - k) for i in range(nx - 1) for k in range(2)]
    xm, xq = lax.ppermute(xp, "gx", up_x), lax.ppermute(xn, "gx", down_x)
    ym, yq = lax.ppermute(yp, "gy", up_y), lax.ppermute(yn, "gy", down_y)
    zz = lax.ppermute(z, "gz", [(0, 1), (1, 0)])
    zm, zq = lax.ppermute(zp, ("gx", "gz"), up_xz), lax.ppermute(zn, ("gx", "gz"), down_xz)
    edge = (EDGE_ROWS, NZ)
    ep, en = call(pack_edges, "pack_edges", (edge, edge))(xm, xq, zz, zm, zq)
    em, eq = lax.ppermute(ep, "gy", up_y), lax.ppermute(en, "gy", down_y)

    wide = (2, 2, XE, YE, NZ)
    flux = (2, 6, XE, YE, NZ)
    rows = (devices, NZ)

    def gather(sums):
        return lax.all_to_all(sums, ALL, 0, 0, tiled=True)

    C, W, T, G, sums = call(first_step, "first_step", (wide, wide, wide, wide, rows), (flux,))(
        models, weights, targets, xm, xq, ym, yq, zz, zm, zq, em, eq
    )
    C, G, sums = call(next_step, "next_step", (wide, wide, rows), (flux,))(C, W, T, G, gather(sums))
    current, gradient, applied, sums = call(
        last_step, "last_step", (block, block, block, rows), (wide, wide, flux)
    )(C, W, T, G, gather(sums))
    (updated,) = call(finish, "finish", (block,))(current, gradient, gather(sums))
    return updated, applied


def solution(mesh):
    spec = P(None, "gx", "gy", "gz")
    return jax.shard_map(
        local, mesh=mesh, in_specs=(spec, spec, spec), out_specs=(spec, spec), check_vma=False
    )
```

time: 448 us -> 141 us (0.31)
  the two profiles are of different devices: /device:TPU:16 before, /device:TPU:1 now
where the time goes in v1:
time: 141 us; the launch traced here: 140 us
  blocking collectives  49.5 us (35%)
  Pallas kernels  46.6 us (33%)
  starting transfers between devices  24.2 us (17%)
  waiting for transfers between devices  14.9 us (11%)
  local copies, waits for them, and re-layouts  4.16 us (3%)
    all_to_all x3, blocking collectives, gather(): return lax.all_to_all(sums, ALL, 0, 0, tiled=True)  49.5 us
    pallas_call x1, Pallas kernels, local(): call(first_step, 'first_step', (wide, wide, wide, wide, rows), (flux,))  17 us
    pallas_call x1, Pallas kernels, local(): call(next_step, 'next_step', (wide, wide, rows), (flux,))  15.2 us
    pallas_call x1, Pallas kernels, local(): call(last_step, 'last_step', (block, block, block, rows), (wide, wide, fl...  12.7 us
    ppermute x2, starting transfers between devices, local(): xm, xq = (lax.ppermute(xp, 'gx', up_x), lax.ppermute(xn, 'gx', down_x))  6.5 us
    ppermute x1, waiting for transfers between devices, local(): lax.ppermute(zn, ('gx', 'gz'), down_xz)  6.06 us
    ppermute x2, starting transfers between devices, local(): em, eq = (lax.ppermute(ep, 'gy', up_y), lax.ppermute(en, 'gy', down_y))  5.58 us
    ppermute x1, starting transfers between devices, local(): lax.ppermute(zp, ('gx', 'gz'), up_xz)  5.08 us
  transfers between devices with their start and end apart: 9, of which 4 were waited for; matrix products, arithmetic and copies ran while one was open for 0% of the time, Pallas kernels for 0%

profile of v1, /device:TPU:1, one launch (start us, length us, event | category | flops | bytes accessed | tf_op | source)
XLA Modules:
  0.0 140.2 jit_solution(12744845668181239590)
XLA Ops:
  0.6 0.0 copy-start
  0.6 1.0 copy-done
  1.7 0.0 copy-start.1
  1.7 1.0 copy-done.1
  2.7 1.0 copy-done.2
  3.8 0.7 pack_faces.1
  4.4 4.6 %collective-permute-start = (f32[34,32,128]{2,1,0:T(8,128)S(1)}, f32[34,32,128]{2,1,0:T(8,128)S(1)}, u32[]{:S(2)}, u32[]{:S(2)}) collective-permute-start(f32[34,32,128]{2,1,0:T(8,128)S(1)} %get-tuple-element.23), channel_id=1, source_target_pairs={{0,8},{8,16},{16,24},{24,32},{32,40},{40,48},{48,56},{56,64},{64,7... | collective-permute-start | bytes 1671176 | tf_op jit(solution)/shard_map/ppermute | solution.py:391
  9.0 1.9 %collective-permute-start.1 = (f32[34,32,128]{2,1,0:T(8,128)S(1)}, f32[34,32,128]{2,1,0:T(8,128)S(1)}, u32[]{:S(2)}, u32[]{:S(2)}) collective-permute-start(f32[34,32,128]{2,1,0:T(8,128)S(1)} %get-tuple-element.24), channel_id=1, source_target_pairs={{8,0},{16,8},{24,16},{32,24},{40,32},{48,40},{56,48},{64,56},{72,6... | collective-permute-start | bytes 1671176 | tf_op jit(solution)/shard_map/ppermute | solution.py:391
  10.9 5.1 %collective-permute-start.5 = (f32[2,32,128]{2,1,0:T(8,128)S(1)}, f32[2,32,128]{2,1,0:T(8,128)S(1)}, u32[]{:S(2)}, u32[]{:S(2)}) collective-permute-start(f32[2,32,128]{2,1,0:T(8,128)S(1)} %get-tuple-element.28), channel_id=1, source_target_pairs={{0,9},{1,8},{8,17},{9,16},{16,25},{17,24},{24,33},{25,32},{32,41},... | collective-permute-start | bytes 98312 | tf_op jit(solution)/shard_map/ppermute | solution.py:394
  16.0 3.1 %collective-permute-start.2 = (f32[544,128]{1,0:T(8,128)S(1)}, f32[544,128]{1,0:T(8,128)S(1)}, u32[]{:S(2)}, u32[]{:S(2)}) collective-permute-start(f32[544,128]{1,0:T(8,128)S(1)} %get-tuple-element.25), channel_id=1, source_target_pairs={{0,2},{2,4},{4,6},{1,3},{3,5},{5,7},{8,10},{10,12},{12,14},{9,11},... | collective-permute-start | bytes 835592 | tf_op jit(solution)/shard_map/ppermute | solution.py:392
  19.2 1.3 collective-permute-start.3
  20.5 0.0 collective-permute-done.5.zm.refs_8_
  20.5 2.3 %collective-permute-start.6 = (f32[2,32,128]{2,1,0:T(8,128)S(1)}, f32[2,32,128]{2,1,0:T(8,128)S(1)}, u32[]{:S(2)}, u32[]{:S(2)}) collective-permute-start(f32[2,32,128]{2,1,0:T(8,128)S(1)} %get-tuple-element.29), channel_id=1, source_target_pairs={{8,1},{9,0},{16,9},{17,8},{24,17},{25,16},{32,25},{33,24},{40,33},... | collective-permute-start | bytes 98312 | tf_op jit(solution)/shard_map/ppermute | solution.py:394
  22.8 6.1 %collective-permute-done.6.zq.refs_9_ = f32[2,32,128]{2,1,0:T(8,128)S(1)} collective-permute-done((f32[2,32,128]{2,1,0:T(8,128)S(1)}, f32[2,32,128]{2,1,0:T(8,128)S(1)}, u32[]{:S(2)}, u32[]{:S(2)}) %collective-permute-start.6) | collective-permute-done | bytes 32800 | tf_op jit(solution)/shard_map/ppermute | solution.py:394
  28.8 0.4 collective-permute-start.4
  29.2 4.7 %collective-permute-done.4.z.refs_7_ = f32[3,2,32,128]{3,2,1,0:T(8,128)S(1)} collective-permute-done((f32[3,2,32,128]{3,2,1,0:T(8,128)S(1)}, f32[3,2,32,128]{3,2,1,0:T(8,128)S(1)}, u32[]{:S(2)}, u32[]{:S(2)}) %collective-permute-start.4) | collective-permute-done | bytes 98336 | tf_op jit(solution)/shard_map/ppermute | solution.py:393
  33.8 0.0 collective-permute-done.xm.refs_3_
  33.8 0.0 collective-permute-done.1.xq.refs_4_
  33.9 4.3 %collective-permute-start.7 = (f32[224,128]{1,0:T(8,128)S(1)}, f32[224,128]{1,0:T(8,128)S(1)}, u32[]{:S(2)}, u32[]{:S(2)}) collective-permute-start(f32[224,128]{1,0:T(8,128)S(1)} %get-tuple-element.30), channel_id=1, source_target_pairs={{0,2},{2,4},{4,6},{1,3},{3,5},{5,7},{8,10},{10,12},{12,14},{9,11},... | collective-permute-start | bytes 344072 | tf_op jit(solution)/shard_map/ppermute | solution.py:397
  38.2 1.3 collective-permute-start.8
  39.5 0.0 collective-permute-done.2.refs_5_
  39.5 0.0 collective-permute-done.3.refs_6_
  39.5 0.6 collective-permute-done.7.refs_10_
  40.1 3.6 %collective-permute-done.8.refs_11_ = f32[224,128]{1,0:T(8,128)S(1)} collective-permute-done((f32[224,128]{1,0:T(8,128)S(1)}, f32[224,128]{1,0:T(8,128)S(1)}, u32[]{:S(2)}, u32[]{:S(2)}) %collective-permute-start.8) | collective-permute-done | bytes 114720 | tf_op jit(solution)/shard_map/ppermute | solution.py:397
  43.7 1.0 copy-done.3
  44.8 17.0 %first_step.1 = (f32[2,2,30,56,128]{4,3,2,1,0:T(8,128)}, f32[2,2,30,56,128]{4,3,2,1,0:T(8,128)}, f32[2,2,30,56,128]{4,3,2,1,0:T(8,128)}, f32[2,2,30,56,128]{4,3,2,1,0:T(8,128)}, f32[128,128]{1,0:T(8,128)S(1)}) custom-call(f32[2,16,32,128]{3,2,1,0:T(8,128)S(1)} %copy-done, f32[2,16,32,128]{3,2,1,0:T(8,128)S(1)} %copy-done.1, ...), custom_call_target="tpu_custom_call" | custom-call | tf_op jit(solution)/shard_map/first_step/pallas_call | solution.py:406
  61.8 21.8 %all_to_all.33 = f32[128,1,128]{2,1,0:T(1,128)S(1)} all-to-all(f32[128,1,128]{2,1,0:T(1,128)S(1)} %bitcast.15), channel_id=1, replica_groups=mesh['gx'=16,'gy'=4,'gz'=2] {'gx','gy','gz'}, dimensions={0} | all-to-all | bytes 131072 | tf_op jit(solution)/shard_map/all_to_all | solution.py:404
  83.6 15.2 %next_step.1 = (f32[2,2,30,56,128]{4,3,2,1,0:T(8,128)S(1)}, f32[2,2,30,56,128]{4,3,2,1,0:T(8,128)}, f32[128,128]{1,0:T(8,128)S(1)}) custom-call(f32[2,2,30,56,128]{4,3,2,1,0:T(8,128)} %get-tuple-element.32.C, f32[2,2,30,56,128]{4,3,2,1,0:T(8,128)} %get-tuple-element.33.W, f32[2,2,30,56,128]{4,3,2,1,0:T(8,128)} %get-tuple-element.34.T, ...), custom_call_target="tpu_custom_call" | custom-call | tf_op jit(solution)/shard_map/next_step/pallas_call | solution.py:409
  98.8 13.9 %all_to_all.34 = f32[128,1,128]{2,1,0:T(1,128)S(1)} all-to-all(f32[128,1,128]{2,1,0:T(1,128)S(1)} %bitcast.17), channel_id=1, replica_groups=mesh['gx'=16,'gy'=4,'gz'=2] {'gx','gy','gz'}, dimensions={0} | all-to-all | bytes 131072 | tf_op jit(solution)/shard_map/all_to_all | solution.py:404
  112.7 12.7 %last_step.1 = (f32[2,16,32,128]{3,2,1,0:T(8,128)S(1)}, f32[2,16,32,128]{3,2,1,0:T(8,128)S(1)}, f32[2,16,32,128]{3,2,1,0:T(8,128)}, f32[128,128]{1,0:T(8,128)S(1)}) custom-call(f32[2,2,30,56,128]{4,3,2,1,0:T(8,128)S(1)} %get-tuple-element.37.C, f32[2,2,30,56,128]{4,3,2,1,0:T(8,128)} %get-tuple-element.33.W, f32[2,2,30,56,128]{4,3,2,1,0:T(8,128)} %get-tuple-element.34.T, ...), custom_call_target="tpu_custom_call" | custom-call | tf_op jit(solution)/shard_map/last_step/pallas_call | solution.py:410
  125.3 13.9 %all_to_all.35 = f32[128,1,128]{2,1,0:T(1,128)S(1)} all-to-all(f32[128,1,128]{2,1,0:T(1,128)S(1)} %bitcast.16), channel_id=1, replica_groups=mesh['gx'=16,'gy'=4,'gz'=2] {'gx','gy','gz'}, dimensions={0} | all-to-all | bytes 131072 | tf_op jit(solution)/shard_map/all_to_all | solution.py:404
  139.2 1.0 finish.1
  (3 shorter events, 0.1 us)
Async XLA Ops:
  0.6 1.0 copy-start
  1.7 1.0 copy-start.1
  2.7 1.0 copy-start.2
  4.4 29.4 %collective-permute-start = (f32[34,32,128]{2,1,0:T(8,128)S(1)}, f32[34,32,128]{2,1,0:T(8,128)S(1)}, u32[]{:S(2)}, u32[]{:S(2)}) collective-permute-start(f32[34,32,128]{2,1,0:T(8,128)S(1)} %get-tuple-element.23), channel_id=1, source_target_pairs={{0,8},{8,16},{16,24},{24,32},{32,40},{40,48},{48,56},{56,64},{64,7... | collective-permute-start | bytes 1671176 | tf_op jit(solution)/shard_map/ppermute | solution.py:391
  9.0 24.8 %collective-permute-start.1 = (f32[34,32,128]{2,1,0:T(8,128)S(1)}, f32[34,32,128]{2,1,0:T(8,128)S(1)}, u32[]{:S(2)}, u32[]{:S(2)}) collective-permute-start(f32[34,32,128]{2,1,0:T(8,128)S(1)} %get-tuple-element.24), channel_id=1, source_target_pairs={{8,0},{16,8},{24,16},{32,24},{40,32},{48,40},{56,48},{64,56},{72,6... | collective-permute-start | bytes 1671176 | tf_op jit(solution)/shard_map/ppermute | solution.py:391
  10.9 9.5 %collective-permute-start.5 = (f32[2,32,128]{2,1,0:T(8,128)S(1)}, f32[2,32,128]{2,1,0:T(8,128)S(1)}, u32[]{:S(2)}, u32[]{:S(2)}) collective-permute-start(f32[2,32,128]{2,1,0:T(8,128)S(1)} %get-tuple-element.28), channel_id=1, source_target_pairs={{0,9},{1,8},{8,17},{9,16},{16,25},{17,24},{24,33},{25,32},{32,41},... | collective-permute-start | bytes 98312 | tf_op jit(solution)/shard_map/ppermute | solution.py:394
  16.0 23.5 %collective-permute-start.2 = (f32[544,128]{1,0:T(8,128)S(1)}, f32[544,128]{1,0:T(8,128)S(1)}, u32[]{:S(2)}, u32[]{:S(2)}) collective-permute-start(f32[544,128]{1,0:T(8,128)S(1)} %get-tuple-element.25), channel_id=1, source_target_pairs={{0,2},{2,4},{4,6},{1,3},{3,5},{5,7},{8,10},{10,12},{12,14},{9,11},... | collective-permute-start | bytes 835592 | tf_op jit(solution)/shard_map/ppermute | solution.py:392
  19.2 20.3 %collective-permute-start.3 = (f32[544,128]{1,0:T(8,128)S(1)}, f32[544,128]{1,0:T(8,128)S(1)}, u32[]{:S(2)}, u32[]{:S(2)}) collective-permute-start(f32[544,128]{1,0:T(8,128)S(1)} %get-tuple-element.26), channel_id=1, source_target_pairs={{2,0},{4,2},{6,4},{3,1},{5,3},{7,5},{10,8},{12,10},{14,12},{11,9},... | collective-permute-start | bytes 835592 | tf_op jit(solution)/shard_map/ppermute | solution.py:392
  20.5 8.3 %collective-permute-start.6 = (f32[2,32,128]{2,1,0:T(8,128)S(1)}, f32[2,32,128]{2,1,0:T(8,128)S(1)}, u32[]{:S(2)}, u32[]{:S(2)}) collective-permute-start(f32[2,32,128]{2,1,0:T(8,128)S(1)} %get-tuple-element.29), channel_id=1, source_target_pairs={{8,1},{9,0},{16,9},{17,8},{24,17},{25,16},{32,25},{33,24},{40,33},... | collective-permute-start | bytes 98312 | tf_op jit(solution)/shard_map/ppermute | solution.py:394
  28.8 5.0 %collective-permute-start.4 = (f32[3,2,32,128]{3,2,1,0:T(8,128)S(1)}, f32[3,2,32,128]{3,2,1,0:T(8,128)S(1)}, u32[]{:S(2)}, u32[]{:S(2)}) collective-permute-start(f32[3,2,32,128]{3,2,1,0:T(8,128)S(1)} %get-tuple-element.27), channel_id=1, source_target_pairs={{0,1},{1,0},{2,3},{3,2},{4,5},{5,4},{6,7},{7,6},{8,9},{9,8},{10,11... | collective-permute-start | bytes 294920 | tf_op jit(solution)/shard_map/ppermute | solution.py:393
  33.9 6.2 %collective-permute-start.7 = (f32[224,128]{1,0:T(8,128)S(1)}, f32[224,128]{1,0:T(8,128)S(1)}, u32[]{:S(2)}, u32[]{:S(2)}) collective-permute-start(f32[224,128]{1,0:T(8,128)S(1)} %get-tuple-element.30), channel_id=1, source_target_pairs={{0,2},{2,4},{4,6},{1,3},{3,5},{5,7},{8,10},{10,12},{12,14},{9,11},... | collective-permute-start | bytes 344072 | tf_op jit(solution)/shard_map/ppermute | solution.py:397
  38.2 5.5 %collective-permute-start.8 = (f32[224,128]{1,0:T(8,128)S(1)}, f32[224,128]{1,0:T(8,128)S(1)}, u32[]{:S(2)}, u32[]{:S(2)}) collective-permute-start(f32[224,128]{1,0:T(8,128)S(1)} %get-tuple-element.31), channel_id=1, source_target_pairs={{2,0},{4,2},{6,4},{3,1},{5,3},{7,5},{10,8},{12,10},{14,12},{11,9},... | collective-permute-start | bytes 344072 | tf_op jit(solution)/shard_map/ppermute | solution.py:397
  43.7 1.0 copy-start.3

commit v2 on v1

--- a/solution.py
+++ b/solution.py
@@ -4,6 +4,7 @@
 from jax.experimental import pallas as pl
 from jax.experimental.pallas import tpu as pltpu
 from jax.sharding import PartitionSpec as P
+
 
 ALL = ("gx", "gy", "gz")
 F32 = jnp.float32
@@ -117,9 +118,7 @@
             yield f, first + k, k, count
 
 
-def assemble(c, w, t, xm, xq, ym, yq, z, zm, zq, em, eq, fields):
-    iz = lax.axis_index("gz")
-
+def place_own(c, w, t, *fields):
     def clear(x, carry):
         for field in fields:
             for tile in range(2):
@@ -136,6 +135,10 @@
         return carry
 
     lax.fori_loop(0, NX, own, 0)
+
+
+def assemble(xm, xq, ym, yq, z, zm, zq, em, eq, fields):
+    iz = lax.axis_index("gz")
     top = Y0 + NY
     for f, depth, at in face_layers():
         for layer in range(depth):
@@ -322,8 +325,8 @@
 
 
 def first_step(*refs):
-    blocks, (C, W, T, G, sums, Fl) = refs[:12], refs[12:]
-    assemble(*blocks, (C, W, T))
+    halos, (C, W, T, G, sums, Fl) = refs[3:12], refs[12:]
+    assemble(*halos, (C, W, T))
     gradients(C, W, T, G, Fl, 5)
     totals(W, G, None, sums)
 
@@ -361,14 +364,13 @@
     lax.fori_loop(0, NX, body, 0)
 
 
-def call(body, name, outs, scratch=(), **more):
+def call(body, outs, scratch=(), mib=2, alias=None):
     return pl.pallas_call(
         body,
         out_shape=tuple(jax.ShapeDtypeStruct(s, F32) for s in outs),
         scratch_shapes=[pltpu.VMEM(s, F32) for s in scratch],
-        compiler_params=pltpu.CompilerParams(vmem_limit_bytes=48 * 1024 * 1024),
-        name=name,
-        **more,
+        compiler_params=pltpu.CompilerParams(vmem_limit_bytes=mib * 1024 * 1024),
+        input_output_aliases=alias or {},
     )
 
 
@@ -376,11 +378,14 @@
     nx, ny = lax.axis_size("gx"), lax.axis_size("gy")
     devices = nx * ny * 2
     block = (2, NX, NY, NZ)
+    wide = (2, 2, XE, YE, NZ)
+    flux = (2, 6, XE, YE, NZ)
+    rows = (devices, NZ)
     x_face = (2 * (D + 2 * DW), NY, NZ)
     y_face = (2 * NX * (D + 2 * DW), NZ)
     z_edge = (2, NY, NZ)
     xp, xn, yp, yn, z, zp, zn = call(
-        pack_faces, "pack_faces", (x_face, x_face, y_face, y_face, (3, 2, NY, NZ), z_edge, z_edge)
+        pack_faces, (x_face, x_face, y_face, y_face, (3, 2, NY, NZ), z_edge, z_edge)
     )(models, weights, targets)
     up_x = [(i, i + 1) for i in range(nx - 1)]
     down_x = [(i + 1, i) for i in range(nx - 1)]
@@ -388,34 +393,36 @@
     down_y = [(i + 1, i) for i in range(ny - 1)]
     up_xz = [(2 * i + k, 2 * i + 2 + 1 - k) for i in range(nx - 1) for k in range(2)]
     down_xz = [(2 * i + 2 + k, 2 * i + 1 - k) for i in range(nx - 1) for k in range(2)]
-    xm, xq = lax.ppermute(xp, "gx", up_x), lax.ppermute(xn, "gx", down_x)
-    ym, yq = lax.ppermute(yp, "gy", up_y), lax.ppermute(yn, "gy", down_y)
+
     zz = lax.ppermute(z, "gz", [(0, 1), (1, 0)])
-    zm, zq = lax.ppermute(zp, ("gx", "gz"), up_xz), lax.ppermute(zn, ("gx", "gz"), down_xz)
+    zm = lax.ppermute(zp, ("gx", "gz"), up_xz)
+    zq = lax.ppermute(zn, ("gx", "gz"), down_xz)
+    ym = lax.ppermute(yp, "gy", up_y)
+    yq = lax.ppermute(yn, "gy", down_y)
+    xm = lax.ppermute(xp, "gx", up_x)
+    xq = lax.ppermute(xn, "gx", down_x)
+    C, W, T = call(place_own, (wide, wide, wide))(models, weights, targets)
     edge = (EDGE_ROWS, NZ)
-    ep, en = call(pack_edges, "pack_edges", (edge, edge))(xm, xq, zz, zm, zq)
+    ep, en = call(pack_edges, (edge, edge))(xm, xq, zz, zm, zq)
     em, eq = lax.ppermute(ep, "gy", up_y), lax.ppermute(en, "gy", down_y)
-
-    wide = (2, 2, XE, YE, NZ)
-    flux = (2, 6, XE, YE, NZ)
-    rows = (devices, NZ)
 
     def gather(sums):
         return lax.all_to_all(sums, ALL, 0, 0, tiled=True)
 
-    C, W, T, G, sums = call(first_step, "first_step", (wide, wide, wide, wide, rows), (flux,))(
-        models, weights, targets, xm, xq, ym, yq, zz, zm, zq, em, eq
+    C, W, T, G, sums = call(first_step, (wide, wide, wide, wide, rows), (flux,), 13, {0: 0, 1: 1, 2: 2})(
+        C, W, T, xm, xq, ym, yq, zz, zm, zq, em, eq
     )
-    C, G, sums = call(next_step, "next_step", (wide, wide, rows), (flux,))(C, W, T, G, gather(sums))
+    C, G, sums = call(next_step, (wide, wide, rows), (flux,), 13)(C, W, T, G, gather(sums))
     current, gradient, applied, sums = call(
-        last_step, "last_step", (block, block, block, rows), (wide, wide, flux)
+        last_step, (block, block, block, rows), (wide, wide, flux), 20
     )(C, W, T, G, gather(sums))
-    (updated,) = call(finish, "finish", (block,))(current, gradient, gather(sums))
+    (updated,) = call(finish, (block,))(current, gradient, gather(sums))
     return updated, applied
 
 
 def solution(mesh):
     spec = P(None, "gx", "gy", "gz")
+
     return jax.shard_map(
         local, mesh=mesh, in_specs=(spec, spec, spec), out_specs=(spec, spec), check_vma=False
     )

time: 141 us -> 124 us (0.88)
  Pallas kernels: 46.6 us -> 31.4 us
  waiting for transfers between devices: 14.9 us -> 13.1 us
    pallas_call x6 -> x7, Pallas kernels: 46.6 us -> 31.4 us  [the longest x1 11.4 us: local(): call(first_step, (wide, wide, wide, wide, rows), (flux,), 13, {0: 0, 1: 1...]
    ppermute x2, waiting for transfers between devices: 4.21 us -> 2.32 us  [local(): em, eq = (lax.ppermute(ep, 'gy', up_y), lax.ppermute(en, 'gy', down_y))]
  transfers between devices with their start and end apart: 9 -> 9, of which waited for: 4 -> 3; matrix products, arithmetic and copies ran while one was open for 0% -> 0% of each run, Pallas kernels for 0% -> 1%
where the time goes in v2:
time: 124 us; the launch traced here: 123 us
  blocking collectives  49.5 us (40%)
  Pallas kernels  31.4 us (25%)
  starting transfers between devices  24.2 us (20%)
  waiting for transfers between devices  13.1 us (11%)
  local copies, waits for them, and re-layouts  4.15 us (3%)
    all_to_all x3, blocking collectives, gather(): return lax.all_to_all(sums, ALL, 0, 0, tiled=True)  49.5 us
    pallas_call x1, Pallas kernels, local(): call(first_step, (wide, wide, wide, wide, rows), (flux,), 13, {0: 0, 1: 1...  11.4 us
    pallas_call x1, Pallas kernels, local(): call(next_step, (wide, wide, rows), (flux,), 13)(C, W, T, G, gather(sums))  8.77 us
    pallas_call x1, Pallas kernels, local(): call(last_step, (block, block, block, rows), (wide, wide, flux), 20)  8.68 us
    ppermute x1, waiting for transfers between devices, local(): zq = lax.ppermute(zn, ('gx', 'gz'), down_xz)  6.06 us
    ppermute x2, starting transfers between devices, local(): em, eq = (lax.ppermute(ep, 'gy', up_y), lax.ppermute(en, 'gy', down_y))  5.58 us
    ppermute x1, starting transfers between devices, local(): zm = lax.ppermute(zp, ('gx', 'gz'), up_xz)  5.08 us
    ppermute x1, waiting for transfers between devices, local(): zz = lax.ppermute(z, 'gz', [(0, 1), (1, 0)])  4.66 us
  transfers between devices with their start and end apart: 9, of which 3 were waited for; matrix products, arithmetic and copies ran while one was open for 0% of the time, Pallas kernels for 1%

profile of v2, /device:TPU:1, one launch (start us, length us, event | category | flops | bytes accessed | tf_op | source)
XLA Modules:
  0.0 123.1 jit_solution(13076496887464659925)
XLA Ops:
  0.6 1.0 copy-done
  1.7 1.0 copy-done.1
  2.7 1.0 copy-done.2
  3.8 0.7 shard_map.51
  4.4 4.6 %collective-permute-start = (f32[34,32,128]{2,1,0:T(8,128)S(1)}, f32[34,32,128]{2,1,0:T(8,128)S(1)}, u32[]{:S(2)}, u32[]{:S(2)}) collective-permute-start(f32[34,32,128]{2,1,0:T(8,128)S(1)} %get-tuple-element.29), channel_id=1, source_target_pairs={{0,8},{8,16},{16,24},{24,32},{32,40},{40,48},{48,56},{56,64},{64,7... | collective-permute-start | bytes 1671176 | tf_op jit(solution)/shard_map/ppermute | solution.py:402
  9.0 1.9 %collective-permute-start.1 = (f32[34,32,128]{2,1,0:T(8,128)S(1)}, f32[34,32,128]{2,1,0:T(8,128)S(1)}, u32[]{:S(2)}, u32[]{:S(2)}) collective-permute-start(f32[34,32,128]{2,1,0:T(8,128)S(1)} %get-tuple-element.30), channel_id=1, source_target_pairs={{8,0},{16,8},{24,16},{32,24},{40,32},{48,40},{56,48},{64,56},{72,6... | collective-permute-start | bytes 1671176 | tf_op jit(solution)/shard_map/ppermute | solution.py:403
  10.9 5.1 %collective-permute-start.5 = (f32[2,32,128]{2,1,0:T(8,128)S(1)}, f32[2,32,128]{2,1,0:T(8,128)S(1)}, u32[]{:S(2)}, u32[]{:S(2)}) collective-permute-start(f32[2,32,128]{2,1,0:T(8,128)S(1)} %get-tuple-element.34), channel_id=1, source_target_pairs={{0,9},{1,8},{8,17},{9,16},{16,25},{17,24},{24,33},{25,32},{32,41},... | collective-permute-start | bytes 98312 | tf_op jit(solution)/shard_map/ppermute | solution.py:398
  16.0 3.1 %collective-permute-start.2 = (f32[544,128]{1,0:T(8,128)S(1)}, f32[544,128]{1,0:T(8,128)S(1)}, u32[]{:S(2)}, u32[]{:S(2)}) collective-permute-start(f32[544,128]{1,0:T(8,128)S(1)} %get-tuple-element.31), channel_id=1, source_target_pairs={{0,2},{2,4},{4,6},{1,3},{3,5},{5,7},{8,10},{10,12},{12,14},{9,11},... | collective-permute-start | bytes 835592 | tf_op jit(solution)/shard_map/ppermute | solution.py:400
  19.2 1.3 %collective-permute-start.3 = (f32[544,128]{1,0:T(8,128)S(1)}, f32[544,128]{1,0:T(8,128)S(1)}, u32[]{:S(2)}, u32[]{:S(2)}) collective-permute-start(f32[544,128]{1,0:T(8,128)S(1)} %get-tuple-element.32), channel_id=1, source_target_pairs={{2,0},{4,2},{6,4},{3,1},{5,3},{7,5},{10,8},{12,10},{14,12},{11,9},... | collective-permute-start | bytes 835592 | tf_op jit(solution)/shard_map/ppermute | solution.py:401
  20.5 0.0 collective-permute-done.5.zm.refs_8_
  20.5 2.3 %collective-permute-start.6 = (f32[2,32,128]{2,1,0:T(8,128)S(1)}, f32[2,32,128]{2,1,0:T(8,128)S(1)}, u32[]{:S(2)}, u32[]{:S(2)}) collective-permute-start(f32[2,32,128]{2,1,0:T(8,128)S(1)} %get-tuple-element.35), channel_id=1, source_target_pairs={{8,1},{9,0},{16,9},{17,8},{24,17},{25,16},{32,25},{33,24},{40,33},... | collective-permute-start | bytes 98312 | tf_op jit(solution)/shard_map/ppermute | solution.py:399
  22.8 6.1 %collective-permute-done.6.zq.refs_9_ = f32[2,32,128]{2,1,0:T(8,128)S(1)} collective-permute-done((f32[2,32,128]{2,1,0:T(8,128)S(1)}, f32[2,32,128]{2,1,0:T(8,128)S(1)}, u32[]{:S(2)}, u32[]{:S(2)}) %collective-permute-start.6) | collective-permute-done | bytes 32800 | tf_op jit(solution)/shard_map/ppermute | solution.py:399
  28.8 0.4 collective-permute-start.4
  29.2 4.7 %collective-permute-done.4.z.refs_7_ = f32[3,2,32,128]{3,2,1,0:T(8,128)S(1)} collective-permute-done((f32[3,2,32,128]{3,2,1,0:T(8,128)S(1)}, f32[3,2,32,128]{3,2,1,0:T(8,128)S(1)}, u32[]{:S(2)}, u32[]{:S(2)}) %collective-permute-start.4) | collective-permute-done | bytes 98336 | tf_op jit(solution)/shard_map/ppermute | solution.py:397
  33.8 0.0 collective-permute-done.xm.refs_3_
  33.8 0.0 collective-permute-done.1.xq.refs_4_
  33.9 4.3 %collective-permute-start.7 = (f32[224,128]{1,0:T(8,128)S(1)}, f32[224,128]{1,0:T(8,128)S(1)}, u32[]{:S(2)}, u32[]{:S(2)}) collective-permute-start(f32[224,128]{1,0:T(8,128)S(1)} %get-tuple-element.36), channel_id=1, source_target_pairs={{0,2},{2,4},{4,6},{1,3},{3,5},{5,7},{8,10},{10,12},{12,14},{9,11},... | collective-permute-start | bytes 344072 | tf_op jit(solution)/shard_map/ppermute | solution.py:407
  38.2 1.3 %collective-permute-start.8 = (f32[224,128]{1,0:T(8,128)S(1)}, f32[224,128]{1,0:T(8,128)S(1)}, u32[]{:S(2)}, u32[]{:S(2)}) collective-permute-start(f32[224,128]{1,0:T(8,128)S(1)} %get-tuple-element.37), channel_id=1, source_target_pairs={{2,0},{4,2},{6,4},{3,1},{5,3},{7,5},{10,8},{12,10},{14,12},{11,9},... | collective-permute-start | bytes 344072 | tf_op jit(solution)/shard_map/ppermute | solution.py:407
  39.5 0.0 copy-start.3
  39.5 1.0 copy-done.3
  40.5 0.8 shard_map.50
  41.4 0.0 collective-permute-done.2.refs_5_
  41.4 0.0 collective-permute-done.3.refs_6_
  41.4 0.0 collective-permute-done.7.refs_10_
  41.4 2.3 %collective-permute-done.8.refs_11_ = f32[224,128]{1,0:T(8,128)S(1)} collective-permute-done((f32[224,128]{1,0:T(8,128)S(1)}, f32[224,128]{1,0:T(8,128)S(1)}, u32[]{:S(2)}, u32[]{:S(2)}) %collective-permute-start.8) | collective-permute-done | bytes 114720 | tf_op jit(solution)/shard_map/ppermute | solution.py:407
  43.7 11.4 %shard_map.53 = (f32[2,2,30,56,128]{4,3,2,1,0:T(8,128)S(1)}, f32[2,2,30,56,128]{4,3,2,1,0:T(8,128)S(1)}, f32[2,2,30,56,128]{4,3,2,1,0:T(8,128)S(1)}, f32[2,2,30,56,128]{4,3,2,1,0:T(8,128)S(1)}, f32[128,128]{1,0:T(8,128)S(1)}) custom-call(f32[2,2,30,56,128]{4,3,2,1,0:T(8,128)S(1)} %get-tuple-element.26.refs, ...), custom_call_target="tpu_custom_call", output_to_operand_aliasing={{0}: (0, {}), {1}: (1, {}), {2}: (2, {})} | custom-call | tf_op jit(solution)/shard_map/pallas_call | solution.py:412
  55.1 21.8 %all_to_all.33 = f32[128,1,128]{2,1,0:T(1,128)S(1)} all-to-all(f32[128,1,128]{2,1,0:T(1,128)S(1)} %bitcast.15), channel_id=1, replica_groups=mesh['gx'=16,'gy'=4,'gz'=2] {'gx','gy','gz'}, dimensions={0} | all-to-all | bytes 131072 | tf_op jit(solution)/shard_map/all_to_all | solution.py:410
  76.9 8.8 %shard_map.54 = (f32[2,2,30,56,128]{4,3,2,1,0:T(8,128)S(1)}, f32[2,2,30,56,128]{4,3,2,1,0:T(8,128)S(1)}, f32[128,128]{1,0:T(8,128)S(1)}) custom-call(f32[2,2,30,56,128]{4,3,2,1,0:T(8,128)S(1)} %get-tuple-element.38.C, f32[2,2,30,56,128]{4,3,2,1,0:T(8,128)S(1)} %get-tuple-element.39.W, f32[2,2,30,56,128]{4,3,2,1,0:T(8,128)S(1)} %get-tuple-element.40.T, ...), custom_call_target="tpu_custom_call" | custom-call | tf_op jit(solution)/shard_map/pallas_call | solution.py:415
  85.7 13.9 %all_to_all.34 = f32[128,1,128]{2,1,0:T(1,128)S(1)} all-to-all(f32[128,1,128]{2,1,0:T(1,128)S(1)} %bitcast.17), channel_id=1, replica_groups=mesh['gx'=16,'gy'=4,'gz'=2] {'gx','gy','gz'}, dimensions={0} | all-to-all | bytes 131072 | tf_op jit(solution)/shard_map/all_to_all | solution.py:410
  99.5 8.7 %shard_map.55 = (f32[2,16,32,128]{3,2,1,0:T(8,128)S(1)}, f32[2,16,32,128]{3,2,1,0:T(8,128)S(1)}, f32[2,16,32,128]{3,2,1,0:T(8,128)}, f32[128,128]{1,0:T(8,128)S(1)}) custom-call(f32[2,2,30,56,128]{4,3,2,1,0:T(8,128)S(1)} %get-tuple-element.43.C, f32[2,2,30,56,128]{4,3,2,1,0:T(8,128)S(1)} %get-tuple-element.39.W, ...), custom_call_target="tpu_custom_call" | custom-call | tf_op jit(solution)/shard_map/pallas_call | solution.py:416
  108.2 13.9 %all_to_all.35 = f32[128,1,128]{2,1,0:T(1,128)S(1)} all-to-all(f32[128,1,128]{2,1,0:T(1,128)S(1)} %bitcast.16), channel_id=1, replica_groups=mesh['gx'=16,'gy'=4,'gz'=2] {'gx','gy','gz'}, dimensions={0} | all-to-all | bytes 131072 | tf_op jit(solution)/shard_map/all_to_all | solution.py:410
  122.1 1.0 shard_map.56
  (4 shorter events, 0.1 us)
Async XLA Ops:
  0.6 1.0 copy-start
  1.7 1.0 copy-start.1
  2.7 1.0 copy-start.2
  4.4 29.4 %collective-permute-start = (f32[34,32,128]{2,1,0:T(8,128)S(1)}, f32[34,32,128]{2,1,0:T(8,128)S(1)}, u32[]{:S(2)}, u32[]{:S(2)}) collective-permute-start(f32[34,32,128]{2,1,0:T(8,128)S(1)} %get-tuple-element.29), channel_id=1, source_target_pairs={{0,8},{8,16},{16,24},{24,32},{32,40},{40,48},{48,56},{56,64},{64,7... | collective-permute-start | bytes 1671176 | tf_op jit(solution)/shard_map/ppermute | solution.py:402
  9.0 24.8 %collective-permute-start.1 = (f32[34,32,128]{2,1,0:T(8,128)S(1)}, f32[34,32,128]{2,1,0:T(8,128)S(1)}, u32[]{:S(2)}, u32[]{:S(2)}) collective-permute-start(f32[34,32,128]{2,1,0:T(8,128)S(1)} %get-tuple-element.30), channel_id=1, source_target_pairs={{8,0},{16,8},{24,16},{32,24},{40,32},{48,40},{56,48},{64,56},{72,6... | collective-permute-start | bytes 1671176 | tf_op jit(solution)/shard_map/ppermute | solution.py:403
  10.9 9.5 %collective-permute-start.5 = (f32[2,32,128]{2,1,0:T(8,128)S(1)}, f32[2,32,128]{2,1,0:T(8,128)S(1)}, u32[]{:S(2)}, u32[]{:S(2)}) collective-permute-start(f32[2,32,128]{2,1,0:T(8,128)S(1)} %get-tuple-element.34), channel_id=1, source_target_pairs={{0,9},{1,8},{8,17},{9,16},{16,25},{17,24},{24,33},{25,32},{32,41},... | collective-permute-start | bytes 98312 | tf_op jit(solution)/shard_map/ppermute | solution.py:398
  16.0 25.3 %collective-permute-start.2 = (f32[544,128]{1,0:T(8,128)S(1)}, f32[544,128]{1,0:T(8,128)S(1)}, u32[]{:S(2)}, u32[]{:S(2)}) collective-permute-start(f32[544,128]{1,0:T(8,128)S(1)} %get-tuple-element.31), channel_id=1, source_target_pairs={{0,2},{2,4},{4,6},{1,3},{3,5},{5,7},{8,10},{10,12},{12,14},{9,11},... | collective-permute-start | bytes 835592 | tf_op jit(solution)/shard_map/ppermute | solution.py:400
  19.2 22.2 %collective-permute-start.3 = (f32[544,128]{1,0:T(8,128)S(1)}, f32[544,128]{1,0:T(8,128)S(1)}, u32[]{:S(2)}, u32[]{:S(2)}) collective-permute-start(f32[544,128]{1,0:T(8,128)S(1)} %get-tuple-element.32), channel_id=1, source_target_pairs={{2,0},{4,2},{6,4},{3,1},{5,3},{7,5},{10,8},{12,10},{14,12},{11,9},... | collective-permute-start | bytes 835592 | tf_op jit(solution)/shard_map/ppermute | solution.py:401
  20.5 8.3 %collective-permute-start.6 = (f32[2,32,128]{2,1,0:T(8,128)S(1)}, f32[2,32,128]{2,1,0:T(8,128)S(1)}, u32[]{:S(2)}, u32[]{:S(2)}) collective-permute-start(f32[2,32,128]{2,1,0:T(8,128)S(1)} %get-tuple-element.35), channel_id=1, source_target_pairs={{8,1},{9,0},{16,9},{17,8},{24,17},{25,16},{32,25},{33,24},{40,33},... | collective-permute-start | bytes 98312 | tf_op jit(solution)/shard_map/ppermute | solution.py:399
  28.8 5.0 %collective-permute-start.4 = (f32[3,2,32,128]{3,2,1,0:T(8,128)S(1)}, f32[3,2,32,128]{3,2,1,0:T(8,128)S(1)}, u32[]{:S(2)}, u32[]{:S(2)}) collective-permute-start(f32[3,2,32,128]{3,2,1,0:T(8,128)S(1)} %get-tuple-element.33), channel_id=1, source_target_pairs={{0,1},{1,0},{2,3},{3,2},{4,5},{5,4},{6,7},{7,6},{8,9},{9,8},{10,11... | collective-permute-start | bytes 294920 | tf_op jit(solution)/shard_map/ppermute | solution.py:397
  33.9 7.5 %collective-permute-start.7 = (f32[224,128]{1,0:T(8,128)S(1)}, f32[224,128]{1,0:T(8,128)S(1)}, u32[]{:S(2)}, u32[]{:S(2)}) collective-permute-start(f32[224,128]{1,0:T(8,128)S(1)} %get-tuple-element.36), channel_id=1, source_target_pairs={{0,2},{2,4},{4,6},{1,3},{3,5},{5,7},{8,10},{10,12},{12,14},{9,11},... | collective-permute-start | bytes 344072 | tf_op jit(solution)/shard_map/ppermute | solution.py:407
  38.2 5.5 %collective-permute-start.8 = (f32[224,128]{1,0:T(8,128)S(1)}, f32[224,128]{1,0:T(8,128)S(1)}, u32[]{:S(2)}, u32[]{:S(2)}) collective-permute-start(f32[224,128]{1,0:T(8,128)S(1)} %get-tuple-element.37), channel_id=1, source_target_pairs={{2,0},{4,2},{6,4},{3,1},{5,3},{7,5},{10,8},{12,10},{14,12},{11,9},... | collective-permute-start | bytes 344072 | tf_op jit(solution)/shard_map/ppermute | solution.py:407
  39.5 1.0 copy-start.3

commit v3 on v0

v3 whole, which is shorter than its diff:
```python
import jax
import jax.numpy as jnp
from jax import lax
from jax.experimental import pallas as pl
from jax.experimental.pallas import tpu as pltpu
from jax.sharding import PartitionSpec as P


ALL = ("gx", "gy", "gz")
F32 = jnp.float32
NX, NY, NZ = 16, 32, 128
D, DW = 7, 5
DEPTHS = (D, DW, DW)
X0, Y0 = 7, 8
XE, YE = NX + 2 * D, 56
TOP = Y0 + NY
GRID_X, GRID_Y = 256, 128
COUPLE = 0.05 * -2.0 * 0.0625
SLOT, TILES = 16, 4
XY_ROWS, EDGE_ROWS = 164, 280


def lane_ids(rows):
    return lax.broadcasted_iota(jnp.int32, (rows, NZ), 1)


def row_ids(rows):
    return lax.broadcasted_iota(jnp.int32, (rows, NZ), 0)


def own_lanes(rows, iz):
    return (lane_ids(rows) % SLOT) // 8 == iz


def highs(axis):
    first = 1 - lax.axis_index(axis) % 2
    return first, 1 - first


def face_layers():
    return ((0, D, 0), (1, DW, 2 * D), (2, DW, 2 * (D + DW)))


def xy_pieces():
    row = 0
    for side in range(2):
        for m in range(2):
            for f, depth, at in face_layers():
                for away in range(1, depth):
                    yield row, depth - away, side, m, f, depth, at, away
                    row += depth - away


def seam_pieces():
    row = XY_ROWS
    for tile in range(TILES):
        for m in range(2):
            for f, count in ((0, 6), (1, 4), (2, 4)):
                yield row, count, tile, m, f
                row += count


def pack(c, w, t, *refs):
    fields, seams, (xa, xb, ya, yb, z, za, zb, sems) = refs[:3], refs[3:6], refs[6:]
    iz = lax.axis_index("gz")
    copies = []
    for f, source in enumerate((c, w, t)):
        for m in range(2):
            copy = pltpu.make_async_copy(
                source.at[m],
                fields[f].at[m, pl.ds(X0, NX), pl.ds(Y0, NY)],
                sems.at[2 * f + m],
            )
            copy.start()
            copies.append(copy)
    for copy in copies:
        copy.wait()
    for high, out in zip(highs("gx"), (xa, xb)):
        for f, depth, at in face_layers():
            start = X0 + high * (NX - depth)
            for layer in range(depth):
                for m in range(2):
                    out[at + 2 * layer + m] = fields[f][m, start + layer, Y0:TOP]
    for high, out in zip(highs("gy"), (ya, yb)):
        for m in range(2):
            for x in range(NX):
                row = (m * NX + x) * sum(DEPTHS)
                for f, depth in enumerate(DEPTHS):
                    start = Y0 + high * (NY - depth)
                    out[row : row + depth] = fields[f][m, X0 + x, pl.ds(start, depth)]
                    row += depth
    lane, own = lane_ids(NY), own_lanes(NY, iz)
    swap = 8 + 112 * iz
    for half in range(2):
        for m in range(2):
            packed = []
            for f in range(3):
                acc = jnp.zeros((NY, NZ), F32)
                for s in range(8):
                    block = fields[f][m, X0 + 8 * half + s, Y0:TOP]
                    turned = pltpu.roll(block, (SLOT * s + 8) % NZ, 1)
                    acc = jnp.where(jnp.logical_and(lane // SLOT == s, own), turned, acc)
                seams[f][m, 1 + half, Y0:TOP] = acc
                packed.append(acc)
            z[half, 0, m] = packed[0] + pltpu.roll(packed[1], swap, 1)
            z[half, 1, m] = packed[2]
    for high, out in zip(highs("gx"), (za, zb)):
        for pair in range(2):
            for m in range(2):
                out[pair, m] = z[high, pair, m]


def clear(*refs):
    fields, seams = refs[6:9], refs[9:12]
    blank = jnp.zeros((YE, NZ), F32)
    for field in fields:
        for m in range(2):
            for x in (*range(X0), *range(X0 + NX, XE)):
                field[m, x] = blank
            for x in range(X0, X0 + NX):
                field[m, x, 0:Y0] = blank[0:Y0]
                field[m, x, TOP:YE] = blank[TOP:YE]
    for seam in seams:
        for m in range(2):
            for tile in (0, 3):
                seam[m, tile] = blank
            for tile in (1, 2):
                seam[m, tile, 0:Y0] = blank[0:Y0]
                seam[m, tile, TOP:YE] = blank[TOP:YE]


def build(xa, xb, z, za, zb, *refs):
    seams, (ea, eb) = refs[3:6], refs[6:]
    iz = lax.axis_index("gz")
    lane, own = lane_ids(NY), own_lanes(NY, iz)
    swap = 8 + 112 * iz

    def others(pairs):
        return pairs[0], pltpu.roll(pairs[0], swap, 1), pairs[1]

    for m in range(2):
        for half in range(2):
            for f, other in enumerate(others([z[half, pair, m] for pair in range(2)])):
                here = (m, 1 + half, slice(Y0, TOP))
                seams[f][here] = jnp.where(own, seams[f][here], other)
    for high, face, edge in zip(highs("gx"), (xa, xb), (za, zb)):
        for m in range(2):
            halves = others([edge[pair, m] for pair in range(2)])
            for f, depth, at in face_layers():
                acc = halves[f]
                for layer in range(depth):
                    s = jnp.where(high == 1, layer, 8 - depth + layer)
                    turned = pltpu.roll(face[at + 2 * layer + m], (SLOT * s + 8) % NZ, 1)
                    acc = jnp.where(jnp.logical_and(lane // SLOT == s, own), turned, acc)
                seams[f][m, 3 * high, Y0:TOP] = acc
    high_x = highs("gx")
    for high, out in zip(highs("gy"), (ea, eb)):
        for row, count, side, m, f, depth, at, away in xy_pieces():
            layer = jnp.where(high_x[side] == 1, away - 1, depth - away)
            start = high * (NY - count)
            out[row : row + count] = (xa, xb)[side][at + 2 * layer + m, pl.ds(start, count)]
        for row, count, tile, m, f in seam_pieces():
            start = Y0 + high * (NY - count)
            out[row : row + count] = seams[f][m, tile, pl.ds(start, count)]
        out[276:280] = jnp.zeros((4, NZ), F32)


def place(xa, xb, ya, yb, *refs):
    fields = refs[3:]
    for high, face in zip(highs("gx"), (xa, xb)):
        for f, depth, at in face_layers():
            start = jnp.where(high == 1, X0 + NX, X0 - depth)
            for layer in range(depth):
                for m in range(2):
                    fields[f][m, start + layer, Y0:TOP] = face[at + 2 * layer + m]
    for high, face in zip(highs("gy"), (ya, yb)):
        for m in range(2):
            for x in range(NX):
                row = (m * NX + x) * sum(DEPTHS)
                for f, depth in enumerate(DEPTHS):
                    start = jnp.where(high == 1, TOP, Y0 - depth)
                    fields[f][m, X0 + x, pl.ds(start, depth)] = face[row : row + depth]
                    row += depth


def place_edges(ea, eb, fields, seams):
    high_x = highs("gx")
    for high, edge in zip(highs("gy"), (ea, eb)):
        for row, count, side, m, f, depth, at, away in xy_pieces():
            x = jnp.where(high_x[side] == 1, X0 + NX - 1 + away, X0 - away)
            start = jnp.where(high == 1, TOP, Y0 - count)
            fields[f][m, x, pl.ds(start, count)] = edge[row : row + count]
        for row, count, tile, m, f in seam_pieces():
            start = jnp.where(high == 1, TOP, Y0 - count)
            seams[f][m, tile, pl.ds(start, count)] = edge[row : row + count]


def cross(a, b):
    return (
        a[1] * b[2] - a[2] * b[1],
        a[2] * b[0] - a[0] * b[2],
        a[0] * b[1] - a[1] * b[0],
    )


class Along:
    def __init__(self):
        iz = lax.axis_index("gz")
        self.iz = iz
        lane = lane_ids(8)
        self.first, self.last = lane == 0, lane == NZ - 1
        self.up_on = (1 - iz).astype(F32)
        self.down_on = iz.astype(F32)

    def slot(self, x):
        place = x + 1
        return place // 8, (119 + 2 * self.iz + NZ - SLOT * (place % 8)) % NZ

    def __call__(self, own, seam, shift):
        over = pltpu.roll(seam, shift, 1)
        up = jnp.where(self.last, over * self.up_on, pltpu.roll(own, NZ - 1, 1))
        down = jnp.where(self.first, over * self.down_on, pltpu.roll(own, 1, 1))
        return up, down


def seam_x(ref, lead, tile, rows):
    lane = lane_ids(8)
    own = ref[(*lead, tile, rows)]
    after = ref[(*lead, min(tile + 1, TILES - 1), rows)]
    before = ref[(*lead, max(tile - 1, 0), rows)]
    up = jnp.where(lane < NZ - SLOT, pltpu.roll(own, NZ - SLOT, 1), pltpu.roll(after, NZ - SLOT, 1))
    down = jnp.where(lane >= SLOT, pltpu.roll(own, SLOT, 1), pltpu.roll(before, SLOT, 1))
    return own, up, down


def chunks(rows):
    return -(-rows // 8)


def seam_gradients(C, W, T, G, Fl, depth):
    ix, iy = lax.axis_index("gx"), lax.axis_index("gy")
    lane = lane_ids(8)

    def keep(tile, y):
        place = ix * NX + (8 * tile - 8) + lane // SLOT
        row = row_ids(8) + (iy * NY - Y0) + y
        inside = jnp.logical_and(place >= 0, place < GRID_X)
        inside = jnp.logical_and(inside, jnp.logical_and(row >= 0, row < GRID_Y))
        return inside.astype(F32)

    def flux_at(k, carry):
        y = Y0 - depth - 1 + 8 * k
        here = pl.ds(y, 8)
        for tile in range(TILES):
            slope = []
            for m in range(2):
                own, after, before = seam_x(C, (m,), tile, here)
                slope.append(
                    (
                        after - before,
                        C[m, tile, pl.ds(y + 1, 8)] - C[m, tile, pl.ds(y - 1, 8)],
                        pltpu.roll(own, NZ - 1, 1) - pltpu.roll(own, 1, 1),
                    )
                )
            a, b = slope
            inside = keep(tile, y)
            crossed = tuple(inside * v for v in cross(a, b))
            for n, value in enumerate(cross(b, crossed) + cross(crossed, a)):
                Fl[n, tile, here] = value
        return carry

    lax.fori_loop(0, chunks(NY + 2 * depth + 2), flux_at, 0)

    def gradient_at(k, carry):
        y = Y0 - depth + 8 * k
        here, up, down = pl.ds(y, 8), pl.ds(y + 1, 8), pl.ds(y - 1, 8)
        for tile in range(TILES):
            inside = keep(tile, y)
            for m in range(2):
                n = 3 * m
                own, after, before = seam_x(C, (m,), tile, here)
                near = after + before + C[m, tile, up] + C[m, tile, down]
                near = near + pltpu.roll(own, NZ - 1, 1) + pltpu.roll(own, 1, 1)
                _, after, before = seam_x(Fl, (n,), tile, here)
                along = Fl[n + 2, tile, here]
                spread = after - before + (Fl[n + 1, tile, up] - Fl[n + 1, tile, down])
                spread = spread + (pltpu.roll(along, NZ - 1, 1) - pltpu.roll(along, 1, 1))
                value = W[m, tile, here] * (own - T[m, tile, here])
                value = value + (6.0 * own - near) + COUPLE * spread
                G[m, tile, here] = inside * value
        return carry

    lax.fori_loop(0, chunks(NY + 2 * depth), gradient_at, 0)


def gradients(fields, seams, G, Gs, Fl, Fs, depth):
    C, W, T = fields
    seam_gradients(*seams, Gs, Fs, depth)
    ix, iy = lax.axis_index("gx"), lax.axis_index("gy")
    along = Along()

    def keep(x, y):
        place = ix * NX + (x - X0)
        inside_x = jnp.logical_and(place >= 0, place < GRID_X).astype(F32)
        row = row_ids(8) + (iy * NY + (y - Y0))
        return jnp.where(jnp.logical_and(row >= 0, row < GRID_Y), inside_x, 0.0)

    def flux_at(x, carry):
        tile, shift = along.slot(x)
        for k in range(chunks(NY + 2 * depth + 2)):
            y = Y0 - depth - 1 + 8 * k
            here, up, down = slice(y, y + 8), slice(y + 1, y + 9), slice(y - 1, y + 7)
            slope, around = [], []
            for m in range(2):
                after, before = along(C[m, x, here], seams[0][m, tile, here], shift)
                slope.append(
                    (
                        C[m, x + 1, here] - C[m, x - 1, here],
                        C[m, x, up] - C[m, x, down],
                        after - before,
                    )
                )
                around.append(after + before)
            a, b = slope
            inside = keep(x, y)
            crossed = tuple(inside * v for v in cross(a, b))
            for m, flux in enumerate((cross(b, crossed), cross(crossed, a))):
                after, before = along(flux[2], Fs[3 * m + 2, tile, here], shift)
                Fl[3 * m, x, here] = flux[0]
                Fl[3 * m + 1, x, here] = flux[1]
                Fl[3 * m + 2, x, here] = COUPLE * (after - before) - around[m]
        return carry

    lax.fori_loop(X0 - depth - 1, X0 + NX + depth + 1, flux_at, 0)

    def gradient_at(x, carry):
        for k in range(chunks(NY + 2 * depth)):
            y = Y0 - depth + 8 * k
            here, up, down = slice(y, y + 8), slice(y + 1, y + 9), slice(y - 1, y + 7)
            inside = keep(x, y)
            for m in range(2):
                n = 3 * m
                own = C[m, x, here]
                near = (C[m, x + 1, here] + C[m, x - 1, here]) + (C[m, x, up] + C[m, x, down])
                spread = Fl[n, x + 1, here] - Fl[n, x - 1, here]
                spread = spread + (Fl[n + 1, x, up] - Fl[n + 1, x, down])
                value = W[m, x, here] * (own - T[m, x, here]) + (6.0 * own - near)
                G[m, x, here] = inside * (value + (Fl[n + 2, x, here] + COUPLE * spread))
        return carry

    lax.fori_loop(X0 - depth, X0 + NX + depth, gradient_at, 0)


def totals(W, G, Gs, applied, sums):
    along = Along()

    def body(x, carry):
        norm, curve = carry
        tile, shift = along.slot(x)
        for k in range(NY // 8):
            y = Y0 + 8 * k
            here, up, down = slice(y, y + 8), slice(y + 1, y + 9), slice(y - 1, y + 7)
            for m in range(2):
                own = G[m, x, here]
                after, before = along(own, Gs[m, tile, here], shift)
                near = after + G[m, x + 1, here] + G[m, x, up]
                if applied is None:
                    near = near + near
                else:
                    near = near + before + G[m, x - 1, here] + G[m, x, down]
                value = W[m, x, here] * own + (6.0 * own - near)
                if applied is not None:
                    applied[m, x - X0, 8 * k : 8 * k + 8] = value
                norm = norm + own * own
                curve = curve + own * value
        return norm, curve

    zero = jnp.zeros((8, NZ), F32)
    norm, curve = lax.fori_loop(X0, X0 + NX, body, (zero, zero))
    norm, curve = jnp.sum(norm), jnp.sum(curve)
    lane = lane_ids(8)
    row = jnp.where(lane == 0, norm, jnp.where(lane == 1, curve, 0.0))
    for k in range(sums.shape[0] // 8):
        sums[8 * k : 8 * k + 8] = row


def step_of(gathered):
    column = jnp.sum(gathered[...], axis=0, keepdims=True)
    lane = lane_ids(1)
    norm = jnp.sum(jnp.where(lane == 0, column, 0.0), axis=1, keepdims=True)
    curve = jnp.sum(jnp.where(lane == 1, column, 0.0), axis=1, keepdims=True)
    return jnp.broadcast_to(norm, (8, NZ)) / jnp.broadcast_to(curve, (8, NZ))


def moved(C, Cs, G, Gs, step, New, News, depth):
    rows = [slice(Y0 - depth + 8 * k, Y0 - depth + 8 * k + 8) for k in range(chunks(NY + 2 * depth))]

    def body(x, carry):
        for here in rows:
            for m in range(2):
                New[m, x, here] = C[m, x, here] - step * G[m, x, here]
        return carry

    lax.fori_loop(X0 - depth, X0 + NX + depth, body, 0)
    for tile in range(TILES):
        for here in rows:
            for m in range(2):
                News[m, tile, here] = Cs[m, tile, here] - step * Gs[m, tile, here]


def first_step(ea, eb, *refs):
    fields, seams, (G, Gs, sums, Fl, Fs) = refs[6:9], refs[9:12], refs[12:]
    place_edges(ea, eb, fields, seams)
    gradients(fields, seams, G, Gs, Fl, Fs, 5)
    totals(fields[1], G, Gs, None, sums)


def next_step(C, W, T, Cs, Ws, Ts, G, Gs, gathered, New, News, Gn, Gns, sums, Fl, Fs):
    moved(C, Cs, G, Gs, step_of(gathered), New, News, 5)
    gradients((New, W, T), (News, Ws, Ts), Gn, Gns, Fl, Fs, 3)
    totals(W, Gn, Gns, None, sums)


def last_step(C, W, T, Cs, Ws, Ts, G, Gs, gathered, *refs):
    current, gradient, applied, sums, New, News, Gn, Gns, Fl, Fs = refs
    moved(C, Cs, G, Gs, step_of(gathered), New, News, 3)
    gradients((New, W, T), (News, Ws, Ts), Gn, Gns, Fl, Fs, 1)
    totals(W, Gn, Gns, applied, sums)

    def body(x, carry):
        for m in range(2):
            current[m, x] = New[m, X0 + x, Y0:TOP]
            gradient[m, x] = Gn[m, X0 + x, Y0:TOP]
        return carry

    lax.fori_loop(0, NX, body, 0)


def finish(current, gradient, gathered, updated):
    step = step_of(gathered)

    def body(x, carry):
        for m in range(2):
            for k in range(NY // 8):
                here = (m, x, slice(8 * k, 8 * k + 8))
                updated[here] = current[here] - step * gradient[here]
        return carry

    lax.fori_loop(0, NX, body, 0)


def call(body, outs, scratch=(), mib=2, alias=None, **more):
    return pl.pallas_call(
        body,
        out_shape=tuple(jax.ShapeDtypeStruct(s, F32) for s in outs),
        scratch_shapes=[pltpu.VMEM(s, F32) if isinstance(s, tuple) else s for s in scratch],
        compiler_params=pltpu.CompilerParams(vmem_limit_bytes=mib * 1024 * 1024),
        input_output_aliases=alias or {},
        **more,
    )


def pairs_of(size):
    first = [(i, i ^ 1) for i in range(size)]
    second = [(i, i - 1 if i % 2 == 0 else i + 1) for i in range(1, size - 1)]
    return first, second


def gather(sums):
    return lax.all_to_all(sums, ALL, 0, 0, tiled=True)


def local(models, targets, weights):
    nx, ny = lax.axis_size("gx"), lax.axis_size("gy")
    block = (2, NX, NY, NZ)
    wide, seam = (2, XE, YE, NZ), (2, TILES, YE, NZ)
    flux = ((6, XE, YE, NZ), (6, TILES, YE, NZ))
    rows = (nx * ny * 2, NZ)
    states = (wide,) * 3 + (seam,) * 3
    x_face, y_face = (2 * sum(DEPTHS), NY, NZ), (2 * NX * sum(DEPTHS), NZ)
    z_half, edge = (2, 2, NY, NZ), (EDGE_ROWS, NZ)
    *state, xa, xb, ya, yb, z, za, zb = call(
        pack,
        (*states, x_face, x_face, y_face, y_face, (2, *z_half), z_half, z_half),
        (pltpu.SemaphoreType.DMA((6,)),),
        in_specs=[pl.BlockSpec(memory_space=pltpu.HBM)] * 3,
    )(models, weights, targets)
    first_x, second_x = pairs_of(nx)
    first_y, second_y = pairs_of(ny)

    def across(pairs):
        return [(2 * i + k, 2 * j + 1 - k) for i, j in pairs for k in range(2)]

    xa, xb = lax.ppermute(xa, "gx", first_x), lax.ppermute(xb, "gx", second_x)
    ya, yb = lax.ppermute(ya, "gy", first_y), lax.ppermute(yb, "gy", second_y)
    z = lax.ppermute(z, "gz", [(0, 1), (1, 0)])
    za = lax.ppermute(za, ("gx", "gz"), across(first_x))
    zb = lax.ppermute(zb, ("gx", "gz"), across(second_x))
    state = call(clear, states, alias={i: i for i in range(6)})(*state)
    *seams, ea, eb = call(build, (seam,) * 3 + (edge, edge), alias={5: 0, 6: 1, 7: 2})(
        xa, xb, z, za, zb, *state[3:]
    )
    ea, eb = lax.ppermute(ea, "gy", first_y), lax.ppermute(eb, "gy", second_y)
    fields = call(place, (wide,) * 3, alias={4: 0, 5: 1, 6: 2})(xa, xb, ya, yb, *state[:3])
    *state, G, Gs, sums = call(
        first_step, (*states, wide, seam, rows), flux, 9, {2 + i: i for i in range(6)}
    )(ea, eb, *fields, *seams)
    C, Cs, G, Gs, sums = call(next_step, (wide, seam, wide, seam, rows), flux, 9)(
        *state, G, Gs, gather(sums)
    )
    state = (C, *state[1:3], Cs, *state[4:])
    current, gradient, applied, sums = call(
        last_step, (block, block, block, rows), (wide, seam, wide, seam, *flux), 14
    )(*state, G, Gs, gather(sums))
    (updated,) = call(finish, (block,))(current, gradient, gather(sums))
    return updated, applied


def solution(mesh):
    spec = P(None, "gx", "gy", "gz")

    return jax.shard_map(
        local, mesh=mesh, in_specs=(spec, spec, spec), out_specs=(spec, spec), check_vma=False
    )
```

time: 448 us -> 117 us (0.26)
  the two profiles are of different devices: /device:TPU:16 before, /device:TPU:1 now
where the time goes in v3:
time: 117 us
  blocking collectives  58.5 us (50%)
  Pallas kernels  30.4 us (26%)
  starting transfers between devices  19.9 us (17%)
  waiting for transfers between devices  4.48 us (4%)
  local copies, waits for them, and re-layouts  3.12 us (3%)
    all_to_all x3, blocking collectives, gather(): return lax.all_to_all(sums, ALL, 0, 0, tiled=True)  58.5 us
    pallas_call x1, Pallas kernels, local(): call(first_step, (*states, wide, seam, rows), flux, 9, {2 + i: i for i in...  10.1 us
    pallas_call x1, Pallas kernels, local(): call(last_step, (block, block, block, rows), (wide, seam, wide, seam, *fl...  8.78 us
    pallas_call x1, Pallas kernels, local(): call(next_step, (wide, seam, wide, seam, rows), flux, 9)  8.77 us
    ppermute x1, starting transfers between devices, local(): zb = lax.ppermute(zb, ('gx', 'gz'), across(second_x))  5.69 us
    ppermute x2, starting transfers between devices, local(): xa, xb = (lax.ppermute(xa, 'gx', first_x), lax.ppermute(xb, 'gx', second_x))  4.67 us
    ppermute x2, starting transfers between devices, local(): ea, eb = (lax.ppermute(ea, 'gy', first_y), lax.ppermute(eb, 'gy', second_y))  4.39 us
    unnamed x6, local copies, waits for them, and re-layouts  3.12 us
  transfers between devices with their start and end apart: 9, of which 3 were waited for; matrix products, arithmetic and copies ran while one was open for 0% of the time, Pallas kernels for 1%

profile of v3, /device:TPU:1, one launch (start us, length us, event | category | flops | bytes accessed | tf_op | source)
XLA Modules:
  0.0 117.1 jit_solution(11629960008072400894)
XLA Ops:
  0.6 1.0 copy-done
  1.7 1.0 copy-done.1
  2.7 1.0 copy-done.2
  3.8 0.8 shard_map.50
  4.6 1.5 %collective-permute-start = (f32[34,32,128]{2,1,0:T(8,128)S(1)}, f32[34,32,128]{2,1,0:T(8,128)S(1)}, u32[]{:S(2)}, u32[]{:S(2)}) collective-permute-start(f32[34,32,128]{2,1,0:T(8,128)S(1)} %get-tuple-element.47), channel_id=1, source_target_pairs={{0,8},{8,0},{16,24},{24,16},{32,40},{40,32},{48,56},{56,48},{64,72... | collective-permute-start | bytes 1671176 | tf_op jit(solution)/shard_map/ppermute | solution.py:494
  6.1 3.2 %collective-permute-start.1 = (f32[34,32,128]{2,1,0:T(8,128)S(1)}, f32[34,32,128]{2,1,0:T(8,128)S(1)}, u32[]{:S(2)}, u32[]{:S(2)}) collective-permute-start(f32[34,32,128]{2,1,0:T(8,128)S(1)} %get-tuple-element.48), channel_id=1, source_target_pairs={{8,16},{16,8},{24,32},{32,24},{40,48},{48,40},{56,64},{64,56},{72,... | collective-permute-start | bytes 1671176 | tf_op jit(solution)/shard_map/ppermute | solution.py:494
  9.3 0.5 collective-permute-start.3
  9.8 5.7 %collective-permute-start.4 = (f32[2,2,32,128]{3,2,1,0:T(8,128)S(1)}, f32[2,2,32,128]{3,2,1,0:T(8,128)S(1)}, u32[]{:S(2)}, u32[]{:S(2)}) collective-permute-start(f32[2,2,32,128]{3,2,1,0:T(8,128)S(1)} %get-tuple-element.51), channel_id=1, source_target_pairs={{8,17},{9,16},{16,9},{17,8},{24,33},{25,32},{32,25},{33,24},{40,49... | collective-permute-start | bytes 196616 | tf_op jit(solution)/shard_map/ppermute | solution.py:498
  15.5 1.3 %collective-permute-start.7 = (f32[544,128]{1,0:T(8,128)S(1)}, f32[544,128]{1,0:T(8,128)S(1)}, u32[]{:S(2)}, u32[]{:S(2)}) collective-permute-start(f32[544,128]{1,0:T(8,128)S(1)} %get-tuple-element.63), channel_id=1, source_target_pairs={{0,2},{2,0},{4,6},{6,4},{1,3},{3,1},{5,7},{7,5},{8,10},{10,8},{12,... | collective-permute-start | bytes 835592 | tf_op jit(solution)/shard_map/ppermute | solution.py:495
  16.8 0.4 collective-permute-done.3.za
  17.1 0.7 collective-permute-start.8
  17.8 0.0 collective-permute-done.4.zb
  17.8 2.7 %collective-permute-start.2 = (f32[2,2,2,32,128]{4,3,2,1,0:T(8,128)S(1)}, f32[2,2,2,32,128]{4,3,2,1,0:T(8,128)S(1)}, u32[]{:S(2)}, u32[]{:S(2)}) collective-permute-start(f32[2,2,2,32,128]{4,3,2,1,0:T(8,128)S(1)} %get-tuple-element.49), channel_id=1, source_target_pairs={{0,1},{1,0},{2,3},{3,2},{4,5},{5,4},{6,7},{7,6},{8,9},{9,8},{10,11... | collective-permute-start | bytes 393224 | tf_op jit(solution)/shard_map/ppermute | solution.py:496
  20.5 0.3 shard_map.51
  20.8 2.4 %collective-permute-done.2.z = f32[2,2,2,32,128]{4,3,2,1,0:T(8,128)S(1)} collective-permute-done((f32[2,2,2,32,128]{4,3,2,1,0:T(8,128)S(1)}, f32[2,2,2,32,128]{4,3,2,1,0:T(8,128)S(1)}, u32[]{:S(2)}, u32[]{:S(2)}) %collective-permute-start.2) | collective-permute-done | bytes 131104 | tf_op jit(solution)/shard_map/ppermute | solution.py:496
  23.2 0.0 collective-permute-done.xa
  23.2 0.0 collective-permute-done.1.xb
  23.2 0.4 shard_map.52
  23.7 3.7 %collective-permute-start.5 = (f32[280,128]{1,0:T(8,128)S(1)}, f32[280,128]{1,0:T(8,128)S(1)}, u32[]{:S(2)}, u32[]{:S(2)}) collective-permute-start(f32[280,128]{1,0:T(8,128)S(1)} %get-tuple-element.61), channel_id=1, source_target_pairs={{0,2},{2,0},{4,6},{6,4},{1,3},{3,1},{5,7},{7,5},{8,10},{10,8},{12,... | collective-permute-start | bytes 430088 | tf_op jit(solution)/shard_map/ppermute | solution.py:503
  27.4 0.7 collective-permute-start.6
  28.0 0.0 collective-permute-done.7.ya
  28.1 0.0 collective-permute-done.8.yb
  28.1 0.2 shard_map.53
  28.2 1.6 %collective-permute-done.5.ea = f32[280,128]{1,0:T(8,128)S(1)} collective-permute-done((f32[280,128]{1,0:T(8,128)S(1)}, f32[280,128]{1,0:T(8,128)S(1)}, u32[]{:S(2)}, u32[]{:S(2)}) %collective-permute-start.5) | collective-permute-done | bytes 143392 | tf_op jit(solution)/shard_map/ppermute | solution.py:503
  29.9 0.0 collective-permute-done.6.eb
  29.9 10.1 %shard_map.54 = (f32[2,30,56,128]{3,2,1,0:T(8,128)S(1)}, f32[2,30,56,128]{3,2,1,0:T(8,128)S(1)}, f32[2,30,56,128]{3,2,1,0:T(8,128)S(1)}, f32[2,4,56,128]{3,2,1,0...) custom-call(f32[280,128]{1,0:T(8,128)S(1)} %collective-permute-done., ...), custom_call_target="tpu_custom_call", output_to_operand_aliasing={{0}: (2, {}), {1}: (3, {}), {2}: (4, {}), {3}: (5, {}), {4}... | custom-call | tf_op jit(solution)/shard_map/pallas_call | solution.py:505
  40.0 30.7 %all_to_all.33 = f32[128,1,128]{2,1,0:T(1,128)S(1)} all-to-all(f32[128,1,128]{2,1,0:T(1,128)S(1)} %bitcast.15), channel_id=1, replica_groups=mesh['gx'=16,'gy'=4,'gz'=2] {'gx','gy','gz'}, dimensions={0} | all-to-all | bytes 131072 | tf_op jit(solution)/shard_map/all_to_all | solution.py:470
  70.8 8.8 %shard_map.55 = (f32[2,30,56,128]{3,2,1,0:T(8,128)S(1)}, f32[2,4,56,128]{3,2,1,0:T(8,128)S(1)}, f32[2,30,56,128]{3,2,1,0:T(8,128)S(1)}, f32[2,4,56,128]{3,2,1,0:T(8,128)S(1)}, f32[128,128]{1,0:T(8,128)S(1)}) custom-call(f32[2,30,56,128]{3,2,1,0:T(8,128)S(1)} %get-tuple-element.74.C, f32[2,30,56,128]{3,2,1,0:T(8,128)S(1)} %get-tuple-element.75.W, ...), custom_call_target="tpu_custom_call" | custom-call | tf_op jit(solution)/shard_map/pallas_call | solution.py:508
  79.5 13.9 %all_to_all.34 = f32[128,1,128]{2,1,0:T(1,128)S(1)} all-to-all(f32[128,1,128]{2,1,0:T(1,128)S(1)} %bitcast.17), channel_id=1, replica_groups=mesh['gx'=16,'gy'=4,'gz'=2] {'gx','gy','gz'}, dimensions={0} | all-to-all | bytes 131072 | tf_op jit(solution)/shard_map/all_to_all | solution.py:470
  93.4 8.8 %shard_map.56 = (f32[2,16,32,128]{3,2,1,0:T(8,128)S(1)}, f32[2,16,32,128]{3,2,1,0:T(8,128)S(1)}, f32[2,16,32,128]{3,2,1,0:T(8,128)}, f32[128,128]{1,0:T(8,128)S(1)}) custom-call(f32[2,30,56,128]{3,2,1,0:T(8,128)S(1)} %get-tuple-element.83.C, f32[2,30,56,128]{3,2,1,0:T(8,128)S(1)} %get-tuple-element.75.W, f32[2,30,56,128]{3,2,1,0:T(8,128)S(1)} %get-tuple-element.76.T, ...), custom_call_target="tpu_custom_call" | custom-call | tf_op jit(solution)/shard_map/pallas_call | solution.py:512
  102.2 13.9 %all_to_all.35 = f32[128,1,128]{2,1,0:T(1,128)S(1)} all-to-all(f32[128,1,128]{2,1,0:T(1,128)S(1)} %bitcast.16), channel_id=1, replica_groups=mesh['gx'=16,'gy'=4,'gz'=2] {'gx','gy','gz'}, dimensions={0} | all-to-all | bytes 131072 | tf_op jit(solution)/shard_map/all_to_all | solution.py:470
  116.1 1.0 shard_map.57
  (3 shorter events, 0.0 us)
Async XLA Ops:
  0.6 1.0 copy-start
  1.7 1.0 copy-start.1
  2.7 1.0 copy-start.2
  4.6 18.6 %collective-permute-start = (f32[34,32,128]{2,1,0:T(8,128)S(1)}, f32[34,32,128]{2,1,0:T(8,128)S(1)}, u32[]{:S(2)}, u32[]{:S(2)}) collective-permute-start(f32[34,32,128]{2,1,0:T(8,128)S(1)} %get-tuple-element.47), channel_id=1, source_target_pairs={{0,8},{8,0},{16,24},{24,16},{32,40},{40,32},{48,56},{56,48},{64,72... | collective-permute-start | bytes 1671176 | tf_op jit(solution)/shard_map/ppermute | solution.py:494
  6.1 17.2 %collective-permute-start.1 = (f32[34,32,128]{2,1,0:T(8,128)S(1)}, f32[34,32,128]{2,1,0:T(8,128)S(1)}, u32[]{:S(2)}, u32[]{:S(2)}) collective-permute-start(f32[34,32,128]{2,1,0:T(8,128)S(1)} %get-tuple-element.48), channel_id=1, source_target_pairs={{8,16},{16,8},{24,32},{32,24},{40,48},{48,40},{56,64},{64,56},{72,... | collective-permute-start | bytes 1671176 | tf_op jit(solution)/shard_map/ppermute | solution.py:494
  9.3 7.9 %collective-permute-start.3 = (f32[2,2,32,128]{3,2,1,0:T(8,128)S(1)}, f32[2,2,32,128]{3,2,1,0:T(8,128)S(1)}, u32[]{:S(2)}, u32[]{:S(2)}) collective-permute-start(f32[2,2,32,128]{3,2,1,0:T(8,128)S(1)} %get-tuple-element.50), channel_id=1, source_target_pairs={{0,9},{1,8},{8,1},{9,0},{16,25},{17,24},{24,17},{25,16},{32,41},{3... | collective-permute-start | bytes 196616 | tf_op jit(solution)/shard_map/ppermute | solution.py:497
  9.8 8.1 %collective-permute-start.4 = (f32[2,2,32,128]{3,2,1,0:T(8,128)S(1)}, f32[2,2,32,128]{3,2,1,0:T(8,128)S(1)}, u32[]{:S(2)}, u32[]{:S(2)}) collective-permute-start(f32[2,2,32,128]{3,2,1,0:T(8,128)S(1)} %get-tuple-element.51), channel_id=1, source_target_pairs={{8,17},{9,16},{16,9},{17,8},{24,33},{25,32},{32,25},{33,24},{40,49... | collective-permute-start | bytes 196616 | tf_op jit(solution)/shard_map/ppermute | solution.py:498
  15.5 12.6 %collective-permute-start.7 = (f32[544,128]{1,0:T(8,128)S(1)}, f32[544,128]{1,0:T(8,128)S(1)}, u32[]{:S(2)}, u32[]{:S(2)}) collective-permute-start(f32[544,128]{1,0:T(8,128)S(1)} %get-tuple-element.63), channel_id=1, source_target_pairs={{0,2},{2,0},{4,6},{6,4},{1,3},{3,1},{5,7},{7,5},{8,10},{10,8},{12,... | collective-permute-start | bytes 835592 | tf_op jit(solution)/shard_map/ppermute | solution.py:495
  17.1 10.9 %collective-permute-start.8 = (f32[544,128]{1,0:T(8,128)S(1)}, f32[544,128]{1,0:T(8,128)S(1)}, u32[]{:S(2)}, u32[]{:S(2)}) collective-permute-start(f32[544,128]{1,0:T(8,128)S(1)} %get-tuple-element.64), channel_id=1, source_target_pairs={{2,4},{4,2},{3,5},{5,3},{10,12},{12,10},{11,13},{13,11},{18,20},{2... | collective-permute-start | bytes 835592 | tf_op jit(solution)/shard_map/ppermute | solution.py:495
  17.8 5.4 %collective-permute-start.2 = (f32[2,2,2,32,128]{4,3,2,1,0:T(8,128)S(1)}, f32[2,2,2,32,128]{4,3,2,1,0:T(8,128)S(1)}, u32[]{:S(2)}, u32[]{:S(2)}) collective-permute-start(f32[2,2,2,32,128]{4,3,2,1,0:T(8,128)S(1)} %get-tuple-element.49), channel_id=1, source_target_pairs={{0,1},{1,0},{2,3},{3,2},{4,5},{5,4},{6,7},{7,6},{8,9},{9,8},{10,11... | collective-permute-start | bytes 393224 | tf_op jit(solution)/shard_map/ppermute | solution.py:496
  23.7 6.2 %collective-permute-start.5 = (f32[280,128]{1,0:T(8,128)S(1)}, f32[280,128]{1,0:T(8,128)S(1)}, u32[]{:S(2)}, u32[]{:S(2)}) collective-permute-start(f32[280,128]{1,0:T(8,128)S(1)} %get-tuple-element.61), channel_id=1, source_target_pairs={{0,2},{2,0},{4,6},{6,4},{1,3},{3,1},{5,7},{7,5},{8,10},{10,8},{12,... | collective-permute-start | bytes 430088 | tf_op jit(solution)/shard_map/ppermute | solution.py:503
  27.4 2.5 %collective-permute-start.6 = (f32[280,128]{1,0:T(8,128)S(1)}, f32[280,128]{1,0:T(8,128)S(1)}, u32[]{:S(2)}, u32[]{:S(2)}) collective-permute-start(f32[280,128]{1,0:T(8,128)S(1)} %get-tuple-element.62), channel_id=1, source_target_pairs={{2,4},{4,2},{3,5},{5,3},{10,12},{12,10},{11,13},{13,11},{18,20},{2... | collective-permute-start | bytes 430088 | tf_op jit(solution)/shard_map/ppermute | solution.py:503

commit v4 on v3

--- a/solution.py
+++ b/solution.py
@@ -9,15 +9,18 @@
 ALL = ("gx", "gy", "gz")
 F32 = jnp.float32
 NX, NY, NZ = 16, 32, 128
-D, DW = 7, 5
-DEPTHS = (D, DW, DW)
-X0, Y0 = 7, 8
-XE, YE = NX + 2 * D, 56
+DEPTHS = (7, 5, 5)
+DX = 3
+X_DEPTHS = (DX, 1, 1)
+X0, Y0 = DX, 8
+XE, YE = NX + 2 * DX, 56
 TOP = Y0 + NY
 GRID_X, GRID_Y = 256, 128
 COUPLE = 0.05 * -2.0 * 0.0625
 SLOT, TILES = 16, 4
-XY_ROWS, EDGE_ROWS = 164, 280
+XY_ROWS, EDGE_ROWS = 44, 128
+SIDE = slice(Y0 - 4, Y0 + NY + 4)
+SIDE_ROWS = NY + 8
 
 
 def lane_ids(rows):
@@ -38,24 +41,23 @@
 
 
 def face_layers():
-    return ((0, D, 0), (1, DW, 2 * D), (2, DW, 2 * (D + DW)))
+    return ((0, DX, 0), (1, 1, 2 * DX), (2, 1, 2 * DX + 2))
 
 
 def xy_pieces():
     row = 0
     for side in range(2):
         for m in range(2):
-            for f, depth, at in face_layers():
-                for away in range(1, depth):
-                    yield row, depth - away, side, m, f, depth, at, away
-                    row += depth - away
+            for away in (1, 2):
+                yield row, 7 - away, side, m, away
+                row += 7 - away
 
 
 def seam_pieces():
     row = XY_ROWS
     for tile in range(TILES):
         for m in range(2):
-            for f, count in ((0, 6), (1, 4), (2, 4)):
+            for f, count in ((0, 6), (1, 4), (2, 4)) if tile in (1, 2) else ((0, 6),):
                 yield row, count, tile, m, f
                 row += count
 
@@ -91,7 +93,9 @@
                     row += depth
     lane, own = lane_ids(NY), own_lanes(NY, iz)
     swap = 8 + 112 * iz
+    edges = []
     for half in range(2):
+        models, targets = [], []
         for m in range(2):
             packed = []
             for f in range(3):
@@ -102,12 +106,13 @@
                     acc = jnp.where(jnp.logical_and(lane // SLOT == s, own), turned, acc)
                 seams[f][m, 1 + half, Y0:TOP] = acc
                 packed.append(acc)
-            z[half, 0, m] = packed[0] + pltpu.roll(packed[1], swap, 1)
-            z[half, 1, m] = packed[2]
+            z[half, m] = packed[0] + pltpu.roll(packed[1], swap, 1)
+            models.append(packed[0])
+            targets.append(packed[2])
+        z[half, 2] = targets[0] + pltpu.roll(targets[1], swap, 1)
+        edges.append(models[0] + pltpu.roll(models[1], swap, 1))
     for high, out in zip(highs("gx"), (za, zb)):
-        for pair in range(2):
-            for m in range(2):
-                out[pair, m] = z[high, pair, m]
+        out[...] = jnp.where(high == 1, edges[1], edges[0])
 
 
 def clear(*refs):
@@ -135,19 +140,22 @@
     lane, own = lane_ids(NY), own_lanes(NY, iz)
     swap = 8 + 112 * iz
 
-    def others(pairs):
-        return pairs[0], pltpu.roll(pairs[0], swap, 1), pairs[1]
-
-    for m in range(2):
-        for half in range(2):
-            for f, other in enumerate(others([z[half, pair, m] for pair in range(2)])):
+    def other(tile):
+        return pltpu.roll(tile, swap, 1)
+
+    for half in range(2):
+        tiles = [z[half, n] for n in range(3)]
+        halves = ((tiles[0], tiles[1]), (other(tiles[0]), other(tiles[1])), (tiles[2], other(tiles[2])))
+        for f in range(3):
+            for m in range(2):
                 here = (m, 1 + half, slice(Y0, TOP))
-                seams[f][here] = jnp.where(own, seams[f][here], other)
+                seams[f][here] = jnp.where(own, seams[f][here], halves[f][m])
+    blank = jnp.zeros((NY, NZ), F32)
     for high, face, edge in zip(highs("gx"), (xa, xb), (za, zb)):
-        for m in range(2):
-            halves = others([edge[pair, m] for pair in range(2)])
+        tile = edge[...]
+        for m, beyond in enumerate((tile, other(tile))):
             for f, depth, at in face_layers():
-                acc = halves[f]
+                acc = beyond if f == 0 else blank
                 for layer in range(depth):
                     s = jnp.where(high == 1, layer, 8 - depth + layer)
                     turned = pltpu.roll(face[at + 2 * layer + m], (SLOT * s + 8) % NZ, 1)
@@ -155,14 +163,14 @@
                 seams[f][m, 3 * high, Y0:TOP] = acc
     high_x = highs("gx")
     for high, out in zip(highs("gy"), (ea, eb)):
-        for row, count, side, m, f, depth, at, away in xy_pieces():
-            layer = jnp.where(high_x[side] == 1, away - 1, depth - away)
+        for row, count, side, m, away in xy_pieces():
+            layer = jnp.where(high_x[side] == 1, away - 1, DX - away)
             start = high * (NY - count)
-            out[row : row + count] = (xa, xb)[side][at + 2 * layer + m, pl.ds(start, count)]
+            out[row : row + count] = (xa, xb)[side][2 * layer + m, pl.ds(start, count)]
         for row, count, tile, m, f in seam_pieces():
             start = Y0 + high * (NY - count)
             out[row : row + count] = seams[f][m, tile, pl.ds(start, count)]
-        out[276:280] = jnp.zeros((4, NZ), F32)
+        out[124:128] = jnp.zeros((4, NZ), F32)
 
 
 def place(xa, xb, ya, yb, *refs):
@@ -186,10 +194,10 @@
 def place_edges(ea, eb, fields, seams):
     high_x = highs("gx")
     for high, edge in zip(highs("gy"), (ea, eb)):
-        for row, count, side, m, f, depth, at, away in xy_pieces():
+        for row, count, side, m, away in xy_pieces():
             x = jnp.where(high_x[side] == 1, X0 + NX - 1 + away, X0 - away)
             start = jnp.where(high == 1, TOP, Y0 - count)
-            fields[f][m, x, pl.ds(start, count)] = edge[row : row + count]
+            fields[0][m, x, pl.ds(start, count)] = edge[row : row + count]
         for row, count, tile, m, f in seam_pieces():
             start = jnp.where(high == 1, TOP, Y0 - count)
             seams[f][m, tile, pl.ds(start, count)] = edge[row : row + count]
@@ -213,7 +221,7 @@
         self.down_on = iz.astype(F32)
 
     def slot(self, x):
-        place = x + 1
+        place = x - X0 + 8
         return place // 8, (119 + 2 * self.iz + NZ - SLOT * (place % 8)) % NZ
 
     def __call__(self, own, seam, shift):
@@ -331,7 +339,7 @@
                 Fl[3 * m + 2, x, here] = COUPLE * (after - before) - around[m]
         return carry
 
-    lax.fori_loop(X0 - depth - 1, X0 + NX + depth + 1, flux_at, 0)
+    lax.fori_loop(X0 - 2, X0 + NX + 2, flux_at, 0, unroll=2)
 
     def gradient_at(x, carry):
         for k in range(chunks(NY + 2 * depth)):
@@ -348,7 +356,7 @@
                 G[m, x, here] = inside * (value + (Fl[n + 2, x, here] + COUPLE * spread))
         return carry
 
-    lax.fori_loop(X0 - depth, X0 + NX + depth, gradient_at, 0)
+    lax.fori_loop(X0 - 1, X0 + NX + 1, gradient_at, 0, unroll=2)
 
 
 def totals(W, G, Gs, applied, sums):
@@ -392,7 +400,15 @@
     return jnp.broadcast_to(norm, (8, NZ)) / jnp.broadcast_to(curve, (8, NZ))
 
 
-def moved(C, Cs, G, Gs, step, New, News, depth):
+def sides(G, Gs, ga, gb):
+    for high, out in zip(highs("gx"), (ga, gb)):
+        for m in range(2):
+            for layer in range(DX):
+                out[2 * layer + m] = G[m, X0 + high * (NX - DX) + layer, SIDE]
+            out[2 * DX + m] = Gs[m, 1 + high, SIDE]
+
+
+def moved(C, Cs, G, Gs, ga, gb, step, New, News, depth):
     rows = [slice(Y0 - depth + 8 * k, Y0 - depth + 8 * k + 8) for k in range(chunks(NY + 2 * depth))]
 
     def body(x, carry):
@@ -401,29 +417,40 @@
                 New[m, x, here] = C[m, x, here] - step * G[m, x, here]
         return carry
 
-    lax.fori_loop(X0 - depth, X0 + NX + depth, body, 0)
-    for tile in range(TILES):
+    lax.fori_loop(X0, X0 + NX, body, 0)
+    for tile in (1, 2):
         for here in rows:
             for m in range(2):
                 News[m, tile, here] = Cs[m, tile, here] - step * Gs[m, tile, here]
+    for high, side in zip(highs("gx"), (ga, gb)):
+        for m in range(2):
+            for k in range(SIDE_ROWS // 8):
+                here, row = slice(SIDE.start + 8 * k, SIDE.start + 8 * k + 8), slice(8 * k, 8 * k + 8)
+                for layer in range(DX):
+                    x = high * (X0 + NX) + layer
+                    New[m, x, here] = C[m, x, here] - step * side[2 * layer + m, row]
+                News[m, 3 * high, here] = Cs[m, 3 * high, here] - step * side[2 * DX + m, row]
 
 
 def first_step(ea, eb, *refs):
-    fields, seams, (G, Gs, sums, Fl, Fs) = refs[6:9], refs[9:12], refs[12:]
+    fields, seams, (G, Gs, ga, gb, sums, Fl, Fs) = refs[6:9], refs[9:12], refs[12:]
     place_edges(ea, eb, fields, seams)
     gradients(fields, seams, G, Gs, Fl, Fs, 5)
+    sides(G, Gs, ga, gb)
     totals(fields[1], G, Gs, None, sums)
 
 
-def next_step(C, W, T, Cs, Ws, Ts, G, Gs, gathered, New, News, Gn, Gns, sums, Fl, Fs):
-    moved(C, Cs, G, Gs, step_of(gathered), New, News, 5)
+def next_step(C, W, T, Cs, Ws, Ts, G, Gs, ga, gb, gathered, *refs):
+    New, News, Gn, Gns, sa, sb, sums, Fl, Fs = refs
+    moved(C, Cs, G, Gs, ga, gb, step_of(gathered), New, News, 5)
     gradients((New, W, T), (News, Ws, Ts), Gn, Gns, Fl, Fs, 3)
+    sides(Gn, Gns, sa, sb)
     totals(W, Gn, Gns, None, sums)
 
 
-def last_step(C, W, T, Cs, Ws, Ts, G, Gs, gathered, *refs):
+def last_step(C, W, T, Cs, Ws, Ts, G, Gs, ga, gb, gathered, *refs):
     current, gradient, applied, sums, New, News, Gn, Gns, Fl, Fs = refs
-    moved(C, Cs, G, Gs, step_of(gathered), New, News, 3)
+    moved(C, Cs, G, Gs, ga, gb, step_of(gathered), New, News, 3)
     gradients((New, W, T), (News, Ws, Ts), Gn, Gns, Fl, Fs, 1)
     totals(W, Gn, Gns, applied, sums)
 
@@ -477,11 +504,12 @@
     flux = ((6, XE, YE, NZ), (6, TILES, YE, NZ))
     rows = (nx * ny * 2, NZ)
     states = (wide,) * 3 + (seam,) * 3
-    x_face, y_face = (2 * sum(DEPTHS), NY, NZ), (2 * NX * sum(DEPTHS), NZ)
-    z_half, edge = (2, 2, NY, NZ), (EDGE_ROWS, NZ)
+    x_face, y_face = (2 * sum(X_DEPTHS), NY, NZ), (2 * NX * sum(DEPTHS), NZ)
+    z_face, z_edge, edge = (2, 3, NY, NZ), (NY, NZ), (EDGE_ROWS, NZ)
+    side = (2 * DX + 2, SIDE_ROWS, NZ)
     *state, xa, xb, ya, yb, z, za, zb = call(
         pack,
-        (*states, x_face, x_face, y_face, y_face, (2, *z_half), z_half, z_half),
+        (*states, x_face, x_face, y_face, y_face, z_face, z_edge, z_edge),
         (pltpu.SemaphoreType.DMA((6,)),),
         in_specs=[pl.BlockSpec(memory_space=pltpu.HBM)] * 3,
     )(models, weights, targets)
@@ -502,16 +530,22 @@
     )
     ea, eb = lax.ppermute(ea, "gy", first_y), lax.ppermute(eb, "gy", second_y)
     fields = call(place, (wide,) * 3, alias={4: 0, 5: 1, 6: 2})(xa, xb, ya, yb, *state[:3])
-    *state, G, Gs, sums = call(
-        first_step, (*states, wide, seam, rows), flux, 9, {2 + i: i for i in range(6)}
+
+    def refresh(ga, gb, sums):
+        ga = lax.ppermute(ga, "gx", first_x)
+        gb = lax.ppermute(gb, "gx", second_x)
+        return ga, gb, gather(sums)
+
+    *state, G, Gs, ga, gb, sums = call(
+        first_step, (*states, wide, seam, side, side, rows), flux, 9, {2 + i: i for i in range(6)}
     )(ea, eb, *fields, *seams)
-    C, Cs, G, Gs, sums = call(next_step, (wide, seam, wide, seam, rows), flux, 9)(
-        *state, G, Gs, gather(sums)
+    C, Cs, G, Gs, ga, gb, sums = call(next_step, (wide, seam, wide, seam, side, side, rows), flux, 9)(
+        *state, G, Gs, *refresh(ga, gb, sums)
     )
     state = (C, *state[1:3], Cs, *state[4:])
     current, gradient, applied, sums = call(
         last_step, (block, block, block, rows), (wide, seam, wide, seam, *flux), 14
-    )(*state, G, Gs, gather(sums))
+    )(*state, G, Gs, *refresh(ga, gb, sums))
     (updated,) = call(finish, (block,))(current, gradient, gather(sums))
     return updated, applied
 

time: 117 us -> 115 us (0.983)
  blocking collectives: 58.5 us -> 50.6 us
  Pallas kernels: 30.4 us -> 22.8 us
  waiting for transfers between devices: 4.48 us -> 11.9 us
  starting transfers between devices: 19.9 us -> 25.5 us
    all_to_all x3, blocking collectives: 58.5 us -> 50.6 us  [gather(): return lax.all_to_all(sums, ALL, 0, 0, tiled=True)]
    ppermute x0 -> x4, starting transfers between devices: none -> 7.61 us  [the longest x2 6.93 us: refresh(): gb = lax.ppermute(gb, 'gx', second_x)]
    pallas_call x3, Pallas kernels: 19.7 us -> 14.1 us  [the longest x1 7.02 us: local(): call(first_step, (*states, wide, seam, side, side, rows), flux, 9, {2 + i...]
    ppermute x1, waiting for transfers between devices: 0.39 us -> 4.46 us  [local(): za = lax.ppermute(za, ('gx', 'gz'), across(first_x))]
    ppermute x1, waiting for transfers between devices: 0.01 us -> 2.49 us  [local(): zb = lax.ppermute(zb, ('gx', 'gz'), across(second_x))]
    ppermute x1, starting transfers between devices: 2.7 us -> 0.79 us  [local(): z = lax.ppermute(z, 'gz', [(0, 1), (1, 0)])]
    pallas_call x1, Pallas kernels: 8.78 us -> 7.13 us  [local(): call(last_step, (block, block, block, rows), (wide, seam, wide, seam, *fl...]
    ppermute x1, waiting for transfers between devices: 2.43 us -> 4 us  [local(): z = lax.ppermute(z, 'gz', [(0, 1), (1, 0)])]
  transfers between devices with their start and end apart: 9 -> 13, of which waited for: 3 -> 4; matrix products, arithmetic and copies ran while one was open for 0% -> 0% of each run, Pallas kernels for 1% -> 0%
where the time goes in v4:
time: 115 us
  blocking collectives  50.6 us (44%)
  starting transfers between devices  25.5 us (22%)
  Pallas kernels  22.8 us (20%)
  waiting for transfers between devices  11.9 us (10%)
  local copies, waits for them, and re-layouts  3.12 us (3%)
    all_to_all x3, blocking collectives, gather(): return lax.all_to_all(sums, ALL, 0, 0, tiled=True)  50.6 us
    pallas_call x1, Pallas kernels, local(): call(last_step, (block, block, block, rows), (wide, seam, wide, seam, *fl...  7.13 us
    pallas_call x1, Pallas kernels, local(): call(first_step, (*states, wide, seam, side, side, rows), flux, 9, {2 + i...  7.02 us
    ppermute x2, starting transfers between devices, refresh(): gb = lax.ppermute(gb, 'gx', second_x)  6.93 us
    pallas_call x1, Pallas kernels, local(): call(next_step, (wide, seam, wide, seam, side, side, rows), flux, 9)  6.25 us
    ppermute x1, starting transfers between devices, local(): zb = lax.ppermute(zb, ('gx', 'gz'), across(second_x))  5.39 us
    ppermute x1, waiting for transfers between devices, local(): za = lax.ppermute(za, ('gx', 'gz'), across(first_x))  4.46 us
    ppermute x2, starting transfers between devices, local(): ea, eb = (lax.ppermute(ea, 'gy', first_y), lax.ppermute(eb, 'gy', second_y))  4.37 us
  transfers between devices with their start and end apart: 13, of which 4 were waited for; matrix products, arithmetic and copies ran while one was open for 0% of the time, Pallas kernels for 0%

profile of v4, /device:TPU:1, one launch (start us, length us, event | category | flops | bytes accessed | tf_op | source)
XLA Modules:
  0.0 114.6 jit_solution(9318982655896792511)
XLA Ops:
  0.6 1.0 copy-done
  1.7 1.0 copy-done.1
  2.7 1.0 copy-done.2
  3.8 0.9 shard_map.50
  4.7 2.1 %collective-permute-start.7 = (f32[544,128]{1,0:T(8,128)S(1)}, f32[544,128]{1,0:T(8,128)S(1)}, u32[]{:S(2)}, u32[]{:S(2)}) collective-permute-start(f32[544,128]{1,0:T(8,128)S(1)} %get-tuple-element.67), channel_id=1, source_target_pairs={{0,2},{2,0},{4,6},{6,4},{1,3},{3,1},{5,7},{7,5},{8,10},{10,8},{12,... | collective-permute-start | bytes 835592 | tf_op jit(solution)/shard_map/ppermute | solution.py:523
  6.8 0.7 collective-permute-start.8
  7.4 1.0 collective-permute-start
  8.5 3.1 %collective-permute-start.1 = (f32[10,32,128]{2,1,0:T(8,128)S(1)}, f32[10,32,128]{2,1,0:T(8,128)S(1)}, u32[]{:S(2)}, u32[]{:S(2)}) collective-permute-start(f32[10,32,128]{2,1,0:T(8,128)S(1)} %get-tuple-element.52), channel_id=1, source_target_pairs={{8,16},{16,8},{24,32},{32,24},{40,48},{48,40},{56,64},{64,56},{72,... | collective-permute-start | bytes 491528 | tf_op jit(solution)/shard_map/ppermute | solution.py:522
  11.6 0.5 collective-permute-start.3
  12.0 4.5 %collective-permute-done.3.za = f32[32,128]{1,0:T(8,128)S(1)} collective-permute-done((f32[32,128]{1,0:T(8,128)S(1)}, f32[32,128]{1,0:T(8,128)S(1)}, u32[]{:S(2)}, u32[]{:S(2)}) %collective-permute-start.3) | collective-permute-done | bytes 16416 | tf_op jit(solution)/shard_map/ppermute | solution.py:525
  16.5 5.4 %collective-permute-start.4 = (f32[32,128]{1,0:T(8,128)S(1)}, f32[32,128]{1,0:T(8,128)S(1)}, u32[]{:S(2)}, u32[]{:S(2)}) collective-permute-start(f32[32,128]{1,0:T(8,128)S(1)} %get-tuple-element.55), channel_id=1, source_target_pairs={{8,17},{9,16},{16,9},{17,8},{24,33},{25,32},{32,25},{33,24},{40,49... | collective-permute-start | bytes 49160 | tf_op jit(solution)/shard_map/ppermute | solution.py:526
  21.9 2.5 %collective-permute-done.4.zb = f32[32,128]{1,0:T(8,128)S(1)} collective-permute-done((f32[32,128]{1,0:T(8,128)S(1)}, f32[32,128]{1,0:T(8,128)S(1)}, u32[]{:S(2)}, u32[]{:S(2)}) %collective-permute-start.4) | collective-permute-done | bytes 16416 | tf_op jit(solution)/shard_map/ppermute | solution.py:526
  24.4 0.8 collective-permute-start.2
  25.2 0.2 shard_map.51
  25.4 4.0 %collective-permute-done.2.z = f32[2,3,32,128]{3,2,1,0:T(8,128)S(1)} collective-permute-done((f32[2,3,32,128]{3,2,1,0:T(8,128)S(1)}, f32[2,3,32,128]{3,2,1,0:T(8,128)S(1)}, u32[]{:S(2)}, u32[]{:S(2)}) %collective-permute-start.2) | collective-permute-done | bytes 98336 | tf_op jit(solution)/shard_map/ppermute | solution.py:524
  29.4 0.2 shard_map.52
  29.6 3.7 %collective-permute-start.5 = (f32[128,128]{1,0:T(8,128)S(1)}, f32[128,128]{1,0:T(8,128)S(1)}, u32[]{:S(2)}, u32[]{:S(2)}) collective-permute-start(f32[128,128]{1,0:T(8,128)S(1)} %get-tuple-element.65), channel_id=1, source_target_pairs={{0,2},{2,0},{4,6},{6,4},{1,3},{3,1},{5,7},{7,5},{8,10},{10,8},{12,... | collective-permute-start | bytes 196616 | tf_op jit(solution)/shard_map/ppermute | solution.py:531
  33.3 0.7 collective-permute-start.6
  34.0 0.0 collective-permute-done.7.ya
  34.0 0.1 shard_map.53
  34.1 0.9 collective-permute-done.5.ea
  35.0 7.0 %shard_map.54 = (f32[2,22,56,128]{3,2,1,0:T(8,128)S(1)}, f32[2,22,56,128]{3,2,1,0:T(8,128)S(1)}, f32[2,22,56,128]{3,2,1,0:T(8,128)S(1)}, f32[2,4,56,128]{3,2,1,0...) custom-call(f32[128,128]{1,0:T(8,128)S(1)} %collective-permute-done., ...), custom_call_target="tpu_custom_call", output_to_operand_aliasing={{0}: (2, {}), {1}: (3, {}), {2}: (4, {}), {3}: (5, {}), {4}... | custom-call | tf_op jit(solution)/shard_map/pallas_call | solution.py:539
  42.0 0.1 collective-permute-start.9
  42.1 4.8 %collective-permute-start.10 = (f32[8,40,128]{2,1,0:T(8,128)S(1)}, f32[8,40,128]{2,1,0:T(8,128)S(1)}, u32[]{:S(2)}, u32[]{:S(2)}) collective-permute-start(f32[8,40,128]{2,1,0:T(8,128)S(1)} %get-tuple-element.87), channel_id=1, source_target_pairs={{8,16},{16,8},{24,32},{32,24},{40,48},{48,40},{56,64},{64,56},{72,... | collective-permute-start | bytes 491528 | tf_op jit(solution)/shard_map/ppermute | solution.py:536
  46.9 21.4 %all_to_all.33 = f32[128,1,128]{2,1,0:T(1,128)S(1)} all-to-all(f32[128,1,128]{2,1,0:T(1,128)S(1)} %bitcast.15), channel_id=1, replica_groups=mesh['gx'=16,'gy'=4,'gz'=2] {'gx','gy','gz'}, dimensions={0} | all-to-all | bytes 131072 | tf_op jit(solution)/shard_map/all_to_all | solution.py:497
  68.3 6.2 %shard_map.55 = (f32[2,22,56,128]{3,2,1,0:T(8,128)S(1)}, f32[2,4,56,128]{3,2,1,0:T(8,128)S(1)}, f32[2,22,56,128]{3,2,1,0:T(8,128)S(1)}, f32[2,4,56,128]{3,2,1,0:...) custom-call(f32[2,22,56,128]{3,2,1,0:T(8,128)S(1)} %get-tuple-element.78.C, ...), custom_call_target="tpu_custom_call" | custom-call | tf_op jit(solution)/shard_map/pallas_call | solution.py:542
  74.6 0.6 collective-permute-start.11
  75.2 2.2 %collective-permute-start.12 = (f32[8,40,128]{2,1,0:T(8,128)S(1)}, f32[8,40,128]{2,1,0:T(8,128)S(1)}, u32[]{:S(2)}, u32[]{:S(2)}) collective-permute-start(f32[8,40,128]{2,1,0:T(8,128)S(1)} %get-tuple-element.94), channel_id=1, source_target_pairs={{8,16},{16,8},{24,32},{32,24},{40,48},{48,40},{56,64},{64,56},{72,... | collective-permute-start | bytes 491528 | tf_op jit(solution)/shard_map/ppermute | solution.py:536
  77.3 15.3 %all_to_all.34 = f32[128,1,128]{2,1,0:T(1,128)S(1)} all-to-all(f32[128,1,128]{2,1,0:T(1,128)S(1)} %bitcast.16), channel_id=1, replica_groups=mesh['gx'=16,'gy'=4,'gz'=2] {'gx','gy','gz'}, dimensions={0} | all-to-all | bytes 131072 | tf_op jit(solution)/shard_map/all_to_all | solution.py:497
  92.6 7.1 %shard_map.56 = (f32[2,16,32,128]{3,2,1,0:T(8,128)S(1)}, f32[2,16,32,128]{3,2,1,0:T(8,128)S(1)}, f32[2,16,32,128]{3,2,1,0:T(8,128)}, f32[128,128]{1,0:T(8,128)S(1)}) custom-call(f32[2,22,56,128]{3,2,1,0:T(8,128)S(1)} %get-tuple-element.89.C, f32[2,22,56,128]{3,2,1,0:T(8,128)S(1)} %get-tuple-element.79.W, f32[2,22,56,128]{3,2,1,0:T(8,128)S(1)} %get-tuple-element.80.T, ...), custom_call_target="tpu_custom_call" | custom-call | tf_op jit(solution)/shard_map/pallas_call | solution.py:546
  99.7 13.9 %all_to_all.35 = f32[128,1,128]{2,1,0:T(1,128)S(1)} all-to-all(f32[128,1,128]{2,1,0:T(1,128)S(1)} %bitcast.17), channel_id=1, replica_groups=mesh['gx'=16,'gy'=4,'gz'=2] {'gx','gy','gz'}, dimensions={0} | all-to-all | bytes 131072 | tf_op jit(solution)/shard_map/all_to_all | solution.py:497
  113.6 1.0 shard_map.57
  (11 shorter events, 0.0 us)
Async XLA Ops:
  0.6 1.0 copy-start
  1.7 1.0 copy-start.1
  2.7 1.0 copy-start.2
  4.7 29.3 %collective-permute-start.7 = (f32[544,128]{1,0:T(8,128)S(1)}, f32[544,128]{1,0:T(8,128)S(1)}, u32[]{:S(2)}, u32[]{:S(2)}) collective-permute-start(f32[544,128]{1,0:T(8,128)S(1)} %get-tuple-element.67), channel_id=1, source_target_pairs={{0,2},{2,0},{4,6},{6,4},{1,3},{3,1},{5,7},{7,5},{8,10},{10,8},{12,... | collective-permute-start | bytes 835592 | tf_op jit(solution)/shard_map/ppermute | solution.py:523
  6.8 27.2 %collective-permute-start.8 = (f32[544,128]{1,0:T(8,128)S(1)}, f32[544,128]{1,0:T(8,128)S(1)}, u32[]{:S(2)}, u32[]{:S(2)}) collective-permute-start(f32[544,128]{1,0:T(8,128)S(1)} %get-tuple-element.68), channel_id=1, source_target_pairs={{2,4},{4,2},{3,5},{5,3},{10,12},{12,10},{11,13},{13,11},{18,20},{2... | collective-permute-start | bytes 835592 | tf_op jit(solution)/shard_map/ppermute | solution.py:523
  7.4 21.9 %collective-permute-start = (f32[10,32,128]{2,1,0:T(8,128)S(1)}, f32[10,32,128]{2,1,0:T(8,128)S(1)}, u32[]{:S(2)}, u32[]{:S(2)}) collective-permute-start(f32[10,32,128]{2,1,0:T(8,128)S(1)} %get-tuple-element.51), channel_id=1, source_target_pairs={{0,8},{8,0},{16,24},{24,16},{32,40},{40,32},{48,56},{56,48},{64,72... | collective-permute-start | bytes 491528 | tf_op jit(solution)/shard_map/ppermute | solution.py:522
  8.5 20.9 %collective-permute-start.1 = (f32[10,32,128]{2,1,0:T(8,128)S(1)}, f32[10,32,128]{2,1,0:T(8,128)S(1)}, u32[]{:S(2)}, u32[]{:S(2)}) collective-permute-start(f32[10,32,128]{2,1,0:T(8,128)S(1)} %get-tuple-element.52), channel_id=1, source_target_pairs={{8,16},{16,8},{24,32},{32,24},{40,48},{48,40},{56,64},{64,56},{72,... | collective-permute-start | bytes 491528 | tf_op jit(solution)/shard_map/ppermute | solution.py:522
  11.6 4.9 %collective-permute-start.3 = (f32[32,128]{1,0:T(8,128)S(1)}, f32[32,128]{1,0:T(8,128)S(1)}, u32[]{:S(2)}, u32[]{:S(2)}) collective-permute-start(f32[32,128]{1,0:T(8,128)S(1)} %get-tuple-element.54), channel_id=1, source_target_pairs={{0,9},{1,8},{8,1},{9,0},{16,25},{17,24},{24,17},{25,16},{32,41},{3... | collective-permute-start | bytes 49160 | tf_op jit(solution)/shard_map/ppermute | solution.py:525
  16.5 7.9 %collective-permute-start.4 = (f32[32,128]{1,0:T(8,128)S(1)}, f32[32,128]{1,0:T(8,128)S(1)}, u32[]{:S(2)}, u32[]{:S(2)}) collective-permute-start(f32[32,128]{1,0:T(8,128)S(1)} %get-tuple-element.55), channel_id=1, source_target_pairs={{8,17},{9,16},{16,9},{17,8},{24,33},{25,32},{32,25},{33,24},{40,49... | collective-permute-start | bytes 49160 | tf_op jit(solution)/shard_map/ppermute | solution.py:526
  24.4 5.0 %collective-permute-start.2 = (f32[2,3,32,128]{3,2,1,0:T(8,128)S(1)}, f32[2,3,32,128]{3,2,1,0:T(8,128)S(1)}, u32[]{:S(2)}, u32[]{:S(2)}) collective-permute-start(f32[2,3,32,128]{3,2,1,0:T(8,128)S(1)} %get-tuple-element.53), channel_id=1, source_target_pairs={{0,1},{1,0},{2,3},{3,2},{4,5},{5,4},{6,7},{7,6},{8,9},{9,8},{10,11... | collective-permute-start | bytes 294920 | tf_op jit(solution)/shard_map/ppermute | solution.py:524
  29.6 5.4 %collective-permute-start.5 = (f32[128,128]{1,0:T(8,128)S(1)}, f32[128,128]{1,0:T(8,128)S(1)}, u32[]{:S(2)}, u32[]{:S(2)}) collective-permute-start(f32[128,128]{1,0:T(8,128)S(1)} %get-tuple-element.65), channel_id=1, source_target_pairs={{0,2},{2,0},{4,6},{6,4},{1,3},{3,1},{5,7},{7,5},{8,10},{10,8},{12,... | collective-permute-start | bytes 196616 | tf_op jit(solution)/shard_map/ppermute | solution.py:531
  33.3 1.7 %collective-permute-start.6 = (f32[128,128]{1,0:T(8,128)S(1)}, f32[128,128]{1,0:T(8,128)S(1)}, u32[]{:S(2)}, u32[]{:S(2)}) collective-permute-start(f32[128,128]{1,0:T(8,128)S(1)} %get-tuple-element.66), channel_id=1, source_target_pairs={{2,4},{4,2},{3,5},{5,3},{10,12},{12,10},{11,13},{13,11},{18,20},{2... | collective-permute-start | bytes 196616 | tf_op jit(solution)/shard_map/ppermute | solution.py:531
  42.0 26.3 %collective-permute-start.9 = (f32[8,40,128]{2,1,0:T(8,128)S(1)}, f32[8,40,128]{2,1,0:T(8,128)S(1)}, u32[]{:S(2)}, u32[]{:S(2)}) collective-permute-start(f32[8,40,128]{2,1,0:T(8,128)S(1)} %get-tuple-element.86), channel_id=1, source_target_pairs={{0,8},{8,0},{16,24},{24,16},{32,40},{40,32},{48,56},{56,48},{64,72... | collective-permute-start | bytes 491528 | tf_op jit(solution)/shard_map/ppermute | solution.py:535
  42.1 26.2 %collective-permute-start.10 = (f32[8,40,128]{2,1,0:T(8,128)S(1)}, f32[8,40,128]{2,1,0:T(8,128)S(1)}, u32[]{:S(2)}, u32[]{:S(2)}) collective-permute-start(f32[8,40,128]{2,1,0:T(8,128)S(1)} %get-tuple-element.87), channel_id=1, source_target_pairs={{8,16},{16,8},{24,32},{32,24},{40,48},{48,40},{56,64},{64,56},{72,... | collective-permute-start | bytes 491528 | tf_op jit(solution)/shard_map/ppermute | solution.py:536
  74.6 18.0 %collective-permute-start.11 = (f32[8,40,128]{2,1,0:T(8,128)S(1)}, f32[8,40,128]{2,1,0:T(8,128)S(1)}, u32[]{:S(2)}, u32[]{:S(2)}) collective-permute-start(f32[8,40,128]{2,1,0:T(8,128)S(1)} %get-tuple-element.93), channel_id=1, source_target_pairs={{0,8},{8,0},{16,24},{24,16},{32,40},{40,32},{48,56},{56,48},{64,72... | collective-permute-start | bytes 491528 | tf_op jit(solution)/shard_map/ppermute | solution.py:535
  75.2 17.4 %collective-permute-start.12 = (f32[8,40,128]{2,1,0:T(8,128)S(1)}, f32[8,40,128]{2,1,0:T(8,128)S(1)}, u32[]{:S(2)}, u32[]{:S(2)}) collective-permute-start(f32[8,40,128]{2,1,0:T(8,128)S(1)} %get-tuple-element.94), channel_id=1, source_target_pairs={{8,16},{16,8},{24,32},{32,24},{40,48},{48,40},{56,64},{64,56},{72,... | collective-permute-start | bytes 491528 | tf_op jit(solution)/shard_map/ppermute | solution.py:536

commit v5 on v4

--- a/solution.py
+++ b/solution.py
@@ -19,6 +19,7 @@
 COUPLE = 0.05 * -2.0 * 0.0625
 SLOT, TILES = 16, 4
 XY_ROWS, EDGE_ROWS = 44, 128
+SEAM_AT = 2 * sum(X_DEPTHS)
 SIDE = slice(Y0 - 4, Y0 + NY + 4)
 SIDE_ROWS = NY + 8
 
@@ -63,7 +64,7 @@
 
 
 def pack(c, w, t, *refs):
-    fields, seams, (xa, xb, ya, yb, z, za, zb, sems) = refs[:3], refs[3:6], refs[6:]
+    fields, seams, (ya, yb, z, sems) = refs[:3], refs[3:6], refs[6:]
     iz = lax.axis_index("gz")
     copies = []
     for f, source in enumerate((c, w, t)):
@@ -77,12 +78,6 @@
             copies.append(copy)
     for copy in copies:
         copy.wait()
-    for high, out in zip(highs("gx"), (xa, xb)):
-        for f, depth, at in face_layers():
-            start = X0 + high * (NX - depth)
-            for layer in range(depth):
-                for m in range(2):
-                    out[at + 2 * layer + m] = fields[f][m, start + layer, Y0:TOP]
     for high, out in zip(highs("gy"), (ya, yb)):
         for m in range(2):
             for x in range(NX):
@@ -93,9 +88,8 @@
                     row += depth
     lane, own = lane_ids(NY), own_lanes(NY, iz)
     swap = 8 + 112 * iz
-    edges = []
     for half in range(2):
-        models, targets = [], []
+        targets = []
         for m in range(2):
             packed = []
             for f in range(3):
@@ -107,12 +101,8 @@
                 seams[f][m, 1 + half, Y0:TOP] = acc
                 packed.append(acc)
             z[half, m] = packed[0] + pltpu.roll(packed[1], swap, 1)
-            models.append(packed[0])
             targets.append(packed[2])
         z[half, 2] = targets[0] + pltpu.roll(targets[1], swap, 1)
-        edges.append(models[0] + pltpu.roll(models[1], swap, 1))
-    for high, out in zip(highs("gx"), (za, zb)):
-        out[...] = jnp.where(high == 1, edges[1], edges[0])
 
 
 def clear(*refs):
@@ -134,10 +124,10 @@
                 seam[m, tile, TOP:YE] = blank[TOP:YE]
 
 
-def build(xa, xb, z, za, zb, *refs):
-    seams, (ea, eb) = refs[3:6], refs[6:]
+def merge(z, C, W, T, *refs):
+    fields, seams, outs = (C, W, T), refs[3:6], refs[6:]
     iz = lax.axis_index("gz")
-    lane, own = lane_ids(NY), own_lanes(NY, iz)
+    own = own_lanes(NY, iz)
     swap = 8 + 112 * iz
 
     def other(tile):
@@ -150,17 +140,26 @@
             for m in range(2):
                 here = (m, 1 + half, slice(Y0, TOP))
                 seams[f][here] = jnp.where(own, seams[f][here], halves[f][m])
-    blank = jnp.zeros((NY, NZ), F32)
-    for high, face, edge in zip(highs("gx"), (xa, xb), (za, zb)):
-        tile = edge[...]
-        for m, beyond in enumerate((tile, other(tile))):
+    for high, out in zip(highs("gx"), outs):
+        for m in range(2):
             for f, depth, at in face_layers():
-                acc = beyond if f == 0 else blank
+                start = X0 + high * (NX - depth)
                 for layer in range(depth):
-                    s = jnp.where(high == 1, layer, 8 - depth + layer)
-                    turned = pltpu.roll(face[at + 2 * layer + m], (SLOT * s + 8) % NZ, 1)
-                    acc = jnp.where(jnp.logical_and(lane // SLOT == s, own), turned, acc)
-                seams[f][m, 3 * high, Y0:TOP] = acc
+                    out[at + 2 * layer + m] = fields[f][m, start + layer, Y0:TOP]
+            out[SEAM_AT + m] = seams[0][m, 1 + high, Y0:TOP]
+
+
+def build(xa, xb, *refs):
+    seams, (ea, eb) = refs[3:6], refs[6:]
+    lane, own = lane_ids(NY), own_lanes(NY, lax.axis_index("gz"))
+    for high, face in zip(highs("gx"), (xa, xb)):
+        slot = jnp.where(high == 1, 0, 7)
+        near = jnp.logical_and(lane // SLOT == slot, own)
+        for m in range(2):
+            seams[0][m, 3 * high, Y0:TOP] = face[SEAM_AT + m]
+            for f, depth, at in face_layers()[1:]:
+                turned = pltpu.roll(face[at + m], (SLOT * slot + 8) % NZ, 1)
+                seams[f][m, 3 * high, Y0:TOP] = jnp.where(near, turned, 0.0)
     high_x = highs("gx")
     for high, out in zip(highs("gy"), (ea, eb)):
         for row, count, side, m, away in xy_pieces():
@@ -209,6 +208,11 @@
         a[2] * b[0] - a[0] * b[2],
         a[0] * b[1] - a[1] * b[0],
     )
+
+
+def beside(own, first, last):
+    up = jnp.where(last, 0.0, pltpu.roll(own, NZ - 1, 1))
+    return up, jnp.where(first, 0.0, pltpu.roll(own, 1, 1))
 
 
 class Along:
@@ -304,8 +308,11 @@
 def gradients(fields, seams, G, Gs, Fl, Fs, depth):
     C, W, T = fields
     seam_gradients(*seams, Gs, Fs, depth)
-    ix, iy = lax.axis_index("gx"), lax.axis_index("gy")
-    along = Along()
+    ix, iy, iz = (lax.axis_index(axis) for axis in ALL)
+    lane = lane_ids(8)
+    first, last = lane == 0, lane == NZ - 1
+    cut = lane - (NZ - 2) * (1 - iz)
+    cut = jnp.logical_and(cut >= 0, cut < 2)
 
     def keep(x, y):
         place = ix * NX + (x - X0)
@@ -314,13 +321,12 @@
         return jnp.where(jnp.logical_and(row >= 0, row < GRID_Y), inside_x, 0.0)
 
     def flux_at(x, carry):
-        tile, shift = along.slot(x)
         for k in range(chunks(NY + 2 * depth + 2)):
             y = Y0 - depth - 1 + 8 * k
             here, up, down = slice(y, y + 8), slice(y + 1, y + 9), slice(y - 1, y + 7)
             slope, around = [], []
             for m in range(2):
-                after, before = along(C[m, x, here], seams[0][m, tile, here], shift)
+                after, before = beside(C[m, x, here], first, last)
                 slope.append(
                     (
                         C[m, x + 1, here] - C[m, x - 1, here],
@@ -333,7 +339,7 @@
             inside = keep(x, y)
             crossed = tuple(inside * v for v in cross(a, b))
             for m, flux in enumerate((cross(b, crossed), cross(crossed, a))):
-                after, before = along(flux[2], Fs[3 * m + 2, tile, here], shift)
+                after, before = beside(flux[2], first, last)
                 Fl[3 * m, x, here] = flux[0]
                 Fl[3 * m + 1, x, here] = flux[1]
                 Fl[3 * m + 2, x, here] = COUPLE * (after - before) - around[m]
@@ -342,6 +348,8 @@
     lax.fori_loop(X0 - 2, X0 + NX + 2, flux_at, 0, unroll=2)
 
     def gradient_at(x, carry):
+        place = x - X0 + 8
+        tile, shift = place // 8, (120 + NZ - SLOT * (place % 8)) % NZ
         for k in range(chunks(NY + 2 * depth)):
             y = Y0 - depth + 8 * k
             here, up, down = slice(y, y + 8), slice(y + 1, y + 9), slice(y - 1, y + 7)
@@ -353,7 +361,8 @@
                 spread = Fl[n, x + 1, here] - Fl[n, x - 1, here]
                 spread = spread + (Fl[n + 1, x, up] - Fl[n + 1, x, down])
                 value = W[m, x, here] * (own - T[m, x, here]) + (6.0 * own - near)
-                G[m, x, here] = inside * (value + (Fl[n + 2, x, here] + COUPLE * spread))
+                value = inside * (value + (Fl[n + 2, x, here] + COUPLE * spread))
+                G[m, x, here] = jnp.where(cut, pltpu.roll(Gs[m, tile, here], shift, 1), value)
         return carry
 
     lax.fori_loop(X0 - 1, X0 + NX + 1, gradient_at, 0, unroll=2)
@@ -385,9 +394,9 @@
 
     zero = jnp.zeros((8, NZ), F32)
     norm, curve = lax.fori_loop(X0, X0 + NX, body, (zero, zero))
-    norm, curve = jnp.sum(norm), jnp.sum(curve)
-    lane = lane_ids(8)
-    row = jnp.where(lane == 0, norm, jnp.where(lane == 1, curve, 0.0))
+    norm, curve = (jnp.sum(v, axis=0, keepdims=True) for v in (norm, curve))
+    row = jnp.where(lane_ids(1) < NZ // 2, norm + pltpu.roll(norm, 64, 1), curve + pltpu.roll(curve, 64, 1))
+    row = jnp.broadcast_to(row, (8, NZ))
     for k in range(sums.shape[0] // 8):
         sums[8 * k : 8 * k + 8] = row
 
@@ -395,8 +404,8 @@
 def step_of(gathered):
     column = jnp.sum(gathered[...], axis=0, keepdims=True)
     lane = lane_ids(1)
-    norm = jnp.sum(jnp.where(lane == 0, column, 0.0), axis=1, keepdims=True)
-    curve = jnp.sum(jnp.where(lane == 1, column, 0.0), axis=1, keepdims=True)
+    norm = jnp.sum(jnp.where(lane < NZ // 2, column, 0.0), axis=1, keepdims=True)
+    curve = jnp.sum(jnp.where(lane >= NZ // 2, column, 0.0), axis=1, keepdims=True)
     return jnp.broadcast_to(norm, (8, NZ)) / jnp.broadcast_to(curve, (8, NZ))
 
 
@@ -504,29 +513,24 @@
     flux = ((6, XE, YE, NZ), (6, TILES, YE, NZ))
     rows = (nx * ny * 2, NZ)
     states = (wide,) * 3 + (seam,) * 3
-    x_face, y_face = (2 * sum(X_DEPTHS), NY, NZ), (2 * NX * sum(DEPTHS), NZ)
-    z_face, z_edge, edge = (2, 3, NY, NZ), (NY, NZ), (EDGE_ROWS, NZ)
-    side = (2 * DX + 2, SIDE_ROWS, NZ)
-    *state, xa, xb, ya, yb, z, za, zb = call(
+    x_face, y_face = (SEAM_AT + 2, NY, NZ), (2 * NX * sum(DEPTHS), NZ)
+    edge, side = (EDGE_ROWS, NZ), (2 * DX + 2, SIDE_ROWS, NZ)
+    *state, ya, yb, z = call(
         pack,
-        (*states, x_face, x_face, y_face, y_face, z_face, z_edge, z_edge),
+        (*states, y_face, y_face, (2, 3, NY, NZ)),
         (pltpu.SemaphoreType.DMA((6,)),),
         in_specs=[pl.BlockSpec(memory_space=pltpu.HBM)] * 3,
     )(models, weights, targets)
     first_x, second_x = pairs_of(nx)
     first_y, second_y = pairs_of(ny)
-
-    def across(pairs):
-        return [(2 * i + k, 2 * j + 1 - k) for i, j in pairs for k in range(2)]
-
+    z = lax.ppermute(z, "gz", [(0, 1), (1, 0)])
+    ya = lax.ppermute(ya, "gy", first_y)
+    *seams, xa, xb = call(merge, (seam,) * 3 + (x_face, x_face), alias={4: 0, 5: 1, 6: 2})(z, *state)
     xa, xb = lax.ppermute(xa, "gx", first_x), lax.ppermute(xb, "gx", second_x)
-    ya, yb = lax.ppermute(ya, "gy", first_y), lax.ppermute(yb, "gy", second_y)
-    z = lax.ppermute(z, "gz", [(0, 1), (1, 0)])
-    za = lax.ppermute(za, ("gx", "gz"), across(first_x))
-    zb = lax.ppermute(zb, ("gx", "gz"), across(second_x))
-    state = call(clear, states, alias={i: i for i in range(6)})(*state)
-    *seams, ea, eb = call(build, (seam,) * 3 + (edge, edge), alias={5: 0, 6: 1, 7: 2})(
-        xa, xb, z, za, zb, *state[3:]
+    yb = lax.ppermute(yb, "gy", second_y)
+    state = call(clear, states, alias={i: i for i in range(6)})(*state[:3], *seams)
+    *seams, ea, eb = call(build, (seam,) * 3 + (edge, edge), alias={2: 0, 3: 1, 4: 2})(
+        xa, xb, *state[3:]
     )
     ea, eb = lax.ppermute(ea, "gy", first_y), lax.ppermute(eb, "gy", second_y)
     fields = call(place, (wide,) * 3, alias={4: 0, 5: 1, 6: 2})(xa, xb, ya, yb, *state[:3])

time: 115 us -> 106 us (0.922)
  waiting for transfers between devices: 11.9 us -> 5.87 us
  starting transfers between devices: 25.5 us -> 21.4 us
  blocking collectives: 50.6 us -> 51.9 us
    ppermute x4 -> x2, waiting for transfers between devices: 6.96 us -> 0.01 us  [the longest x1 0.01 us: local(): ya = lax.ppermute(ya, 'gy', first_y)]
    ppermute x4 -> x2, starting transfers between devices: 8.63 us -> 1.88 us  [the longest x1 1.21 us: local(): ya = lax.ppermute(ya, 'gy', first_y)]
    ppermute x2, waiting for transfers between devices: 0.01 us -> 4.86 us  [local(): xa, xb = (lax.ppermute(xa, 'gx', first_x), lax.ppermute(xb, 'gx', second_x))]
    ppermute x1, waiting for transfers between devices: 4 us -> 0.12 us  [local(): z = lax.ppermute(z, 'gz', [(0, 1), (1, 0)])]
    ppermute x1, starting transfers between devices: 0.79 us -> 3.81 us  [local(): z = lax.ppermute(z, 'gz', [(0, 1), (1, 0)])]
    all_to_all x3, blocking collectives: 50.6 us -> 51.9 us  [gather(): return lax.all_to_all(sums, ALL, 0, 0, tiled=True)]
  transfers between devices with their start and end apart: 13 -> 11, of which waited for: 4 -> 3; matrix products, arithmetic and copies ran while one was open for 0% -> 0% of each run, Pallas kernels for 0% -> 0%
where the time goes in v5:
time: 106 us; the launch traced here: 105 us
  blocking collectives  51.9 us (49%)
  Pallas kernels  22.2 us (21%)
  starting transfers between devices  21.4 us (20%)
  waiting for transfers between devices  5.87 us (6%)
  local copies, waits for them, and re-layouts  3.12 us (3%)
    all_to_all x3, blocking collectives, gather(): return lax.all_to_all(sums, ALL, 0, 0, tiled=True)  51.9 us
    pallas_call x1, Pallas kernels, local(): call(last_step, (block, block, block, rows), (wide, seam, wide, seam, *fl...  7.15 us
    pallas_call x1, Pallas kernels, local(): call(first_step, (*states, wide, seam, side, side, rows), flux, 9, {2 + i...  6.42 us
    pallas_call x1, Pallas kernels, local(): call(next_step, (wide, seam, wide, seam, side, side, rows), flux, 9)  6.24 us
    ppermute x2, starting transfers between devices, refresh(): gb = lax.ppermute(gb, 'gx', second_x)  6.22 us
    ppermute x2, starting transfers between devices, local(): xa, xb = (lax.ppermute(xa, 'gx', first_x), lax.ppermute(xb, 'gx', second_x))  5.06 us
    ppermute x2, waiting for transfers between devices, local(): xa, xb = (lax.ppermute(xa, 'gx', first_x), lax.ppermute(xb, 'gx', second_x))  4.86 us
    ppermute x2, starting transfers between devices, local(): ea, eb = (lax.ppermute(ea, 'gy', first_y), lax.ppermute(eb, 'gy', second_y))  3.85 us
  transfers between devices with their start and end apart: 11, of which 3 were waited for; matrix products, arithmetic and copies ran while one was open for 0% of the time, Pallas kernels for 0%

profile of v5, /device:TPU:1, one launch (start us, length us, event | category | flops | bytes accessed | tf_op | source)
XLA Modules:
  0.0 105.2 jit_solution(3434808138064526297)
XLA Ops:
  0.6 1.0 copy-done
  1.7 1.0 copy-done.1
  2.7 1.0 copy-done.2
  3.8 0.9 shard_map.50
  4.6 3.8 %collective-permute-start = (f32[2,3,32,128]{3,2,1,0:T(8,128)S(1)}, f32[2,3,32,128]{3,2,1,0:T(8,128)S(1)}, u32[]{:S(2)}, u32[]{:S(2)}) collective-permute-start(f32[2,3,32,128]{3,2,1,0:T(8,128)S(1)} %get-tuple-element.52), channel_id=1, source_target_pairs={{0,1},{1,0},{2,3},{3,2},{4,5},{5,4},{6,7},{7,6},{8,9},{9,8},{10,11... | collective-permute-start | bytes 294920 | tf_op jit(solution)/shard_map/ppermute | solution.py:526
  8.5 1.2 %collective-permute-start.5 = (f32[544,128]{1,0:T(8,128)S(1)}, f32[544,128]{1,0:T(8,128)S(1)}, u32[]{:S(2)}, u32[]{:S(2)}) collective-permute-start(f32[544,128]{1,0:T(8,128)S(1)} %get-tuple-element.69), channel_id=1, source_target_pairs={{0,2},{2,0},{4,6},{6,4},{1,3},{3,1},{5,7},{7,5},{8,10},{10,8},{12,... | collective-permute-start | bytes 835592 | tf_op jit(solution)/shard_map/ppermute | solution.py:527
  9.7 0.7 collective-permute-start.6
  10.3 0.1 collective-permute-done.z
  10.5 0.1 shard_map.51
  10.6 1.8 %collective-permute-start.1 = (f32[12,32,128]{2,1,0:T(8,128)S(1)}, f32[12,32,128]{2,1,0:T(8,128)S(1)}, u32[]{:S(2)}, u32[]{:S(2)}) collective-permute-start(f32[12,32,128]{2,1,0:T(8,128)S(1)} %get-tuple-element.59), channel_id=1, source_target_pairs={{0,8},{8,0},{16,24},{24,16},{32,40},{40,32},{48,56},{56,48},{64,72... | collective-permute-start | bytes 589832 | tf_op jit(solution)/shard_map/ppermute | solution.py:529
  12.4 3.2 %collective-permute-start.2 = (f32[12,32,128]{2,1,0:T(8,128)S(1)}, f32[12,32,128]{2,1,0:T(8,128)S(1)}, u32[]{:S(2)}, u32[]{:S(2)}) collective-permute-start(f32[12,32,128]{2,1,0:T(8,128)S(1)} %get-tuple-element.60), channel_id=1, source_target_pairs={{8,16},{16,8},{24,32},{32,24},{40,48},{48,40},{56,64},{64,56},{72,... | collective-permute-start | bytes 589832 | tf_op jit(solution)/shard_map/ppermute | solution.py:529
  15.6 0.2 shard_map.52
  15.8 0.0 collective-permute-done.1.xa
  15.8 4.9 %collective-permute-done.2.xb = f32[12,32,128]{2,1,0:T(8,128)S(1)} collective-permute-done((f32[12,32,128]{2,1,0:T(8,128)S(1)}, f32[12,32,128]{2,1,0:T(8,128)S(1)}, u32[]{:S(2)}, u32[]{:S(2)}) %collective-permute-start.2) | collective-permute-done | bytes 196640 | tf_op jit(solution)/shard_map/ppermute | solution.py:529
  20.7 0.1 shard_map.53
  20.8 3.2 %collective-permute-start.3 = (f32[128,128]{1,0:T(8,128)S(1)}, f32[128,128]{1,0:T(8,128)S(1)}, u32[]{:S(2)}, u32[]{:S(2)}) collective-permute-start(f32[128,128]{1,0:T(8,128)S(1)} %get-tuple-element.67), channel_id=1, source_target_pairs={{0,2},{2,0},{4,6},{6,4},{1,3},{3,1},{5,7},{7,5},{8,10},{10,8},{12,... | collective-permute-start | bytes 196616 | tf_op jit(solution)/shard_map/ppermute | solution.py:535
  24.0 0.7 collective-permute-start.4
  24.7 0.0 collective-permute-done.5.ya
  24.7 0.0 collective-permute-done.6.yb
  24.7 0.1 shard_map.54
  24.8 0.9 collective-permute-done.3.ea
  25.7 6.4 %shard_map.55 = (f32[2,22,56,128]{3,2,1,0:T(8,128)S(1)}, f32[2,22,56,128]{3,2,1,0:T(8,128)S(1)}, f32[2,22,56,128]{3,2,1,0:T(8,128)S(1)}, f32[2,4,56,128]{3,2,1,0...) custom-call(f32[128,128]{1,0:T(8,128)S(1)} %collective-permute-done., ...), custom_call_target="tpu_custom_call", output_to_operand_aliasing={{0}: (2, {}), {1}: (3, {}), {2}: (4, {}), {3}: (5, {}), {4}... | custom-call | tf_op jit(solution)/shard_map/pallas_call | solution.py:543
  32.1 0.0 collective-permute-start.7
  32.1 4.1 %collective-permute-start.8 = (f32[8,40,128]{2,1,0:T(8,128)S(1)}, f32[8,40,128]{2,1,0:T(8,128)S(1)}, u32[]{:S(2)}, u32[]{:S(2)}) collective-permute-start(f32[8,40,128]{2,1,0:T(8,128)S(1)} %get-tuple-element.89), channel_id=1, source_target_pairs={{8,16},{16,8},{24,32},{32,24},{40,48},{48,40},{56,64},{64,56},{72,... | collective-permute-start | bytes 491528 | tf_op jit(solution)/shard_map/ppermute | solution.py:540
  36.2 22.8 %all_to_all.33 = f32[128,1,128]{2,1,0:T(1,128)S(1)} all-to-all(f32[128,1,128]{2,1,0:T(1,128)S(1)} %bitcast.15), channel_id=1, replica_groups=mesh['gx'=16,'gy'=4,'gz'=2] {'gx','gy','gz'}, dimensions={0} | all-to-all | bytes 131072 | tf_op jit(solution)/shard_map/all_to_all | solution.py:506
  59.0 6.2 %shard_map.56 = (f32[2,22,56,128]{3,2,1,0:T(8,128)S(1)}, f32[2,4,56,128]{3,2,1,0:T(8,128)S(1)}, f32[2,22,56,128]{3,2,1,0:T(8,128)S(1)}, f32[2,4,56,128]{3,2,1,0:...) custom-call(f32[2,22,56,128]{3,2,1,0:T(8,128)S(1)} %get-tuple-element.80.C, ...), custom_call_target="tpu_custom_call" | custom-call | tf_op jit(solution)/shard_map/pallas_call | solution.py:546
  65.2 0.5 collective-permute-start.9
  65.7 2.2 %collective-permute-start.10 = (f32[8,40,128]{2,1,0:T(8,128)S(1)}, f32[8,40,128]{2,1,0:T(8,128)S(1)}, u32[]{:S(2)}, u32[]{:S(2)}) collective-permute-start(f32[8,40,128]{2,1,0:T(8,128)S(1)} %get-tuple-element.96), channel_id=1, source_target_pairs={{8,16},{16,8},{24,32},{32,24},{40,48},{48,40},{56,64},{64,56},{72,... | collective-permute-start | bytes 491528 | tf_op jit(solution)/shard_map/ppermute | solution.py:540
  67.9 15.3 %all_to_all.34 = f32[128,1,128]{2,1,0:T(1,128)S(1)} all-to-all(f32[128,1,128]{2,1,0:T(1,128)S(1)} %bitcast.16), channel_id=1, replica_groups=mesh['gx'=16,'gy'=4,'gz'=2] {'gx','gy','gz'}, dimensions={0} | all-to-all | bytes 131072 | tf_op jit(solution)/shard_map/all_to_all | solution.py:506
  83.2 7.2 %shard_map.57 = (f32[2,16,32,128]{3,2,1,0:T(8,128)S(1)}, f32[2,16,32,128]{3,2,1,0:T(8,128)S(1)}, f32[2,16,32,128]{3,2,1,0:T(8,128)}, f32[128,128]{1,0:T(8,128)S(1)}) custom-call(f32[2,22,56,128]{3,2,1,0:T(8,128)S(1)} %get-tuple-element.91.C, f32[2,22,56,128]{3,2,1,0:T(8,128)S(1)} %get-tuple-element.81.W, f32[2,22,56,128]{3,2,1,0:T(8,128)S(1)} %get-tuple-element.82.T, ...), custom_call_target="tpu_custom_call" | custom-call | tf_op jit(solution)/shard_map/pallas_call | solution.py:550
  90.3 13.9 %all_to_all.35 = f32[128,1,128]{2,1,0:T(1,128)S(1)} all-to-all(f32[128,1,128]{2,1,0:T(1,128)S(1)} %bitcast.17), channel_id=1, replica_groups=mesh['gx'=16,'gy'=4,'gz'=2] {'gx','gy','gz'}, dimensions={0} | all-to-all | bytes 131072 | tf_op jit(solution)/shard_map/all_to_all | solution.py:506
  104.2 1.0 shard_map.58
  (8 shorter events, 0.0 us)
Async XLA Ops:
  0.6 1.0 copy-start
  1.7 1.0 copy-start.1
  2.7 1.0 copy-start.2
  4.6 5.8 %collective-permute-start = (f32[2,3,32,128]{3,2,1,0:T(8,128)S(1)}, f32[2,3,32,128]{3,2,1,0:T(8,128)S(1)}, u32[]{:S(2)}, u32[]{:S(2)}) collective-permute-start(f32[2,3,32,128]{3,2,1,0:T(8,128)S(1)} %get-tuple-element.52), channel_id=1, source_target_pairs={{0,1},{1,0},{2,3},{3,2},{4,5},{5,4},{6,7},{7,6},{8,9},{9,8},{10,11... | collective-permute-start | bytes 294920 | tf_op jit(solution)/shard_map/ppermute | solution.py:526
  8.5 16.2 %collective-permute-start.5 = (f32[544,128]{1,0:T(8,128)S(1)}, f32[544,128]{1,0:T(8,128)S(1)}, u32[]{:S(2)}, u32[]{:S(2)}) collective-permute-start(f32[544,128]{1,0:T(8,128)S(1)} %get-tuple-element.69), channel_id=1, source_target_pairs={{0,2},{2,0},{4,6},{6,4},{1,3},{3,1},{5,7},{7,5},{8,10},{10,8},{12,... | collective-permute-start | bytes 835592 | tf_op jit(solution)/shard_map/ppermute | solution.py:527
  9.7 15.0 %collective-permute-start.6 = (f32[544,128]{1,0:T(8,128)S(1)}, f32[544,128]{1,0:T(8,128)S(1)}, u32[]{:S(2)}, u32[]{:S(2)}) collective-permute-start(f32[544,128]{1,0:T(8,128)S(1)} %get-tuple-element.70), channel_id=1, source_target_pairs={{2,4},{4,2},{3,5},{5,3},{10,12},{12,10},{11,13},{13,11},{18,20},{2... | collective-permute-start | bytes 835592 | tf_op jit(solution)/shard_map/ppermute | solution.py:530
  10.6 5.3 %collective-permute-start.1 = (f32[12,32,128]{2,1,0:T(8,128)S(1)}, f32[12,32,128]{2,1,0:T(8,128)S(1)}, u32[]{:S(2)}, u32[]{:S(2)}) collective-permute-start(f32[12,32,128]{2,1,0:T(8,128)S(1)} %get-tuple-element.59), channel_id=1, source_target_pairs={{0,8},{8,0},{16,24},{24,16},{32,40},{40,32},{48,56},{56,48},{64,72... | collective-permute-start | bytes 589832 | tf_op jit(solution)/shard_map/ppermute | solution.py:529
  12.4 8.3 %collective-permute-start.2 = (f32[12,32,128]{2,1,0:T(8,128)S(1)}, f32[12,32,128]{2,1,0:T(8,128)S(1)}, u32[]{:S(2)}, u32[]{:S(2)}) collective-permute-start(f32[12,32,128]{2,1,0:T(8,128)S(1)} %get-tuple-element.60), channel_id=1, source_target_pairs={{8,16},{16,8},{24,32},{32,24},{40,48},{48,40},{56,64},{64,56},{72,... | collective-permute-start | bytes 589832 | tf_op jit(solution)/shard_map/ppermute | solution.py:529
  20.8 4.9 %collective-permute-start.3 = (f32[128,128]{1,0:T(8,128)S(1)}, f32[128,128]{1,0:T(8,128)S(1)}, u32[]{:S(2)}, u32[]{:S(2)}) collective-permute-start(f32[128,128]{1,0:T(8,128)S(1)} %get-tuple-element.67), channel_id=1, source_target_pairs={{0,2},{2,0},{4,6},{6,4},{1,3},{3,1},{5,7},{7,5},{8,10},{10,8},{12,... | collective-permute-start | bytes 196616 | tf_op jit(solution)/shard_map/ppermute | solution.py:535
  24.0 1.7 %collective-permute-start.4 = (f32[128,128]{1,0:T(8,128)S(1)}, f32[128,128]{1,0:T(8,128)S(1)}, u32[]{:S(2)}, u32[]{:S(2)}) collective-permute-start(f32[128,128]{1,0:T(8,128)S(1)} %get-tuple-element.68), channel_id=1, source_target_pairs={{2,4},{4,2},{3,5},{5,3},{10,12},{12,10},{11,13},{13,11},{18,20},{2... | collective-permute-start | bytes 196616 | tf_op jit(solution)/shard_map/ppermute | solution.py:535
  32.1 26.9 %collective-permute-start.7 = (f32[8,40,128]{2,1,0:T(8,128)S(1)}, f32[8,40,128]{2,1,0:T(8,128)S(1)}, u32[]{:S(2)}, u32[]{:S(2)}) collective-permute-start(f32[8,40,128]{2,1,0:T(8,128)S(1)} %get-tuple-element.88), channel_id=1, source_target_pairs={{0,8},{8,0},{16,24},{24,16},{32,40},{40,32},{48,56},{56,48},{64,72... | collective-permute-start | bytes 491528 | tf_op jit(solution)/shard_map/ppermute | solution.py:539
  32.1 26.8 %collective-permute-start.8 = (f32[8,40,128]{2,1,0:T(8,128)S(1)}, f32[8,40,128]{2,1,0:T(8,128)S(1)}, u32[]{:S(2)}, u32[]{:S(2)}) collective-permute-start(f32[8,40,128]{2,1,0:T(8,128)S(1)} %get-tuple-element.89), channel_id=1, source_target_pairs={{8,16},{16,8},{24,32},{32,24},{40,48},{48,40},{56,64},{64,56},{72,... | collective-permute-start | bytes 491528 | tf_op jit(solution)/shard_map/ppermute | solution.py:540
  65.2 18.0 %collective-permute-start.9 = (f32[8,40,128]{2,1,0:T(8,128)S(1)}, f32[8,40,128]{2,1,0:T(8,128)S(1)}, u32[]{:S(2)}, u32[]{:S(2)}) collective-permute-start(f32[8,40,128]{2,1,0:T(8,128)S(1)} %get-tuple-element.95), channel_id=1, source_target_pairs={{0,8},{8,0},{16,24},{24,16},{32,40},{40,32},{48,56},{56,48},{64,72... | collective-permute-start | bytes 491528 | tf_op jit(solution)/shard_map/ppermute | solution.py:539
  65.7 17.4 %collective-permute-start.10 = (f32[8,40,128]{2,1,0:T(8,128)S(1)}, f32[8,40,128]{2,1,0:T(8,128)S(1)}, u32[]{:S(2)}, u32[]{:S(2)}) collective-permute-start(f32[8,40,128]{2,1,0:T(8,128)S(1)} %get-tuple-element.96), channel_id=1, source_target_pairs={{8,16},{16,8},{24,32},{32,24},{40,48},{48,40},{56,64},{64,56},{72,... | collective-permute-start | bytes 491528 | tf_op jit(solution)/shard_map/ppermute | solution.py:540

commit v6 on v5

--- a/solution.py
+++ b/solution.py
@@ -22,6 +22,7 @@
 SEAM_AT = 2 * sum(X_DEPTHS)
 SIDE = slice(Y0 - 4, Y0 + NY + 4)
 SIDE_ROWS = NY + 8
+UNROLL, SEAM_UNROLL = 2, 1
 
 
 def lane_ids(rows):
@@ -281,7 +282,7 @@
                 Fl[n, tile, here] = value
         return carry
 
-    lax.fori_loop(0, chunks(NY + 2 * depth + 2), flux_at, 0)
+    lax.fori_loop(0, chunks(NY + 2 * depth + 2), flux_at, 0, unroll=SEAM_UNROLL)
 
     def gradient_at(k, carry):
         y = Y0 - depth + 8 * k
@@ -302,7 +303,7 @@
                 G[m, tile, here] = inside * value
         return carry
 
-    lax.fori_loop(0, chunks(NY + 2 * depth), gradient_at, 0)
+    lax.fori_loop(0, chunks(NY + 2 * depth), gradient_at, 0, unroll=SEAM_UNROLL)
 
 
 def gradients(fields, seams, G, Gs, Fl, Fs, depth):
@@ -345,8 +346,6 @@
                 Fl[3 * m + 2, x, here] = COUPLE * (after - before) - around[m]
         return carry
 
-    lax.fori_loop(X0 - 2, X0 + NX + 2, flux_at, 0, unroll=2)
-
     def gradient_at(x, carry):
         place = x - X0 + 8
         tile, shift = place // 8, (120 + NZ - SLOT * (place % 8)) % NZ
@@ -365,7 +364,25 @@
                 G[m, x, here] = jnp.where(cut, pltpu.roll(Gs[m, tile, here], shift, 1), value)
         return carry
 
-    lax.fori_loop(X0 - 1, X0 + NX + 1, gradient_at, 0, unroll=2)
+    def pair_at(x, fluxes, slopes):
+        if fluxes:
+            flux_at(x, 0)
+            flux_at(x + 1, 0)
+        if slopes:
+            gradient_at(x - 3, 0)
+            gradient_at(x - 2, 0)
+
+    def both_at(i, carry):
+        pair_at(X0 - 2 + 2 * i, True, True)
+        return carry
+
+    def lead_at(i, carry):
+        pair_at(X0 - 2 + 2 * i, True, False)
+        return carry
+
+    lax.fori_loop(0, 2, lead_at, 0)
+    lax.fori_loop(2, NX // 2 + 2, both_at, 0)
+    pair_at(X0 + NX + 2, False, True)
 
 
 def totals(W, G, Gs, applied, sums):
@@ -393,7 +410,7 @@
         return norm, curve
 
     zero = jnp.zeros((8, NZ), F32)
-    norm, curve = lax.fori_loop(X0, X0 + NX, body, (zero, zero))
+    norm, curve = lax.fori_loop(X0, X0 + NX, body, (zero, zero), unroll=UNROLL)
     norm, curve = (jnp.sum(v, axis=0, keepdims=True) for v in (norm, curve))
     row = jnp.where(lane_ids(1) < NZ // 2, norm + pltpu.roll(norm, 64, 1), curve + pltpu.roll(curve, 64, 1))
     row = jnp.broadcast_to(row, (8, NZ))

time: 106 us -> 102 us (0.962)
  Pallas kernels: 22.2 us -> 18.4 us
    pallas_call x1, Pallas kernels: 6.24 us -> 4.95 us  [local(): call(next_step, (wide, seam, wide, seam, side, side, rows), flux, 9)]
    pallas_call x1, Pallas kernels: 6.42 us -> 5.13 us  [local(): call(first_step, (*states, wide, seam, side, side, rows), flux, 9, {2 + i...]
    pallas_call x1, Pallas kernels: 7.15 us -> 5.93 us  [local(): call(last_step, (block, block, block, rows), (wide, seam, wide, seam, *fl...]
where the time goes in v6:
time: 102 us; the launch traced here: 101 us
  blocking collectives  51.9 us (51%)
  starting transfers between devices  21.4 us (21%)
  Pallas kernels  18.4 us (18%)
  waiting for transfers between devices  5.87 us (6%)
  local copies, waits for them, and re-layouts  3.12 us (3%)
    all_to_all x3, blocking collectives, gather(): return lax.all_to_all(sums, ALL, 0, 0, tiled=True)  51.9 us
    ppermute x2, starting transfers between devices, refresh(): gb = lax.ppermute(gb, 'gx', second_x)  6.22 us
    pallas_call x1, Pallas kernels, local(): call(last_step, (block, block, block, rows), (wide, seam, wide, seam, *fl...  5.93 us
    pallas_call x1, Pallas kernels, local(): call(first_step, (*states, wide, seam, side, side, rows), flux, 9, {2 + i...  5.13 us
    ppermute x2, starting transfers between devices, local(): xa, xb = (lax.ppermute(xa, 'gx', first_x), lax.ppermute(xb, 'gx', second_x))  5.06 us
    pallas_call x1, Pallas kernels, local(): call(next_step, (wide, seam, wide, seam, side, side, rows), flux, 9)  4.95 us
    ppermute x2, waiting for transfers between devices, local(): xa, xb = (lax.ppermute(xa, 'gx', first_x), lax.ppermute(xb, 'gx', second_x))  4.86 us
    ppermute x2, starting transfers between devices, local(): ea, eb = (lax.ppermute(ea, 'gy', first_y), lax.ppermute(eb, 'gy', second_y))  3.85 us
  transfers between devices with their start and end apart: 11, of which 3 were waited for; matrix products, arithmetic and copies ran while one was open for 0% of the time, Pallas kernels for 0%

profile of v6, /device:TPU:1, one launch (start us, length us, event | category | flops | bytes accessed | tf_op | source)
XLA Modules:
  0.0 101.4 jit_solution(7238249047006225044)
XLA Ops:
  0.6 1.0 %copy-done = f32[2,16,32,128]{3,2,1,0:T(8,128)S(1)} copy-done((f32[2,16,32,128]{3,2,1,0:T(8,128)S(1)}, f32[2,16,32,128]{3,2,1,0:T(8,128)}, u32[]{:S(2)}) %copy-start) | copy-done | bytes 524312
  1.7 1.0 %copy-done.1 = f32[2,16,32,128]{3,2,1,0:T(8,128)S(1)} copy-done((f32[2,16,32,128]{3,2,1,0:T(8,128)S(1)}, f32[2,16,32,128]{3,2,1,0:T(8,128)}, u32[]{:S(2)}) %copy-start.1) | copy-done | bytes 524312
  2.7 1.0 %copy-done.2 = f32[2,16,32,128]{3,2,1,0:T(8,128)S(1)} copy-done((f32[2,16,32,128]{3,2,1,0:T(8,128)S(1)}, f32[2,16,32,128]{3,2,1,0:T(8,128)}, u32[]{:S(2)}) %copy-start.2) | copy-done | bytes 524312
  3.8 0.9 shard_map.50
  4.6 3.8 %collective-permute-start = (f32[2,3,32,128]{3,2,1,0:T(8,128)S(1)}, f32[2,3,32,128]{3,2,1,0:T(8,128)S(1)}, u32[]{:S(2)}, u32[]{:S(2)}) collective-permute-start(f32[2,3,32,128]{3,2,1,0:T(8,128)S(1)} %get-tuple-element.52), channel_id=1, source_target_pairs={{0,1},{1,0},{2,3},{3,2},{4,5},{5,4},{6,7},{7,6},{8,9},{9,8},{10,11... | collective-permute-start | bytes 294920 | tf_op jit(solution)/shard_map/ppermute | solution.py:543
  8.5 1.2 %collective-permute-start.5 = (f32[544,128]{1,0:T(8,128)S(1)}, f32[544,128]{1,0:T(8,128)S(1)}, u32[]{:S(2)}, u32[]{:S(2)}) collective-permute-start(f32[544,128]{1,0:T(8,128)S(1)} %get-tuple-element.69), channel_id=1, source_target_pairs={{0,2},{2,0},{4,6},{6,4},{1,3},{3,1},{5,7},{7,5},{8,10},{10,8},{12,... | collective-permute-start | bytes 835592 | tf_op jit(solution)/shard_map/ppermute | solution.py:544
  9.7 0.7 collective-permute-start.6
  10.3 0.1 collective-permute-done.z
  10.5 0.1 shard_map.51
  10.6 1.8 %collective-permute-start.1 = (f32[12,32,128]{2,1,0:T(8,128)S(1)}, f32[12,32,128]{2,1,0:T(8,128)S(1)}, u32[]{:S(2)}, u32[]{:S(2)}) collective-permute-start(f32[12,32,128]{2,1,0:T(8,128)S(1)} %get-tuple-element.59), channel_id=1, source_target_pairs={{0,8},{8,0},{16,24},{24,16},{32,40},{40,32},{48,56},{56,48},{64,72... | collective-permute-start | bytes 589832 | tf_op jit(solution)/shard_map/ppermute | solution.py:546
  12.4 3.2 %collective-permute-start.2 = (f32[12,32,128]{2,1,0:T(8,128)S(1)}, f32[12,32,128]{2,1,0:T(8,128)S(1)}, u32[]{:S(2)}, u32[]{:S(2)}) collective-permute-start(f32[12,32,128]{2,1,0:T(8,128)S(1)} %get-tuple-element.60), channel_id=1, source_target_pairs={{8,16},{16,8},{24,32},{32,24},{40,48},{48,40},{56,64},{64,56},{72,... | collective-permute-start | bytes 589832 | tf_op jit(solution)/shard_map/ppermute | solution.py:546
  15.6 0.2 shard_map.52
  15.8 0.0 collective-permute-done.1.xa
  15.8 4.9 %collective-permute-done.2.xb = f32[12,32,128]{2,1,0:T(8,128)S(1)} collective-permute-done((f32[12,32,128]{2,1,0:T(8,128)S(1)}, f32[12,32,128]{2,1,0:T(8,128)S(1)}, u32[]{:S(2)}, u32[]{:S(2)}) %collective-permute-start.2) | collective-permute-done | bytes 196640 | tf_op jit(solution)/shard_map/ppermute | solution.py:546
  20.7 0.1 shard_map.53
  20.8 3.2 %collective-permute-start.3 = (f32[128,128]{1,0:T(8,128)S(1)}, f32[128,128]{1,0:T(8,128)S(1)}, u32[]{:S(2)}, u32[]{:S(2)}) collective-permute-start(f32[128,128]{1,0:T(8,128)S(1)} %get-tuple-element.67), channel_id=1, source_target_pairs={{0,2},{2,0},{4,6},{6,4},{1,3},{3,1},{5,7},{7,5},{8,10},{10,8},{12,... | collective-permute-start | bytes 196616 | tf_op jit(solution)/shard_map/ppermute | solution.py:552
  24.0 0.7 collective-permute-start.4
  24.7 0.0 collective-permute-done.5.ya
  24.7 0.0 collective-permute-done.6.yb
  24.7 0.1 shard_map.54
  24.8 0.9 collective-permute-done.3.ea
  25.7 5.1 %shard_map.55 = (f32[2,22,56,128]{3,2,1,0:T(8,128)S(1)}, f32[2,22,56,128]{3,2,1,0:T(8,128)S(1)}, f32[2,22,56,128]{3,2,1,0:T(8,128)S(1)}, f32[2,4,56,128]{3,2,1,0...) custom-call(f32[128,128]{1,0:T(8,128)S(1)} %collective-permute-done., ...), custom_call_target="tpu_custom_call", output_to_operand_aliasing={{0}: (2, {}), {1}: (3, {}), {2}: (4, {}), {3}: (5, {}), {4}... | custom-call | tf_op jit(solution)/shard_map/pallas_call | solution.py:560
  30.8 0.0 collective-permute-start.7
  30.8 4.1 %collective-permute-start.8 = (f32[8,40,128]{2,1,0:T(8,128)S(1)}, f32[8,40,128]{2,1,0:T(8,128)S(1)}, u32[]{:S(2)}, u32[]{:S(2)}) collective-permute-start(f32[8,40,128]{2,1,0:T(8,128)S(1)} %get-tuple-element.89), channel_id=1, source_target_pairs={{8,16},{16,8},{24,32},{32,24},{40,48},{48,40},{56,64},{64,56},{72,... | collective-permute-start | bytes 491528 | tf_op jit(solution)/shard_map/ppermute | solution.py:557
  34.9 22.8 %all_to_all.33 = f32[128,1,128]{2,1,0:T(1,128)S(1)} all-to-all(f32[128,1,128]{2,1,0:T(1,128)S(1)} %bitcast.15), channel_id=1, replica_groups=mesh['gx'=16,'gy'=4,'gz'=2] {'gx','gy','gz'}, dimensions={0} | all-to-all | bytes 131072 | tf_op jit(solution)/shard_map/all_to_all | solution.py:523
  57.7 5.0 %shard_map.56 = (f32[2,22,56,128]{3,2,1,0:T(8,128)S(1)}, f32[2,4,56,128]{3,2,1,0:T(8,128)S(1)}, f32[2,22,56,128]{3,2,1,0:T(8,128)S(1)}, f32[2,4,56,128]{3,2,1,0:...) custom-call(f32[2,22,56,128]{3,2,1,0:T(8,128)S(1)} %get-tuple-element.80.C, ...), custom_call_target="tpu_custom_call" | custom-call | tf_op jit(solution)/shard_map/pallas_call | solution.py:563
  62.6 0.5 collective-permute-start.9
  63.2 2.2 %collective-permute-start.10 = (f32[8,40,128]{2,1,0:T(8,128)S(1)}, f32[8,40,128]{2,1,0:T(8,128)S(1)}, u32[]{:S(2)}, u32[]{:S(2)}) collective-permute-start(f32[8,40,128]{2,1,0:T(8,128)S(1)} %get-tuple-element.96), channel_id=1, source_target_pairs={{8,16},{16,8},{24,32},{32,24},{40,48},{48,40},{56,64},{64,56},{72,... | collective-permute-start | bytes 491528 | tf_op jit(solution)/shard_map/ppermute | solution.py:557
  65.3 15.3 %all_to_all.34 = f32[128,1,128]{2,1,0:T(1,128)S(1)} all-to-all(f32[128,1,128]{2,1,0:T(1,128)S(1)} %bitcast.16), channel_id=1, replica_groups=mesh['gx'=16,'gy'=4,'gz'=2] {'gx','gy','gz'}, dimensions={0} | all-to-all | bytes 131072 | tf_op jit(solution)/shard_map/all_to_all | solution.py:523
  80.6 5.9 %shard_map.57 = (f32[2,16,32,128]{3,2,1,0:T(8,128)S(1)}, f32[2,16,32,128]{3,2,1,0:T(8,128)S(1)}, f32[2,16,32,128]{3,2,1,0:T(8,128)}, f32[128,128]{1,0:T(8,128)S(1)}) custom-call(f32[2,22,56,128]{3,2,1,0:T(8,128)S(1)} %get-tuple-element.91.C, f32[2,22,56,128]{3,2,1,0:T(8,128)S(1)} %get-tuple-element.81.W, f32[2,22,56,128]{3,2,1,0:T(8,128)S(1)} %get-tuple-element.82.T, ...), custom_call_target="tpu_custom_call" | custom-call | tf_op jit(solution)/shard_map/pallas_call | solution.py:567
  86.5 13.9 %all_to_all.35 = f32[128,1,128]{2,1,0:T(1,128)S(1)} all-to-all(f32[128,1,128]{2,1,0:T(1,128)S(1)} %bitcast.17), channel_id=1, replica_groups=mesh['gx'=16,'gy'=4,'gz'=2] {'gx','gy','gz'}, dimensions={0} | all-to-all | bytes 131072 | tf_op jit(solution)/shard_map/all_to_all | solution.py:523
  100.4 1.0 shard_map.58
  (8 shorter events, 0.0 us)
Async XLA Ops:
  0.6 1.0 %copy-start = (f32[2,16,32,128]{3,2,1,0:T(8,128)S(1)}, f32[2,16,32,128]{3,2,1,0:T(8,128)}, u32[]{:S(2)}) copy-start(f32[2,16,32,128]{3,2,1,0:T(8,128)} %c.1) | copy-start | bytes 1572868
  1.7 1.0 %copy-start.1 = (f32[2,16,32,128]{3,2,1,0:T(8,128)S(1)}, f32[2,16,32,128]{3,2,1,0:T(8,128)}, u32[]{:S(2)}) copy-start(f32[2,16,32,128]{3,2,1,0:T(8,128)} %w.1) | copy-start | bytes 1572868
  2.7 1.0 %copy-start.2 = (f32[2,16,32,128]{3,2,1,0:T(8,128)S(1)}, f32[2,16,32,128]{3,2,1,0:T(8,128)}, u32[]{:S(2)}) copy-start(f32[2,16,32,128]{3,2,1,0:T(8,128)} %t.1) | copy-start | bytes 1572868
  4.6 5.8 %collective-permute-start = (f32[2,3,32,128]{3,2,1,0:T(8,128)S(1)}, f32[2,3,32,128]{3,2,1,0:T(8,128)S(1)}, u32[]{:S(2)}, u32[]{:S(2)}) collective-permute-start(f32[2,3,32,128]{3,2,1,0:T(8,128)S(1)} %get-tuple-element.52), channel_id=1, source_target_pairs={{0,1},{1,0},{2,3},{3,2},{4,5},{5,4},{6,7},{7,6},{8,9},{9,8},{10,11... | collective-permute-start | bytes 294920 | tf_op jit(solution)/shard_map/ppermute | solution.py:543
  8.5 16.2 %collective-permute-start.5 = (f32[544,128]{1,0:T(8,128)S(1)}, f32[544,128]{1,0:T(8,128)S(1)}, u32[]{:S(2)}, u32[]{:S(2)}) collective-permute-start(f32[544,128]{1,0:T(8,128)S(1)} %get-tuple-element.69), channel_id=1, source_target_pairs={{0,2},{2,0},{4,6},{6,4},{1,3},{3,1},{5,7},{7,5},{8,10},{10,8},{12,... | collective-permute-start | bytes 835592 | tf_op jit(solution)/shard_map/ppermute | solution.py:544
  9.7 15.0 %collective-permute-start.6 = (f32[544,128]{1,0:T(8,128)S(1)}, f32[544,128]{1,0:T(8,128)S(1)}, u32[]{:S(2)}, u32[]{:S(2)}) collective-permute-start(f32[544,128]{1,0:T(8,128)S(1)} %get-tuple-element.70), channel_id=1, source_target_pairs={{2,4},{4,2},{3,5},{5,3},{10,12},{12,10},{11,13},{13,11},{18,20},{2... | collective-permute-start | bytes 835592 | tf_op jit(solution)/shard_map/ppermute | solution.py:547
  10.6 5.3 %collective-permute-start.1 = (f32[12,32,128]{2,1,0:T(8,128)S(1)}, f32[12,32,128]{2,1,0:T(8,128)S(1)}, u32[]{:S(2)}, u32[]{:S(2)}) collective-permute-start(f32[12,32,128]{2,1,0:T(8,128)S(1)} %get-tuple-element.59), channel_id=1, source_target_pairs={{0,8},{8,0},{16,24},{24,16},{32,40},{40,32},{48,56},{56,48},{64,72... | collective-permute-start | bytes 589832 | tf_op jit(solution)/shard_map/ppermute | solution.py:546
  12.4 8.3 %collective-permute-start.2 = (f32[12,32,128]{2,1,0:T(8,128)S(1)}, f32[12,32,128]{2,1,0:T(8,128)S(1)}, u32[]{:S(2)}, u32[]{:S(2)}) collective-permute-start(f32[12,32,128]{2,1,0:T(8,128)S(1)} %get-tuple-element.60), channel_id=1, source_target_pairs={{8,16},{16,8},{24,32},{32,24},{40,48},{48,40},{56,64},{64,56},{72,... | collective-permute-start | bytes 589832 | tf_op jit(solution)/shard_map/ppermute | solution.py:546
  20.8 4.9 %collective-permute-start.3 = (f32[128,128]{1,0:T(8,128)S(1)}, f32[128,128]{1,0:T(8,128)S(1)}, u32[]{:S(2)}, u32[]{:S(2)}) collective-permute-start(f32[128,128]{1,0:T(8,128)S(1)} %get-tuple-element.67), channel_id=1, source_target_pairs={{0,2},{2,0},{4,6},{6,4},{1,3},{3,1},{5,7},{7,5},{8,10},{10,8},{12,... | collective-permute-start | bytes 196616 | tf_op jit(solution)/shard_map/ppermute | solution.py:552
  24.0 1.7 %collective-permute-start.4 = (f32[128,128]{1,0:T(8,128)S(1)}, f32[128,128]{1,0:T(8,128)S(1)}, u32[]{:S(2)}, u32[]{:S(2)}) collective-permute-start(f32[128,128]{1,0:T(8,128)S(1)} %get-tuple-element.68), channel_id=1, source_target_pairs={{2,4},{4,2},{3,5},{5,3},{10,12},{12,10},{11,13},{13,11},{18,20},{2... | collective-permute-start | bytes 196616 | tf_op jit(solution)/shard_map/ppermute | solution.py:552
  30.8 26.9 %collective-permute-start.7 = (f32[8,40,128]{2,1,0:T(8,128)S(1)}, f32[8,40,128]{2,1,0:T(8,128)S(1)}, u32[]{:S(2)}, u32[]{:S(2)}) collective-permute-start(f32[8,40,128]{2,1,0:T(8,128)S(1)} %get-tuple-element.88), channel_id=1, source_target_pairs={{0,8},{8,0},{16,24},{24,16},{32,40},{40,32},{48,56},{56,48},{64,72... | collective-permute-start | bytes 491528 | tf_op jit(solution)/shard_map/ppermute | solution.py:556
  30.8 26.8 %collective-permute-start.8 = (f32[8,40,128]{2,1,0:T(8,128)S(1)}, f32[8,40,128]{2,1,0:T(8,128)S(1)}, u32[]{:S(2)}, u32[]{:S(2)}) collective-permute-start(f32[8,40,128]{2,1,0:T(8,128)S(1)} %get-tuple-element.89), channel_id=1, source_target_pairs={{8,16},{16,8},{24,32},{32,24},{40,48},{48,40},{56,64},{64,56},{72,... | collective-permute-start | bytes 491528 | tf_op jit(solution)/shard_map/ppermute | solution.py:557
  62.6 18.0 %collective-permute-start.9 = (f32[8,40,128]{2,1,0:T(8,128)S(1)}, f32[8,40,128]{2,1,0:T(8,128)S(1)}, u32[]{:S(2)}, u32[]{:S(2)}) collective-permute-start(f32[8,40,128]{2,1,0:T(8,128)S(1)} %get-tuple-element.95), channel_id=1, source_target_pairs={{0,8},{8,0},{16,24},{24,16},{32,40},{40,32},{48,56},{56,48},{64,72... | collective-permute-start | bytes 491528 | tf_op jit(solution)/shard_map/ppermute | solution.py:556
  63.2 17.4 %collective-permute-start.10 = (f32[8,40,128]{2,1,0:T(8,128)S(1)}, f32[8,40,128]{2,1,0:T(8,128)S(1)}, u32[]{:S(2)}, u32[]{:S(2)}) collective-permute-start(f32[8,40,128]{2,1,0:T(8,128)S(1)} %get-tuple-element.96), channel_id=1, source_target_pairs={{8,16},{16,8},{24,32},{32,24},{40,48},{48,40},{56,64},{64,56},{72,... | collective-permute-start | bytes 491528 | tf_op jit(solution)/shard_map/ppermute | solution.py:557

commit v7 on v6

--- a/solution.py
+++ b/solution.py
@@ -22,7 +22,7 @@
 SEAM_AT = 2 * sum(X_DEPTHS)
 SIDE = slice(Y0 - 4, Y0 + NY + 4)
 SIDE_ROWS = NY + 8
-UNROLL, SEAM_UNROLL = 2, 1
+UNROLL = 4
 
 
 def lane_ids(rows):
@@ -282,8 +282,6 @@
                 Fl[n, tile, here] = value
         return carry
 
-    lax.fori_loop(0, chunks(NY + 2 * depth + 2), flux_at, 0, unroll=SEAM_UNROLL)
-
     def gradient_at(k, carry):
         y = Y0 - depth + 8 * k
         here, up, down = pl.ds(y, 8), pl.ds(y + 1, 8), pl.ds(y - 1, 8)
@@ -303,7 +301,15 @@
                 G[m, tile, here] = inside * value
         return carry
 
-    lax.fori_loop(0, chunks(NY + 2 * depth), gradient_at, 0, unroll=SEAM_UNROLL)
+    def both_at(k, carry):
+        flux_at(k, 0)
+        gradient_at(k - 2, 0)
+        return carry
+
+    count = chunks(NY + 2 * depth)
+    lax.fori_loop(0, 2, flux_at, 0)
+    lax.fori_loop(2, count, both_at, 0)
+    lax.fori_loop(count - 2, count, gradient_at, 0)
 
 
 def gradients(fields, seams, G, Gs, Fl, Fs, depth):
@@ -489,7 +495,9 @@
     lax.fori_loop(0, NX, body, 0)
 
 
-def finish(current, gradient, gathered, updated):
+def finish(current, gradient, applied, gathered, updated, applied_out, sem):
+    copy = pltpu.make_async_copy(applied, applied_out, sem.at[0])
+    copy.start()
     step = step_of(gathered)
 
     def body(x, carry):
@@ -500,6 +508,7 @@
         return carry
 
     lax.fori_loop(0, NX, body, 0)
+    copy.wait()
 
 
 def call(body, outs, scratch=(), mib=2, alias=None, **more):
@@ -567,8 +576,12 @@
     current, gradient, applied, sums = call(
         last_step, (block, block, block, rows), (wide, seam, wide, seam, *flux), 14
     )(*state, G, Gs, *refresh(ga, gb, sums))
-    (updated,) = call(finish, (block,))(current, gradient, gather(sums))
-    return updated, applied
+    return call(
+        finish,
+        (block, block),
+        (pltpu.SemaphoreType.DMA((1,)),),
+        out_specs=(pl.BlockSpec(memory_space=pltpu.VMEM), pl.BlockSpec(memory_space=pltpu.HBM)),
+    )(current, gradient, applied, gather(sums))
 
 
 def solution(mesh):

time: 102 us -> 101 us (level)
  Pallas kernels: 18.4 us -> 17.1 us
    pallas_call x1, Pallas kernels: 5.93 us -> 4.79 us  [local(): call(last_step, (block, block, block, rows), (wide, seam, wide, seam, *fl...]
  transfers between devices with their start and end apart: 11 -> 11, of which waited for: 3 -> 3; matrix products, arithmetic and copies ran while one was open for 0% -> 0% of each run, Pallas kernels for 0% -> 1%
where the time goes in v7:
time: 101 us; the launch traced here: 100 us
  blocking collectives  51.9 us (51%)
  starting transfers between devices  21.4 us (21%)
  Pallas kernels  17.1 us (17%)
  waiting for transfers between devices  5.87 us (6%)
  local copies, waits for them, and re-layouts  3.12 us (3%)
    all_to_all x3, blocking collectives, gather(): return lax.all_to_all(sums, ALL, 0, 0, tiled=True)  51.9 us
    ppermute x2, starting transfers between devices, refresh(): gb = lax.ppermute(gb, 'gx', second_x)  6.22 us
    ppermute x2, starting transfers between devices, local(): xa, xb = (lax.ppermute(xa, 'gx', first_x), lax.ppermute(xb, 'gx', second_x))  5.06 us
    ppermute x2, waiting for transfers between devices, local(): xa, xb = (lax.ppermute(xa, 'gx', first_x), lax.ppermute(xb, 'gx', second_x))  4.86 us
    pallas_call x1, Pallas kernels, local(): call(last_step, (block, block, block, rows), (wide, seam, wide, seam, *fl...  4.79 us
    pallas_call x1, Pallas kernels, local(): call(first_step, (*states, wide, seam, side, side, rows), flux, 9, {2 + i...  4.76 us
    pallas_call x1, Pallas kernels, local(): call(next_step, (wide, seam, wide, seam, side, side, rows), flux, 9)  4.58 us
    ppermute x2, starting transfers between devices, local(): ea, eb = (lax.ppermute(ea, 'gy', first_y), lax.ppermute(eb, 'gy', second_y))  3.85 us
  transfers between devices with their start and end apart: 11, of which 3 were waited for; matrix products, arithmetic and copies ran while one was open for 0% of the time, Pallas kernels for 1%

profile of v7, /device:TPU:1, one launch (start us, length us, event | category | flops | bytes accessed | tf_op | source)
XLA Modules:
  0.0 100.1 jit_solution(11949429575885978874)
XLA Ops:
  0.6 1.0 %copy-done = f32[2,16,32,128]{3,2,1,0:T(8,128)S(1)} copy-done((f32[2,16,32,128]{3,2,1,0:T(8,128)S(1)}, f32[2,16,32,128]{3,2,1,0:T(8,128)}, u32[]{:S(2)}) %copy-start) | copy-done | bytes 524312
  1.7 1.0 %copy-done.1 = f32[2,16,32,128]{3,2,1,0:T(8,128)S(1)} copy-done((f32[2,16,32,128]{3,2,1,0:T(8,128)S(1)}, f32[2,16,32,128]{3,2,1,0:T(8,128)}, u32[]{:S(2)}) %copy-start.1) | copy-done | bytes 524312
  2.7 1.0 %copy-done.2 = f32[2,16,32,128]{3,2,1,0:T(8,128)S(1)} copy-done((f32[2,16,32,128]{3,2,1,0:T(8,128)S(1)}, f32[2,16,32,128]{3,2,1,0:T(8,128)}, u32[]{:S(2)}) %copy-start.2) | copy-done | bytes 524312
  3.8 0.9 shard_map.50
  4.6 3.8 %collective-permute-start = (f32[2,3,32,128]{3,2,1,0:T(8,128)S(1)}, f32[2,3,32,128]{3,2,1,0:T(8,128)S(1)}, u32[]{:S(2)}, u32[]{:S(2)}) collective-permute-start(f32[2,3,32,128]{3,2,1,0:T(8,128)S(1)} %get-tuple-element.52), channel_id=1, source_target_pairs={{0,1},{1,0},{2,3},{3,2},{4,5},{5,4},{6,7},{7,6},{8,9},{9,8},{10,11... | collective-permute-start | bytes 294920 | tf_op jit(solution)/shard_map/ppermute | solution.py:552
  8.5 1.2 %collective-permute-start.5 = (f32[544,128]{1,0:T(8,128)S(1)}, f32[544,128]{1,0:T(8,128)S(1)}, u32[]{:S(2)}, u32[]{:S(2)}) collective-permute-start(f32[544,128]{1,0:T(8,128)S(1)} %get-tuple-element.69), channel_id=1, source_target_pairs={{0,2},{2,0},{4,6},{6,4},{1,3},{3,1},{5,7},{7,5},{8,10},{10,8},{12,... | collective-permute-start | bytes 835592 | tf_op jit(solution)/shard_map/ppermute | solution.py:553
  9.7 0.7 collective-permute-start.6
  10.3 0.1 collective-permute-done.z
  10.5 0.1 shard_map.51
  10.6 1.8 %collective-permute-start.1 = (f32[12,32,128]{2,1,0:T(8,128)S(1)}, f32[12,32,128]{2,1,0:T(8,128)S(1)}, u32[]{:S(2)}, u32[]{:S(2)}) collective-permute-start(f32[12,32,128]{2,1,0:T(8,128)S(1)} %get-tuple-element.59), channel_id=1, source_target_pairs={{0,8},{8,0},{16,24},{24,16},{32,40},{40,32},{48,56},{56,48},{64,72... | collective-permute-start | bytes 589832 | tf_op jit(solution)/shard_map/ppermute | solution.py:555
  12.4 3.2 %collective-permute-start.2 = (f32[12,32,128]{2,1,0:T(8,128)S(1)}, f32[12,32,128]{2,1,0:T(8,128)S(1)}, u32[]{:S(2)}, u32[]{:S(2)}) collective-permute-start(f32[12,32,128]{2,1,0:T(8,128)S(1)} %get-tuple-element.60), channel_id=1, source_target_pairs={{8,16},{16,8},{24,32},{32,24},{40,48},{48,40},{56,64},{64,56},{72,... | collective-permute-start | bytes 589832 | tf_op jit(solution)/shard_map/ppermute | solution.py:555
  15.6 0.2 shard_map.52
  15.8 0.0 collective-permute-done.1.xa
  15.8 4.9 %collective-permute-done.2.xb = f32[12,32,128]{2,1,0:T(8,128)S(1)} collective-permute-done((f32[12,32,128]{2,1,0:T(8,128)S(1)}, f32[12,32,128]{2,1,0:T(8,128)S(1)}, u32[]{:S(2)}, u32[]{:S(2)}) %collective-permute-start.2) | collective-permute-done | bytes 196640 | tf_op jit(solution)/shard_map/ppermute | solution.py:555
  20.7 0.1 shard_map.53
  20.8 3.2 %collective-permute-start.3 = (f32[128,128]{1,0:T(8,128)S(1)}, f32[128,128]{1,0:T(8,128)S(1)}, u32[]{:S(2)}, u32[]{:S(2)}) collective-permute-start(f32[128,128]{1,0:T(8,128)S(1)} %get-tuple-element.67), channel_id=1, source_target_pairs={{0,2},{2,0},{4,6},{6,4},{1,3},{3,1},{5,7},{7,5},{8,10},{10,8},{12,... | collective-permute-start | bytes 196616 | tf_op jit(solution)/shard_map/ppermute | solution.py:561
  24.0 0.7 collective-permute-start.4
  24.7 0.0 collective-permute-done.5.ya
  24.7 0.0 collective-permute-done.6.yb
  24.7 0.1 shard_map.54
  24.8 0.9 collective-permute-done.3.ea
  25.7 4.8 %shard_map.55 = (f32[2,22,56,128]{3,2,1,0:T(8,128)S(1)}, f32[2,22,56,128]{3,2,1,0:T(8,128)S(1)}, f32[2,22,56,128]{3,2,1,0:T(8,128)S(1)}, f32[2,4,56,128]{3,2,1,0...) custom-call(f32[128,128]{1,0:T(8,128)S(1)} %collective-permute-done., ...), custom_call_target="tpu_custom_call", output_to_operand_aliasing={{0}: (2, {}), {1}: (3, {}), {2}: (4, {}), {3}: (5, {}), {4}... | custom-call | tf_op jit(solution)/shard_map/pallas_call | solution.py:569
  30.4 0.0 collective-permute-start.7
  30.5 4.1 %collective-permute-start.8 = (f32[8,40,128]{2,1,0:T(8,128)S(1)}, f32[8,40,128]{2,1,0:T(8,128)S(1)}, u32[]{:S(2)}, u32[]{:S(2)}) collective-permute-start(f32[8,40,128]{2,1,0:T(8,128)S(1)} %get-tuple-element.89), channel_id=1, source_target_pairs={{8,16},{16,8},{24,32},{32,24},{40,48},{48,40},{56,64},{64,56},{72,... | collective-permute-start | bytes 491528 | tf_op jit(solution)/shard_map/ppermute | solution.py:566
  34.5 22.8 %all_to_all.33 = f32[128,1,128]{2,1,0:T(1,128)S(1)} all-to-all(f32[128,1,128]{2,1,0:T(1,128)S(1)} %bitcast.15), channel_id=1, replica_groups=mesh['gx'=16,'gy'=4,'gz'=2] {'gx','gy','gz'}, dimensions={0} | all-to-all | bytes 131072 | tf_op jit(solution)/shard_map/all_to_all | solution.py:532
  57.3 4.6 %shard_map.56 = (f32[2,22,56,128]{3,2,1,0:T(8,128)S(1)}, f32[2,4,56,128]{3,2,1,0:T(8,128)S(1)}, f32[2,22,56,128]{3,2,1,0:T(8,128)S(1)}, f32[2,4,56,128]{3,2,1,0:...) custom-call(f32[2,22,56,128]{3,2,1,0:T(8,128)S(1)} %get-tuple-element.80.C, ...), custom_call_target="tpu_custom_call" | custom-call | tf_op jit(solution)/shard_map/pallas_call | solution.py:572
  61.9 0.5 collective-permute-start.9
  62.4 2.2 %collective-permute-start.10 = (f32[8,40,128]{2,1,0:T(8,128)S(1)}, f32[8,40,128]{2,1,0:T(8,128)S(1)}, u32[]{:S(2)}, u32[]{:S(2)}) collective-permute-start(f32[8,40,128]{2,1,0:T(8,128)S(1)} %get-tuple-element.96), channel_id=1, source_target_pairs={{8,16},{16,8},{24,32},{32,24},{40,48},{48,40},{56,64},{64,56},{72,... | collective-permute-start | bytes 491528 | tf_op jit(solution)/shard_map/ppermute | solution.py:566
  64.6 15.3 %all_to_all.34 = f32[128,1,128]{2,1,0:T(1,128)S(1)} all-to-all(f32[128,1,128]{2,1,0:T(1,128)S(1)} %bitcast.16), channel_id=1, replica_groups=mesh['gx'=16,'gy'=4,'gz'=2] {'gx','gy','gz'}, dimensions={0} | all-to-all | bytes 131072 | tf_op jit(solution)/shard_map/all_to_all | solution.py:532
  79.8 4.8 %shard_map.57 = (f32[2,16,32,128]{3,2,1,0:T(8,128)S(1)}, f32[2,16,32,128]{3,2,1,0:T(8,128)S(1)}, f32[2,16,32,128]{3,2,1,0:T(8,128)S(1)}, f32[128,128]{1,0:T(8,128)S(1)}) custom-call(f32[2,22,56,128]{3,2,1,0:T(8,128)S(1)} %get-tuple-element.91.C, f32[2,22,56,128]{3,2,1,0:T(8,128)S(1)} %get-tuple-element.81.W, f32[2,22,56,128]{3,2,1,0:T(8,128)S(1)} %get-tuple-element.82.T, ...), custom_call_target="tpu_custom_call" | custom-call | tf_op jit(solution)/shard_map/pallas_call | solution.py:576
  84.6 13.9 %all_to_all.35 = f32[128,1,128]{2,1,0:T(1,128)S(1)} all-to-all(f32[128,1,128]{2,1,0:T(1,128)S(1)} %bitcast.17), channel_id=1, replica_groups=mesh['gx'=16,'gy'=4,'gz'=2] {'gx','gy','gz'}, dimensions={0} | all-to-all | bytes 131072 | tf_op jit(solution)/shard_map/all_to_all | solution.py:532
  98.5 1.6 %shard_map.58 = (f32[2,16,32,128]{3,2,1,0:T(8,128)}, f32[2,16,32,128]{3,2,1,0:T(8,128)}) custom-call(f32[2,16,32,128]{3,2,1,0:T(8,128)S(1)} %get-tuple-element.98.current, f32[2,16,32,128]{3,2,1,0:T(8,128)S(1)} %get-tuple-element.99.gradient, f32[2,16,32,128]{3,2,1,0:T(8,128)S(1)} %get-tuple-element.100.applied, f32[128,128]{1,0:T(8,128)S(1)} %bitcast.14), custom_call_target="tpu_custom_call" | custom-call | tf_op jit(solution)/shard_map/pallas_call | solution.py:579
  (8 shorter events, 0.0 us)
Async XLA Ops:
  0.6 1.0 %copy-start = (f32[2,16,32,128]{3,2,1,0:T(8,128)S(1)}, f32[2,16,32,128]{3,2,1,0:T(8,128)}, u32[]{:S(2)}) copy-start(f32[2,16,32,128]{3,2,1,0:T(8,128)} %c.1) | copy-start | bytes 1572868
  1.7 1.0 %copy-start.1 = (f32[2,16,32,128]{3,2,1,0:T(8,128)S(1)}, f32[2,16,32,128]{3,2,1,0:T(8,128)}, u32[]{:S(2)}) copy-start(f32[2,16,32,128]{3,2,1,0:T(8,128)} %w.1) | copy-start | bytes 1572868
  2.7 1.0 %copy-start.2 = (f32[2,16,32,128]{3,2,1,0:T(8,128)S(1)}, f32[2,16,32,128]{3,2,1,0:T(8,128)}, u32[]{:S(2)}) copy-start(f32[2,16,32,128]{3,2,1,0:T(8,128)} %t.1) | copy-start | bytes 1572868
  4.6 5.8 %collective-permute-start = (f32[2,3,32,128]{3,2,1,0:T(8,128)S(1)}, f32[2,3,32,128]{3,2,1,0:T(8,128)S(1)}, u32[]{:S(2)}, u32[]{:S(2)}) collective-permute-start(f32[2,3,32,128]{3,2,1,0:T(8,128)S(1)} %get-tuple-element.52), channel_id=1, source_target_pairs={{0,1},{1,0},{2,3},{3,2},{4,5},{5,4},{6,7},{7,6},{8,9},{9,8},{10,11... | collective-permute-start | bytes 294920 | tf_op jit(solution)/shard_map/ppermute | solution.py:552
  8.5 16.2 %collective-permute-start.5 = (f32[544,128]{1,0:T(8,128)S(1)}, f32[544,128]{1,0:T(8,128)S(1)}, u32[]{:S(2)}, u32[]{:S(2)}) collective-permute-start(f32[544,128]{1,0:T(8,128)S(1)} %get-tuple-element.69), channel_id=1, source_target_pairs={{0,2},{2,0},{4,6},{6,4},{1,3},{3,1},{5,7},{7,5},{8,10},{10,8},{12,... | collective-permute-start | bytes 835592 | tf_op jit(solution)/shard_map/ppermute | solution.py:553
  9.7 15.0 %collective-permute-start.6 = (f32[544,128]{1,0:T(8,128)S(1)}, f32[544,128]{1,0:T(8,128)S(1)}, u32[]{:S(2)}, u32[]{:S(2)}) collective-permute-start(f32[544,128]{1,0:T(8,128)S(1)} %get-tuple-element.70), channel_id=1, source_target_pairs={{2,4},{4,2},{3,5},{5,3},{10,12},{12,10},{11,13},{13,11},{18,20},{2... | collective-permute-start | bytes 835592 | tf_op jit(solution)/shard_map/ppermute | solution.py:556
  10.6 5.3 %collective-permute-start.1 = (f32[12,32,128]{2,1,0:T(8,128)S(1)}, f32[12,32,128]{2,1,0:T(8,128)S(1)}, u32[]{:S(2)}, u32[]{:S(2)}) collective-permute-start(f32[12,32,128]{2,1,0:T(8,128)S(1)} %get-tuple-element.59), channel_id=1, source_target_pairs={{0,8},{8,0},{16,24},{24,16},{32,40},{40,32},{48,56},{56,48},{64,72... | collective-permute-start | bytes 589832 | tf_op jit(solution)/shard_map/ppermute | solution.py:555
  12.4 8.3 %collective-permute-start.2 = (f32[12,32,128]{2,1,0:T(8,128)S(1)}, f32[12,32,128]{2,1,0:T(8,128)S(1)}, u32[]{:S(2)}, u32[]{:S(2)}) collective-permute-start(f32[12,32,128]{2,1,0:T(8,128)S(1)} %get-tuple-element.60), channel_id=1, source_target_pairs={{8,16},{16,8},{24,32},{32,24},{40,48},{48,40},{56,64},{64,56},{72,... | collective-permute-start | bytes 589832 | tf_op jit(solution)/shard_map/ppermute | solution.py:555
  20.8 4.9 %collective-permute-start.3 = (f32[128,128]{1,0:T(8,128)S(1)}, f32[128,128]{1,0:T(8,128)S(1)}, u32[]{:S(2)}, u32[]{:S(2)}) collective-permute-start(f32[128,128]{1,0:T(8,128)S(1)} %get-tuple-element.67), channel_id=1, source_target_pairs={{0,2},{2,0},{4,6},{6,4},{1,3},{3,1},{5,7},{7,5},{8,10},{10,8},{12,... | collective-permute-start | bytes 196616 | tf_op jit(solution)/shard_map/ppermute | solution.py:561
  24.0 1.7 %collective-permute-start.4 = (f32[128,128]{1,0:T(8,128)S(1)}, f32[128,128]{1,0:T(8,128)S(1)}, u32[]{:S(2)}, u32[]{:S(2)}) collective-permute-start(f32[128,128]{1,0:T(8,128)S(1)} %get-tuple-element.68), channel_id=1, source_target_pairs={{2,4},{4,2},{3,5},{5,3},{10,12},{12,10},{11,13},{13,11},{18,20},{2... | collective-permute-start | bytes 196616 | tf_op jit(solution)/shard_map/ppermute | solution.py:561
  30.4 26.9 %collective-permute-start.7 = (f32[8,40,128]{2,1,0:T(8,128)S(1)}, f32[8,40,128]{2,1,0:T(8,128)S(1)}, u32[]{:S(2)}, u32[]{:S(2)}) collective-permute-start(f32[8,40,128]{2,1,0:T(8,128)S(1)} %get-tuple-element.88), channel_id=1, source_target_pairs={{0,8},{8,0},{16,24},{24,16},{32,40},{40,32},{48,56},{56,48},{64,72... | collective-permute-start | bytes 491528 | tf_op jit(solution)/shard_map/ppermute | solution.py:565
  30.5 26.8 %collective-permute-start.8 = (f32[8,40,128]{2,1,0:T(8,128)S(1)}, f32[8,40,128]{2,1,0:T(8,128)S(1)}, u32[]{:S(2)}, u32[]{:S(2)}) collective-permute-start(f32[8,40,128]{2,1,0:T(8,128)S(1)} %get-tuple-element.89), channel_id=1, source_target_pairs={{8,16},{16,8},{24,32},{32,24},{40,48},{48,40},{56,64},{64,56},{72,... | collective-permute-start | bytes 491528 | tf_op jit(solution)/shard_map/ppermute | solution.py:566
  61.9 18.0 %collective-permute-start.9 = (f32[8,40,128]{2,1,0:T(8,128)S(1)}, f32[8,40,128]{2,1,0:T(8,128)S(1)}, u32[]{:S(2)}, u32[]{:S(2)}) collective-permute-start(f32[8,40,128]{2,1,0:T(8,128)S(1)} %get-tuple-element.95), channel_id=1, source_target_pairs={{0,8},{8,0},{16,24},{24,16},{32,40},{40,32},{48,56},{56,48},{64,72... | collective-permute-start | bytes 491528 | tf_op jit(solution)/shard_map/ppermute | solution.py:565
  62.4 17.4 %collective-permute-start.10 = (f32[8,40,128]{2,1,0:T(8,128)S(1)}, f32[8,40,128]{2,1,0:T(8,128)S(1)}, u32[]{:S(2)}, u32[]{:S(2)}) collective-permute-start(f32[8,40,128]{2,1,0:T(8,128)S(1)} %get-tuple-element.96), channel_id=1, source_target_pairs={{8,16},{16,8},{24,32},{32,24},{40,48},{48,40},{56,64},{64,56},{72,... | collective-permute-start | bytes 491528 | tf_op jit(solution)/shard_map/ppermute | solution.py:566

commit v8 on v7

--- a/solution.py
+++ b/solution.py
@@ -147,7 +147,9 @@
                 start = X0 + high * (NX - depth)
                 for layer in range(depth):
                     out[at + 2 * layer + m] = fields[f][m, start + layer, Y0:TOP]
-            out[SEAM_AT + m] = seams[0][m, 1 + high, Y0:TOP]
+        near = lane_ids(NY) // (NZ // 2) == high
+        both = [seams[0][m, 1 + high, Y0:TOP] for m in range(2)]
+        out[SEAM_AT] = jnp.where(near, both[0], pltpu.roll(both[1], NZ // 2, 1))
 
 
 def build(xa, xb, *refs):
@@ -157,7 +159,7 @@
         slot = jnp.where(high == 1, 0, 7)
         near = jnp.logical_and(lane // SLOT == slot, own)
         for m in range(2):
-            seams[0][m, 3 * high, Y0:TOP] = face[SEAM_AT + m]
+            seams[0][m, 3 * high, Y0:TOP] = face[SEAM_AT] if m == 0 else pltpu.roll(face[SEAM_AT], NZ // 2, 1)
             for f, depth, at in face_layers()[1:]:
                 turned = pltpu.roll(face[at + m], (SLOT * slot + 8) % NZ, 1)
                 seams[f][m, 3 * high, Y0:TOP] = jnp.where(near, turned, 0.0)
@@ -539,7 +541,7 @@
     flux = ((6, XE, YE, NZ), (6, TILES, YE, NZ))
     rows = (nx * ny * 2, NZ)
     states = (wide,) * 3 + (seam,) * 3
-    x_face, y_face = (SEAM_AT + 2, NY, NZ), (2 * NX * sum(DEPTHS), NZ)
+    x_face, y_face = (SEAM_AT + 1, NY, NZ), (2 * NX * sum(DEPTHS), NZ)
     edge, side = (EDGE_ROWS, NZ), (2 * DX + 2, SIDE_ROWS, NZ)
     *state, ya, yb, z = call(
         pack,

time: 101 us -> 100 us (0.990)
  no operation moved by 1% of the time
where the time goes in v8:
time: 100 us; the launch traced here: 99.8 us
  blocking collectives  51.9 us (52%)
  starting transfers between devices  21.4 us (21%)
  Pallas kernels  17.1 us (17%)
  waiting for transfers between devices  5.52 us (6%)
  local copies, waits for them, and re-layouts  3.12 us (3%)
    all_to_all x3, blocking collectives, gather(): return lax.all_to_all(sums, ALL, 0, 0, tiled=True)  51.9 us
    ppermute x2, starting transfers between devices, refresh(): gb = lax.ppermute(gb, 'gx', second_x)  6.22 us
    ppermute x2, starting transfers between devices, local(): xa, xb = (lax.ppermute(xa, 'gx', first_x), lax.ppermute(xb, 'gx', second_x))  5.06 us
    pallas_call x1, Pallas kernels, local(): call(last_step, (block, block, block, rows), (wide, seam, wide, seam, *fl...  4.79 us
    pallas_call x1, Pallas kernels, local(): call(first_step, (*states, wide, seam, side, side, rows), flux, 9, {2 + i...  4.76 us
    pallas_call x1, Pallas kernels, local(): call(next_step, (wide, seam, wide, seam, side, side, rows), flux, 9)  4.58 us
    ppermute x2, waiting for transfers between devices, local(): xa, xb = (lax.ppermute(xa, 'gx', first_x), lax.ppermute(xb, 'gx', second_x))  4.51 us
    ppermute x2, starting transfers between devices, local(): ea, eb = (lax.ppermute(ea, 'gy', first_y), lax.ppermute(eb, 'gy', second_y))  3.85 us
  transfers between devices with their start and end apart: 11, of which 3 were waited for; matrix products, arithmetic and copies ran while one was open for 0% of the time, Pallas kernels for 1%

profile of v8, /device:TPU:1, one launch (start us, length us, event | category | flops | bytes accessed | tf_op | source)
XLA Modules:
  0.0 99.8 jit_solution(2709245621382069740)
XLA Ops:
  0.6 1.0 %copy-done = f32[2,16,32,128]{3,2,1,0:T(8,128)S(1)} copy-done((f32[2,16,32,128]{3,2,1,0:T(8,128)S(1)}, f32[2,16,32,128]{3,2,1,0:T(8,128)}, u32[]{:S(2)}) %copy-start) | copy-done | bytes 524312
  1.7 1.0 %copy-done.1 = f32[2,16,32,128]{3,2,1,0:T(8,128)S(1)} copy-done((f32[2,16,32,128]{3,2,1,0:T(8,128)S(1)}, f32[2,16,32,128]{3,2,1,0:T(8,128)}, u32[]{:S(2)}) %copy-start.1) | copy-done | bytes 524312
  2.7 1.0 %copy-done.2 = f32[2,16,32,128]{3,2,1,0:T(8,128)S(1)} copy-done((f32[2,16,32,128]{3,2,1,0:T(8,128)S(1)}, f32[2,16,32,128]{3,2,1,0:T(8,128)}, u32[]{:S(2)}) %copy-start.2) | copy-done | bytes 524312
  3.8 0.9 shard_map.50
  4.6 3.8 %collective-permute-start = (f32[2,3,32,128]{3,2,1,0:T(8,128)S(1)}, f32[2,3,32,128]{3,2,1,0:T(8,128)S(1)}, u32[]{:S(2)}, u32[]{:S(2)}) collective-permute-start(f32[2,3,32,128]{3,2,1,0:T(8,128)S(1)} %get-tuple-element.52), channel_id=1, source_target_pairs={{0,1},{1,0},{2,3},{3,2},{4,5},{5,4},{6,7},{7,6},{8,9},{9,8},{10,11... | collective-permute-start | bytes 294920 | tf_op jit(solution)/shard_map/ppermute | solution.py:554
  8.5 1.2 %collective-permute-start.5 = (f32[544,128]{1,0:T(8,128)S(1)}, f32[544,128]{1,0:T(8,128)S(1)}, u32[]{:S(2)}, u32[]{:S(2)}) collective-permute-start(f32[544,128]{1,0:T(8,128)S(1)} %get-tuple-element.69), channel_id=1, source_target_pairs={{0,2},{2,0},{4,6},{6,4},{1,3},{3,1},{5,7},{7,5},{8,10},{10,8},{12,... | collective-permute-start | bytes 835592 | tf_op jit(solution)/shard_map/ppermute | solution.py:555
  9.7 0.7 collective-permute-start.6
  10.3 0.1 collective-permute-done.z
  10.5 0.1 shard_map.51
  10.6 1.8 %collective-permute-start.1 = (f32[11,32,128]{2,1,0:T(8,128)S(1)}, f32[11,32,128]{2,1,0:T(8,128)S(1)}, u32[]{:S(2)}, u32[]{:S(2)}) collective-permute-start(f32[11,32,128]{2,1,0:T(8,128)S(1)} %get-tuple-element.59), channel_id=1, source_target_pairs={{0,8},{8,0},{16,24},{24,16},{32,40},{40,32},{48,56},{56,48},{64,72... | collective-permute-start | bytes 540680 | tf_op jit(solution)/shard_map/ppermute | solution.py:557
  12.4 3.2 %collective-permute-start.2 = (f32[11,32,128]{2,1,0:T(8,128)S(1)}, f32[11,32,128]{2,1,0:T(8,128)S(1)}, u32[]{:S(2)}, u32[]{:S(2)}) collective-permute-start(f32[11,32,128]{2,1,0:T(8,128)S(1)} %get-tuple-element.60), channel_id=1, source_target_pairs={{8,16},{16,8},{24,32},{32,24},{40,48},{48,40},{56,64},{64,56},{72,... | collective-permute-start | bytes 540680 | tf_op jit(solution)/shard_map/ppermute | solution.py:557
  15.6 0.2 shard_map.52
  15.8 4.5 %collective-permute-done.2.xb = f32[11,32,128]{2,1,0:T(8,128)S(1)} collective-permute-done((f32[11,32,128]{2,1,0:T(8,128)S(1)}, f32[11,32,128]{2,1,0:T(8,128)S(1)}, u32[]{:S(2)}, u32[]{:S(2)}) %collective-permute-start.2) | collective-permute-done | bytes 180256 | tf_op jit(solution)/shard_map/ppermute | solution.py:557
  20.4 0.1 shard_map.53
  20.5 3.2 %collective-permute-start.3 = (f32[128,128]{1,0:T(8,128)S(1)}, f32[128,128]{1,0:T(8,128)S(1)}, u32[]{:S(2)}, u32[]{:S(2)}) collective-permute-start(f32[128,128]{1,0:T(8,128)S(1)} %get-tuple-element.67), channel_id=1, source_target_pairs={{0,2},{2,0},{4,6},{6,4},{1,3},{3,1},{5,7},{7,5},{8,10},{10,8},{12,... | collective-permute-start | bytes 196616 | tf_op jit(solution)/shard_map/ppermute | solution.py:563
  23.7 0.7 collective-permute-start.4
  24.3 0.0 collective-permute-done.6.yb
  24.4 0.1 shard_map.54
  24.5 0.9 collective-permute-done.3.ea
  25.3 0.0 collective-permute-done.4.eb
  25.3 4.8 %shard_map.55 = (f32[2,22,56,128]{3,2,1,0:T(8,128)S(1)}, f32[2,22,56,128]{3,2,1,0:T(8,128)S(1)}, f32[2,22,56,128]{3,2,1,0:T(8,128)S(1)}, f32[2,4,56,128]{3,2,1,0...) custom-call(f32[128,128]{1,0:T(8,128)S(1)} %collective-permute-done., ...), custom_call_target="tpu_custom_call", output_to_operand_aliasing={{0}: (2, {}), {1}: (3, {}), {2}: (4, {}), {3}: (5, {}), {4}... | custom-call | tf_op jit(solution)/shard_map/pallas_call | solution.py:571
  30.1 0.0 collective-permute-start.7
  30.1 4.1 %collective-permute-start.8 = (f32[8,40,128]{2,1,0:T(8,128)S(1)}, f32[8,40,128]{2,1,0:T(8,128)S(1)}, u32[]{:S(2)}, u32[]{:S(2)}) collective-permute-start(f32[8,40,128]{2,1,0:T(8,128)S(1)} %get-tuple-element.89), channel_id=1, source_target_pairs={{8,16},{16,8},{24,32},{32,24},{40,48},{48,40},{56,64},{64,56},{72,... | collective-permute-start | bytes 491528 | tf_op jit(solution)/shard_map/ppermute | solution.py:568
  34.2 22.8 %all_to_all.33 = f32[128,1,128]{2,1,0:T(1,128)S(1)} all-to-all(f32[128,1,128]{2,1,0:T(1,128)S(1)} %bitcast.15), channel_id=1, replica_groups=mesh['gx'=16,'gy'=4,'gz'=2] {'gx','gy','gz'}, dimensions={0} | all-to-all | bytes 131072 | tf_op jit(solution)/shard_map/all_to_all | solution.py:534
  56.9 0.0 collective-permute-done.7.ga
  57.0 4.6 %shard_map.56 = (f32[2,22,56,128]{3,2,1,0:T(8,128)S(1)}, f32[2,4,56,128]{3,2,1,0:T(8,128)S(1)}, f32[2,22,56,128]{3,2,1,0:T(8,128)S(1)}, f32[2,4,56,128]{3,2,1,0:...) custom-call(f32[2,22,56,128]{3,2,1,0:T(8,128)S(1)} %get-tuple-element.80.C, ...), custom_call_target="tpu_custom_call" | custom-call | tf_op jit(solution)/shard_map/pallas_call | solution.py:574
  61.5 0.5 collective-permute-start.9
  62.1 2.2 %collective-permute-start.10 = (f32[8,40,128]{2,1,0:T(8,128)S(1)}, f32[8,40,128]{2,1,0:T(8,128)S(1)}, u32[]{:S(2)}, u32[]{:S(2)}) collective-permute-start(f32[8,40,128]{2,1,0:T(8,128)S(1)} %get-tuple-element.96), channel_id=1, source_target_pairs={{8,16},{16,8},{24,32},{32,24},{40,48},{48,40},{56,64},{64,56},{72,... | collective-permute-start | bytes 491528 | tf_op jit(solution)/shard_map/ppermute | solution.py:568
  64.2 15.3 %all_to_all.34 = f32[128,1,128]{2,1,0:T(1,128)S(1)} all-to-all(f32[128,1,128]{2,1,0:T(1,128)S(1)} %bitcast.16), channel_id=1, replica_groups=mesh['gx'=16,'gy'=4,'gz'=2] {'gx','gy','gz'}, dimensions={0} | all-to-all | bytes 131072 | tf_op jit(solution)/shard_map/all_to_all | solution.py:534
  79.5 4.8 %shard_map.57 = (f32[2,16,32,128]{3,2,1,0:T(8,128)S(1)}, f32[2,16,32,128]{3,2,1,0:T(8,128)S(1)}, f32[2,16,32,128]{3,2,1,0:T(8,128)S(1)}, f32[128,128]{1,0:T(8,128)S(1)}) custom-call(f32[2,22,56,128]{3,2,1,0:T(8,128)S(1)} %get-tuple-element.91.C, f32[2,22,56,128]{3,2,1,0:T(8,128)S(1)} %get-tuple-element.81.W, f32[2,22,56,128]{3,2,1,0:T(8,128)S(1)} %get-tuple-element.82.T, ...), custom_call_target="tpu_custom_call" | custom-call | tf_op jit(solution)/shard_map/pallas_call | solution.py:578
  84.3 13.9 %all_to_all.35 = f32[128,1,128]{2,1,0:T(1,128)S(1)} all-to-all(f32[128,1,128]{2,1,0:T(1,128)S(1)} %bitcast.17), channel_id=1, replica_groups=mesh['gx'=16,'gy'=4,'gz'=2] {'gx','gy','gz'}, dimensions={0} | all-to-all | bytes 131072 | tf_op jit(solution)/shard_map/all_to_all | solution.py:534
  98.2 1.6 %shard_map.58 = (f32[2,16,32,128]{3,2,1,0:T(8,128)}, f32[2,16,32,128]{3,2,1,0:T(8,128)}) custom-call(f32[2,16,32,128]{3,2,1,0:T(8,128)S(1)} %get-tuple-element.98.current, f32[2,16,32,128]{3,2,1,0:T(8,128)S(1)} %get-tuple-element.99.gradient, f32[2,16,32,128]{3,2,1,0:T(8,128)S(1)} %get-tuple-element.100.applied, f32[128,128]{1,0:T(8,128)S(1)} %bitcast.14), custom_call_target="tpu_custom_call" | custom-call | tf_op jit(solution)/shard_map/pallas_call | solution.py:581
  (8 shorter events, 0.0 us)
Async XLA Ops:
  0.6 1.0 %copy-start = (f32[2,16,32,128]{3,2,1,0:T(8,128)S(1)}, f32[2,16,32,128]{3,2,1,0:T(8,128)}, u32[]{:S(2)}) copy-start(f32[2,16,32,128]{3,2,1,0:T(8,128)} %c.1) | copy-start | bytes 1572868
  1.7 1.0 %copy-start.1 = (f32[2,16,32,128]{3,2,1,0:T(8,128)S(1)}, f32[2,16,32,128]{3,2,1,0:T(8,128)}, u32[]{:S(2)}) copy-start(f32[2,16,32,128]{3,2,1,0:T(8,128)} %w.1) | copy-start | bytes 1572868
  2.7 1.0 %copy-start.2 = (f32[2,16,32,128]{3,2,1,0:T(8,128)S(1)}, f32[2,16,32,128]{3,2,1,0:T(8,128)}, u32[]{:S(2)}) copy-start(f32[2,16,32,128]{3,2,1,0:T(8,128)} %t.1) | copy-start | bytes 1572868
  4.6 5.8 %collective-permute-start = (f32[2,3,32,128]{3,2,1,0:T(8,128)S(1)}, f32[2,3,32,128]{3,2,1,0:T(8,128)S(1)}, u32[]{:S(2)}, u32[]{:S(2)}) collective-permute-start(f32[2,3,32,128]{3,2,1,0:T(8,128)S(1)} %get-tuple-element.52), channel_id=1, source_target_pairs={{0,1},{1,0},{2,3},{3,2},{4,5},{5,4},{6,7},{7,6},{8,9},{9,8},{10,11... | collective-permute-start | bytes 294920 | tf_op jit(solution)/shard_map/ppermute | solution.py:554
  8.5 15.9 %collective-permute-start.5 = (f32[544,128]{1,0:T(8,128)S(1)}, f32[544,128]{1,0:T(8,128)S(1)}, u32[]{:S(2)}, u32[]{:S(2)}) collective-permute-start(f32[544,128]{1,0:T(8,128)S(1)} %get-tuple-element.69), channel_id=1, source_target_pairs={{0,2},{2,0},{4,6},{6,4},{1,3},{3,1},{5,7},{7,5},{8,10},{10,8},{12,... | collective-permute-start | bytes 835592 | tf_op jit(solution)/shard_map/ppermute | solution.py:555
  9.7 14.7 %collective-permute-start.6 = (f32[544,128]{1,0:T(8,128)S(1)}, f32[544,128]{1,0:T(8,128)S(1)}, u32[]{:S(2)}, u32[]{:S(2)}) collective-permute-start(f32[544,128]{1,0:T(8,128)S(1)} %get-tuple-element.70), channel_id=1, source_target_pairs={{2,4},{4,2},{3,5},{5,3},{10,12},{12,10},{11,13},{13,11},{18,20},{2... | collective-permute-start | bytes 835592 | tf_op jit(solution)/shard_map/ppermute | solution.py:558
  10.6 5.3 %collective-permute-start.1 = (f32[11,32,128]{2,1,0:T(8,128)S(1)}, f32[11,32,128]{2,1,0:T(8,128)S(1)}, u32[]{:S(2)}, u32[]{:S(2)}) collective-permute-start(f32[11,32,128]{2,1,0:T(8,128)S(1)} %get-tuple-element.59), channel_id=1, source_target_pairs={{0,8},{8,0},{16,24},{24,16},{32,40},{40,32},{48,56},{56,48},{64,72... | collective-permute-start | bytes 540680 | tf_op jit(solution)/shard_map/ppermute | solution.py:557
  12.4 7.9 %collective-permute-start.2 = (f32[11,32,128]{2,1,0:T(8,128)S(1)}, f32[11,32,128]{2,1,0:T(8,128)S(1)}, u32[]{:S(2)}, u32[]{:S(2)}) collective-permute-start(f32[11,32,128]{2,1,0:T(8,128)S(1)} %get-tuple-element.60), channel_id=1, source_target_pairs={{8,16},{16,8},{24,32},{32,24},{40,48},{48,40},{56,64},{64,56},{72,... | collective-permute-start | bytes 540680 | tf_op jit(solution)/shard_map/ppermute | solution.py:557
  20.5 4.9 %collective-permute-start.3 = (f32[128,128]{1,0:T(8,128)S(1)}, f32[128,128]{1,0:T(8,128)S(1)}, u32[]{:S(2)}, u32[]{:S(2)}) collective-permute-start(f32[128,128]{1,0:T(8,128)S(1)} %get-tuple-element.67), channel_id=1, source_target_pairs={{0,2},{2,0},{4,6},{6,4},{1,3},{3,1},{5,7},{7,5},{8,10},{10,8},{12,... | collective-permute-start | bytes 196616 | tf_op jit(solution)/shard_map/ppermute | solution.py:563
  23.7 1.7 %collective-permute-start.4 = (f32[128,128]{1,0:T(8,128)S(1)}, f32[128,128]{1,0:T(8,128)S(1)}, u32[]{:S(2)}, u32[]{:S(2)}) collective-permute-start(f32[128,128]{1,0:T(8,128)S(1)} %get-tuple-element.68), channel_id=1, source_target_pairs={{2,4},{4,2},{3,5},{5,3},{10,12},{12,10},{11,13},{13,11},{18,20},{2... | collective-permute-start | bytes 196616 | tf_op jit(solution)/shard_map/ppermute | solution.py:563
  30.1 26.9 %collective-permute-start.7 = (f32[8,40,128]{2,1,0:T(8,128)S(1)}, f32[8,40,128]{2,1,0:T(8,128)S(1)}, u32[]{:S(2)}, u32[]{:S(2)}) collective-permute-start(f32[8,40,128]{2,1,0:T(8,128)S(1)} %get-tuple-element.88), channel_id=1, source_target_pairs={{0,8},{8,0},{16,24},{24,16},{32,40},{40,32},{48,56},{56,48},{64,72... | collective-permute-start | bytes 491528 | tf_op jit(solution)/shard_map/ppermute | solution.py:567
  30.1 26.8 %collective-permute-start.8 = (f32[8,40,128]{2,1,0:T(8,128)S(1)}, f32[8,40,128]{2,1,0:T(8,128)S(1)}, u32[]{:S(2)}, u32[]{:S(2)}) collective-permute-start(f32[8,40,128]{2,1,0:T(8,128)S(1)} %get-tuple-element.89), channel_id=1, source_target_pairs={{8,16},{16,8},{24,32},{32,24},{40,48},{48,40},{56,64},{64,56},{72,... | collective-permute-start | bytes 491528 | tf_op jit(solution)/shard_map/ppermute | solution.py:568
  61.5 18.0 %collective-permute-start.9 = (f32[8,40,128]{2,1,0:T(8,128)S(1)}, f32[8,40,128]{2,1,0:T(8,128)S(1)}, u32[]{:S(2)}, u32[]{:S(2)}) collective-permute-start(f32[8,40,128]{2,1,0:T(8,128)S(1)} %get-tuple-element.95), channel_id=1, source_target_pairs={{0,8},{8,0},{16,24},{24,16},{32,40},{40,32},{48,56},{56,48},{64,72... | collective-permute-start | bytes 491528 | tf_op jit(solution)/shard_map/ppermute | solution.py:567
  62.1 17.4 %collective-permute-start.10 = (f32[8,40,128]{2,1,0:T(8,128)S(1)}, f32[8,40,128]{2,1,0:T(8,128)S(1)}, u32[]{:S(2)}, u32[]{:S(2)}) collective-permute-start(f32[8,40,128]{2,1,0:T(8,128)S(1)} %get-tuple-element.96), channel_id=1, source_target_pairs={{8,16},{16,8},{24,32},{32,24},{40,48},{48,40},{56,64},{64,56},{72,... | collective-permute-start | bytes 491528 | tf_op jit(solution)/shard_map/ppermute | solution.py:568
